TPU v7x, 256 devices: a whole 4x4x8 slice. The times are simulated.
256 devices in a mesh: data: 256 (over z, y, x, core).
Axes of the slice: x: 4, y: 4, z: 8, core: 2. Of those that a mesh axis runs over, the one named last changes fastest.
Arguments:
- w_one: float32 [6, 512, 1024], P(None, 'data')
- w_two: float32 [6, 1024, 512], P(None, 'data')
- mom_one: float32 [6, 512, 1024], P(None, 'data')
- mom_two: float32 [6, 1024, 512], P(None, 'data')
- x_zero: bfloat16 [196608, 512], P('data')
- y_zero: bfloat16 [196608, 512], P('data')
- x_one: bfloat16 [196608, 512], P('data')
- y_one: bfloat16 [196608, 512], P('data')
Outputs:
- output 1: float32 [6, 512, 1024], P(None, 'data')
- output 2: float32 [6, 1024, 512], P(None, 'data')
- output 3: float32 [6, 512, 1024], P(None, 'data')
- output 4: float32 [6, 1024, 512], P(None, 'data')
- output 5: float32 [196608], P('data')
- output 6: float32 [196608, 512], P('data')
All inputs are finite; a program needn't handle non-finite values.
Results may differ from a plain program's by a relative error of at most 0.00922473.
Values are sent between devices in bfloat16 or wider.
A program may use at most 768 MiB of HBM per device.

v0:
```python
import jax
import jax.numpy as jnp
from jax import lax
from jax.sharding import PartitionSpec as P

LEARN_RATE = 0.1
MOMENTUM = 0.9


def run_stack(w_one_b, w_two_b, h_cur):
    saved_vals = []
    for layer_idx in range(w_one_b.shape[0]):
        act_in = h_cur.astype(jnp.bfloat16)
        pre_act = jnp.dot(act_in, w_one_b[layer_idx], preferred_element_type=jnp.float32)
        hidden, gelu_back = jax.vjp(jax.nn.gelu, pre_act)
        hidden = hidden.astype(jnp.bfloat16)
        h_cur = h_cur + jnp.dot(hidden, w_two_b[layer_idx], preferred_element_type=jnp.float32)
        saved_vals.append((act_in, hidden, gelu_back))
    return h_cur, saved_vals


def layer_grads(d_state, w_out, layer_vals):
    act_in, hidden, gelu_back = layer_vals
    d_low = d_state.astype(jnp.bfloat16)
    grad_out = jnp.einsum("tf,td->fd", hidden, d_low, preferred_element_type=jnp.float32).astype(jnp.bfloat16)
    d_hidden = jnp.einsum("td,fd->tf", d_low, w_out, preferred_element_type=jnp.float32)
    d_pre = gelu_back(d_hidden)[0].astype(jnp.bfloat16)
    grad_in = jnp.einsum("td,tf->df", act_in, d_pre, preferred_element_type=jnp.float32).astype(jnp.bfloat16)
    return grad_in, grad_out, d_pre


def solution(mesh):
    n_dev = mesh.shape["data"]
    w_spec = P(None, "data", None)
    row_spec = P("data", None)

    def device_step(w_one, w_two, mom_one, mom_two, x_zero, y_zero, x_one, y_one):
        layers = w_one.shape[0]
        tok_dev, d_model = x_zero.shape
        w_one_b = lax.all_gather(w_one.astype(jnp.bfloat16), "data", axis=1, tiled=True)
        w_two_b = lax.all_gather(w_two.astype(jnp.bfloat16), "data", axis=1, tiled=True)
        h_end, saved_vals = run_stack(w_one_b, w_two_b, x_zero.astype(jnp.float32))
        d_state = (h_end - y_zero.astype(jnp.float32)) / (n_dev * tok_dev * d_model)
        shard_in = [None] * layers
        shard_out = [None] * layers
        for layer_idx in reversed(range(layers)):
            grad_in, grad_out, d_pre = layer_grads(d_state, w_two_b[layer_idx], saved_vals[layer_idx])
            shard_out[layer_idx] = lax.psum_scatter(grad_out, "data", scatter_dimension=0, tiled=True)
            shard_in[layer_idx] = lax.psum_scatter(grad_in, "data", scatter_dimension=0, tiled=True)
            if layer_idx > 0:
                d_state = d_state + jnp.einsum("tf,df->td", d_pre, w_one_b[layer_idx], preferred_element_type=jnp.float32)
        new_mom_one = MOMENTUM * mom_one + jnp.stack(shard_in).astype(jnp.float32)
        new_mom_two = MOMENTUM * mom_two + jnp.stack(shard_out).astype(jnp.float32)
        new_w_one = w_one - LEARN_RATE * new_mom_one
        new_w_two = w_two - LEARN_RATE * new_mom_two
        next_one_b = lax.all_gather(new_w_one.astype(jnp.bfloat16), "data", axis=1, tiled=True)
        next_two_b = lax.all_gather(new_w_two.astype(jnp.bfloat16), "data", axis=1, tiled=True)
        h_last = run_stack(next_one_b, next_two_b, x_one.astype(jnp.float32))[0]
        loss_rows = jnp.sum(jnp.square(h_last - y_one.astype(jnp.float32)), axis=1) / (2 * d_model)
        return new_w_one, new_w_two, new_mom_one, new_mom_two, loss_rows, h_last

    return jax.shard_map(device_step, mesh=mesh, in_specs=(w_spec, w_spec, w_spec, w_spec, row_spec, row_spec, row_spec, row_spec), out_specs=(w_spec, w_spec, w_spec, w_spec, P("data"), row_spec), check_vma=False)
```

profile of v0, /device:TPU:1, one launch (start us, length us, event | category | flops | bytes accessed | tf_op | source)
XLA Modules:
  0.0 982.1 jit_solution(9390723587215806367)
XLA Ops:
  10.3 123.9 %all-gather.5.cloned.1.call-done = bf16[6,512,1024]{2,0,1:T(8,128)(2,1)} async-done(((bf16[6,2,1024]{2,0,1:T(8,128)(2,1)}), bf16[6,512,1024]{2,0,1:T(8,128)(2,1)}) %all-gather.5.cloned.1.call-update) | async-done | bytes 6291472 | tf_op jit(solution)/shard_map/all_gather | solution.py:40
  134.2 29.1 %fusion.204 = (bf16[1,512,1024]{2,0,1:T(2,128)(2,1)}, bf16[1,512,1024]{2,0,1:T(2,128)(2,1)}, bf16[1,512,1024]{2,0,1:T(2,128)(2,1)}, bf16[1,512,1024]{2,0,1:T(2,1...) fusion(bf16[6,512,1024]{2,0,1:T(8,128)(2,1)} %all-gather.5.cloned.1.call-done), kind=kLoop, calls=%fused_computation.280 | loop fusion | bytes 12582912 | tf_op jit(solution)/shard_map/slice | solution.py:14
  163.3 2.7 fusion.128
  166.0 87.2 %all-gather.7.cloned.1.call-done = bf16[6,1024,512]{2,0,1:T(8,128)(2,1)} async-done(((bf16[6,4,512]{2,0,1:T(8,128)(2,1)}), bf16[6,1024,512]{2,0,1:T(8,128)(2,1)}) %all-gather.7.cloned.1.call-update) | async-done | bytes 6291472 | tf_op jit(solution)/shard_map/all_gather | solution.py:41
  253.2 28.4 %fusion.205 = (bf16[1,1024,512]{2,0,1:T(2,128)(2,1)S(1)}, bf16[1,1024,512]{2,0,1:T(2,128)(2,1)S(1)}, bf16[1,1024,512]{2,0,1:T(2,128)(2,1)S(1)}, bf16[1,1024,512]...) fusion(bf16[6,1024,512]{2,0,1:T(8,128)(2,1)} %all-gather.7.cloned.1.call-done), kind=kLoop, calls=%fused_computation.281 | loop fusion | bytes 12582912 | tf_op jit(solution)/shard_map/slice | solution.py:17
  299.9 2.9 subtract_multiply_fusion
  302.8 5.4 fusion.41
  308.2 2.9 convolution_add_fusion.3
  311.1 3.1 fusion.34
  315.3 3.1 fusion.27
  319.5 3.1 fusion.20
  323.6 3.3 fusion.13
  336.8 2.0 convolution_convert_fusion.6
  338.8 6.2 fusion.120
  345.0 3.6 convolution_convert_fusion.5
  348.6 2.4 convolution_convert_fusion.4
  351.0 2.4 convolution_convert_fusion.3
  353.4 2.8 convolution_convert_fusion.2
  356.2 2.4 convolution_convert_fusion.1
  358.6 2.4 convolution_convert_fusion
  367.8 293.3 %all-reduce.15.cloned.1.call-done = (bf16[512,1024]{0,1:T(8,128)(2,1)}, bf16[512,1024]{0,1:T(8,128)(2,1)}, bf16[512,1024]{0,1:T(8,128)(2,1)}, bf16[512,1024]{0,1...) async-done(((bf16[512,1024]{0,1:T(8,128)(2,1)}, ...) | async-done | bytes 12582928
  675.3 109.0 %all-gather.11.cloned.1.call-done = bf16[6,1024,512]{2,0,1:T(8,128)(2,1)} async-done(((bf16[6,4,512]{2,0,1:T(8,128)(2,1)}), bf16[6,1024,512]{2,0,1:T(8,128)(2,1)}) %all-gather.11.cloned.1.call-update) | async-done | bytes 6291472 | tf_op jit(solution)/shard_map/all_gather | solution.py:57
  784.3 28.7 %fusion.203 = (bf16[1,1024,512]{2,0,1:T(2,128)(2,1)S(1)}, bf16[1,1024,512]{2,0,1:T(2,128)(2,1)}, bf16[1,1024,512]{2,0,1:T(2,128)(2,1)}, bf16[1,1024,512]{2,0,1:T...) fusion(bf16[6,1024,512]{2,0,1:T(8,128)(2,1)} %all-gather.11.cloned.1.call-done), kind=kLoop, calls=%fused_computation.279 | loop fusion | bytes 12582912 | tf_op jit(solution)/shard_map/slice | solution.py:17
  813.0 89.6 %all-gather.9.cloned.1.call-done = bf16[6,512,1024]{2,0,1:T(8,128)(2,1)} async-done(((bf16[6,2,1024]{2,0,1:T(8,128)(2,1)}), bf16[6,512,1024]{2,0,1:T(8,128)(2,1)}) %all-gather.9.cloned.1.call-update) | async-done | bytes 6291472 | tf_op jit(solution)/shard_map/all_gather | solution.py:56
  902.6 30.7 %fusion.202 = (bf16[1,512,1024]{2,0,1:T(2,128)(2,1)}, bf16[1,512,1024]{2,0,1:T(2,128)(2,1)}, bf16[1,512,1024]{2,0,1:T(2,128)(2,1)}, bf16[1,512,1024]{2,0,1:T(2,1...) fusion(bf16[6,512,1024]{2,0,1:T(8,128)(2,1)} %all-gather.9.cloned.1.call-done), kind=kLoop, calls=%fused_computation.278 | loop fusion | bytes 12582912 | tf_op jit(solution)/shard_map/slice | solution.py:14
  933.3 5.7 convert_add_fusion
  939.0 6.6 fusion.105
  945.6 6.6 fusion.108
  952.2 6.6 fusion.111
  958.8 6.6 fusion.114
  965.5 6.2 multiply_reduce_fusion
  972.3 3.0 copy.182
  (159 shorter events, 55.7 us)
Async XLA Ops:
  7.2 127.0 %all-gather.5.cloned.1.call-start = ((), (), s32[]{:S(2)}) async-start(), calls=%async_computation | async-start | bytes 8421376 | tf_op jit(solution)/shard_map/all_gather | solution.py:40
  8.7 244.5 %all-gather.7.cloned.1.call-start = ((), (), s32[]{:S(2)}) async-start(), calls=%async_computation.1 | async-start | bytes 8421376 | tf_op jit(solution)/shard_map/all_gather | solution.py:41
  10.2 153.1 %copy-start.28 = (bf16[768,512]{1,0:T(8,128)(2,1)S(1)}, bf16[768,512]{1,0:T(8,128)(2,1)}, u32[]{:S(2)}) copy-start(bf16[768,512]{1,0:T(8,128)(2,1)} %param.12) | copy-start | bytes 2359300
  10.2 650.9 %all-reduce.15.cloned.1.call-start = ((), (), s32[]{:S(2)}) async-start(), calls=%async_computation.4 | async-start | bytes 25165824
  253.2 28.4 %copy-start.4 = (f32[768,1024]{1,0:T(8,128)S(1)}, f32[768,1024]{1,0:T(8,128)}, u32[]{:S(2)}) copy-start(f32[768,1024]{1,0:T(8,128)} %fusion.128) | copy-start | bytes 9437188
  284.0 39.6 %copy-start.14 = (f32[768,1024]{1,0:T(8,128)}, f32[768,1024]{1,0:T(8,128)S(1)}, u32[]{:S(2)}) copy-start(f32[768,1024]{1,0:T(8,128)S(1)} %fusion.140) | copy-start | bytes 9437188
  284.0 3.1 copy-start
  285.3 4.2 copy-start.19
  288.1 31.3 %copy-start.12 = (f32[768,1024]{1,0:T(8,128)}, f32[768,1024]{1,0:T(8,128)S(1)}, u32[]{:S(2)}) copy-start(f32[768,1024]{1,0:T(8,128)S(1)} %fusion.142) | copy-start | bytes 9437188
  288.1 3.2 copy-start.1
  289.4 4.2 copy-start.17
  292.3 22.9 %copy-start.10 = (f32[768,1024]{1,0:T(8,128)}, f32[768,1024]{1,0:T(8,128)S(1)}, u32[]{:S(2)}) copy-start(f32[768,1024]{1,0:T(8,128)S(1)} %fusion.144) | copy-start | bytes 9437188
  296.1 15.0 %copy-start.6 = (f32[768,1024]{1,0:T(8,128)}, f32[768,1024]{1,0:T(8,128)S(1)}, u32[]{:S(2)}) copy-start(f32[768,1024]{1,0:T(8,128)S(1)} %fusion.146) | copy-start | bytes 9437188
  299.9 2.9 copy-start.8
  311.1 3.1 copy-start.38
  315.3 3.1 copy-start.40
  319.4 3.1 copy-start.42
  323.6 3.3 copy-start.45
  345.0 3.6 copy-start.15
  345.0 3.6 copy-start.46
  353.4 2.8 copy-start.7
  353.4 2.8 copy-start.39
  358.6 3.7 copy-start.24
  367.7 297.6 %copy-start.32 = (f32[6,4,512]{2,1,0:T(4,128)S(1)}, f32[6,4,512]{2,1,0:T(4,128)}, u32[]{:S(2)}) copy-start(f32[6,4,512]{2,1,0:T(4,128)} %param.9) | copy-start | bytes 147460
  367.7 297.6 %copy-start.34 = (f32[6,4,512]{2,1,0:T(4,128)S(1)}, f32[6,4,512]{2,1,0:T(4,128)}, u32[]{:S(2)}) copy-start(f32[6,4,512]{2,1,0:T(4,128)} %param.11) | copy-start | bytes 147460
  367.7 303.8 %copy-start.33 = (f32[6,2,1024]{2,1,0:T(2,128)S(1)}, f32[6,2,1024]{2,1,0:T(2,128)}, u32[]{:S(2)}) copy-start(f32[6,2,1024]{2,1,0:T(2,128)} %param.8) | copy-start | bytes 147460
  367.7 303.8 %copy-start.35 = (f32[6,2,1024]{2,1,0:T(2,128)S(1)}, f32[6,2,1024]{2,1,0:T(2,128)}, u32[]{:S(2)}) copy-start(f32[6,2,1024]{2,1,0:T(2,128)} %param.10) | copy-start | bytes 147460
  367.8 305.1 %copy-start.29 = (bf16[768,512]{1,0:T(8,128)(2,1)S(1)}, bf16[768,512]{1,0:T(8,128)(2,1)}, u32[]{:S(2)}) copy-start(bf16[768,512]{1,0:T(8,128)(2,1)} %param.15) | copy-start | bytes 2359300
  367.8 416.5 %all-gather.11.cloned.1.call-start = ((), (), s32[]{:S(2)}) async-start(), calls=%async_computation.3 | async-start | bytes 8421376 | tf_op jit(solution)/shard_map/all_gather | solution.py:57
  666.7 235.9 %all-gather.9.cloned.1.call-start = ((), (), s32[]{:S(2)}) async-start(), calls=%async_computation.2 | async-start | bytes 8421376 | tf_op jit(solution)/shard_map/all_gather | solution.py:56
  666.7 7.3 copy-start.30
  958.8 6.6 copy-start.31
  (20 other events, 46.4 us)
Sparse Core Ops, SparseCore 0:
  12.1 122.0 all-gather.4
  138.3 114.8 all-gather.6
  367.8 293.1 all-reduce.14
  666.8 117.4 all-gather.10
  787.7 114.8 all-gather.8
where the time goes:
time: 989 us; the launch traced here: 982 us
  waiting for transfers between devices  703 us (71%)
  local copies, waits for them, and re-layouts  147 us (15%)
  matrix products  113 us (11%)
  between operations  14.6 us (1%)
    unnamed x6, waiting for transfers between devices  293 us
    all_gather x1, waiting for transfers between devices, device_step(): lax.all_gather(w_one.astype(jnp.bfloat16), 'data', axis=1, tiled=True)  124 us
    all_gather x1, waiting for transfers between devices, device_step(): lax.all_gather(new_w_two.astype(jnp.bfloat16), 'data', axis=1, tiled=True)  109 us
    all_gather x1, waiting for transfers between devices, device_step(): lax.all_gather(new_w_one.astype(jnp.bfloat16), 'data', axis=1, tiled=True)  89.6 us
    all_gather x1, waiting for transfers between devices, device_step(): lax.all_gather(w_two.astype(jnp.bfloat16), 'data', axis=1, tiled=True)  87.2 us
    slice x2, local copies, waits for them, and re-layouts, run_stack(): w_one_b[layer_idx]  59.8 us
    slice x2, local copies, waits for them, and re-layouts, run_stack(): w_two_b[layer_idx]  57.1 us
    dot_general x12, matrix products, run_stack(): jnp.dot(hidden, w_two_b[layer_idx], preferred_element_type=jnp.float32)  47.7 us
  transfers between devices with their start and end apart: 5, of which 5 were waited for; matrix products, arithmetic and copies ran while one was open for 7% of the time, Pallas kernels for 0%

commit v1 on v0

--- a/solution.py
+++ b/solution.py
@@ -1,10 +1,261 @@
-import jax
-import jax.numpy as jnp
+import functools
+import jax, jax.numpy as jnp
 from jax import lax
+from jax.experimental import pallas as pl
+from jax.experimental.pallas import tpu as pltpu
 from jax.sharding import PartitionSpec as P
 
 LEARN_RATE = 0.1
 MOMENTUM = 0.9
+F32, BF16 = jnp.float32, jnp.bfloat16
+GRID = (8, 4, 4, 2)
+
+
+def start_copy(src, dst, send_sem, recv_sem, dev):
+    pltpu.make_async_remote_copy(src_ref=src, dst_ref=dst, send_sem=send_sem, recv_sem=recv_sem,
+                                 device_id=(dev,), device_id_type=pl.DeviceIdType.MESH).start()
+
+
+def wait_bytes(ref, sem):
+    pltpu.make_async_copy(ref, ref, sem).wait()
+
+
+class Place:
+    def __init__(self, grid):
+        self.grid = grid
+        nz, ny, nx, nc = grid
+        me = lax.axis_index("data")
+        self.me = me
+        self.c = lax.rem(me, nc)
+        self.x = lax.rem(me // nc, nx)
+        self.y = lax.rem(me // (nc * nx), ny)
+        self.z = me // (nc * nx * ny)
+        self.sign = 1 - 2 * self.c
+        self.size = {"z": nz, "y": ny, "x": nx}
+        self.pos = {"z": self.z, "y": self.y, "x": self.x}
+        self.stride = {"z": ny * nx * nc, "y": nx * nc, "x": nc}
+        self.sib = me + 1 - 2 * self.c
+        self.m = lax.rem(me, nc * nx)
+        self.base = me - self.m
+
+    def wrap(self, v, d):
+        n = self.size[d]
+        return lax.rem(v + 2 * n, n)
+
+    def dev(self, d, v):
+        return self.me + (v - self.pos[d]) * self.stride[d]
+
+
+ORDERS = (("z", "x", "y"), ("z", "y", "x"), ("x", "y", "z"))
+
+
+def block_of(buf, u, pl_, done, d, v):
+    idx = []
+    for k in ("z", "y", "x"):
+        if k in done:
+            idx.append(slice(None))
+        elif k == d:
+            idx.append(v)
+        else:
+            idx.append(pl_.pos[k])
+    return buf.at[(u, *idx, pl_.c)]
+
+
+class Gather:
+    def __init__(self, place, buf, u, order, send_sem, recv_sem):
+        self.p, self.buf, self.u, self.order = place, buf, u, order
+        self.send_sem, self.recv_sem = send_sem, recv_sem
+        n2, n3 = place.size[order[1]], place.size[order[2]]
+        self.sem_of = {1: 1, 2: 1 + max(n2 - 1, 1)}
+        self.last_sem = self.sem_of[2] + max(n3 - 1, 1)
+
+    def block(self, stage, v):
+        return block_of(self.buf, self.u, self.p, self.order[:stage], self.order[stage], v)
+
+    def direct_start(self):
+        p, d = self.p, self.order[0]
+        own = self.block(0, p.pos[d])
+        for k in range(1, p.size[d]):
+            start_copy(own, own, self.send_sem.at[self.u, 0], self.recv_sem.at[self.u, 0], p.dev(d, p.wrap(p.pos[d] + k, d)))
+
+    def many(self, stage):
+        p, d = self.p, self.order[stage]
+        return self.block(stage, pl.ds(0, p.size[d] - 1))
+
+    def direct_wait(self):
+        if self.p.size[self.order[0]] > 1:
+            wait_bytes(self.many(0), self.recv_sem.at[self.u, 0])
+
+    def ring_send(self, stage, way, step):
+        p, d = self.p, self.order[stage]
+        n = p.size[d]
+        s = p.sign * way
+        ref = self.block(stage, p.wrap(p.pos[d] - (step - 1) * s, d))
+        sem = self.sem_of[stage] + (step - 1 if way == 1 else n // 2 + step - 1)
+        start_copy(ref, ref, self.send_sem.at[self.u, stage], self.recv_sem.at[self.u, sem], p.dev(d, p.wrap(p.pos[d] + s, d)))
+
+    def ring_wait(self, stage, way, step):
+        p, d = self.p, self.order[stage]
+        n = p.size[d]
+        s = p.sign * way
+        sem = self.sem_of[stage] + (step - 1 if way == 1 else n // 2 + step - 1)
+        wait_bytes(self.block(stage, p.wrap(p.pos[d] - step * s, d)), self.recv_sem.at[self.u, sem])
+
+    def hops(self, stage):
+        n = self.p.size[self.order[stage]]
+        return n // 2, (n - 1) // 2
+
+    def ring_start(self, stage):
+        far, near = self.hops(stage)
+        if far:
+            self.ring_send(stage, 1, 1)
+        if near:
+            self.ring_send(stage, -1, 1)
+
+    def ring_step(self, stage, step):
+        far, near = self.hops(stage)
+        for way, n in ((1, far), (-1, near)):
+            if step <= n:
+                self.ring_wait(stage, way, step)
+                if step < n:
+                    self.ring_send(stage, way, step + 1)
+
+    def swap_ref(self, c):
+        return self.buf.at[self.u, :, :, :, c]
+
+    def swap_start(self):
+        ref = self.swap_ref(self.p.c)
+        start_copy(ref, ref, self.send_sem.at[self.u, 3], self.recv_sem.at[self.u, self.last_sem], self.p.sib)
+
+    def swap_wait(self):
+        wait_bytes(self.swap_ref(1 - self.p.c), self.recv_sem.at[self.u, self.last_sem])
+
+    def events(self):
+        out = [self.direct_start]
+
+        def first():
+            self.direct_wait()
+            self.ring_start(1)
+
+        out.append(first)
+        for stage in (1, 2):
+            far = self.hops(stage)[0]
+            for step in range(1, far + 1):
+                def ev(stage=stage, step=step, last=step == far):
+                    self.ring_step(stage, step)
+                    if last:
+                        if stage == 1:
+                            self.ring_start(2)
+                        else:
+                            self.swap_start()
+                out.append(ev)
+            if far == 0:
+                def ev0(stage=stage):
+                    if stage == 1:
+                        self.ring_start(2)
+                    else:
+                        self.swap_start()
+                out.append(ev0)
+        out.append(self.swap_wait)
+        return out
+
+    def drain(self):
+        for stage in range(3):
+            if self.p.size[self.order[stage]] > 1:
+                wait_bytes(self.many(stage), self.send_sem.at[self.u, stage])
+        wait_bytes(self.swap_ref(self.p.c), self.send_sem.at[self.u, 3])
+
+
+def enter(p):
+    barrier = pltpu.get_barrier_semaphore()
+    peers = []
+    group = p.grid[2] * p.grid[3]
+    for k in range(1, group):
+        peers.append(p.base + lax.rem(p.m + k, group))
+    for d in ("y", "z"):
+        for k in range(1, p.size[d]):
+            peers.append(p.dev(d, p.wrap(p.pos[d] + k, d)))
+    for peer in peers:
+        pl.semaphore_signal(barrier, inc=1, device_id=(peer,), device_id_type=pl.DeviceIdType.MESH)
+    pl.semaphore_wait(barrier, len(peers))
+
+
+def to_tiles_start(p, src1, src2, r1, r2, sems, k0):
+    group = p.grid[2] * p.grid[3]
+    half = group // 2
+    pltpu.make_async_copy(src1.at[:, :, pl.ds(pl.multiple_of(p.m * 128, 128), 128)], r1.at[p.m], sems.at[k0 + 1]).start()
+    for k in range(1, group):
+        j = lax.rem(p.m + k, group)
+        start_copy(src1.at[:, :, pl.ds(pl.multiple_of(j * 128, 128), 128)], r1.at[p.m], sems.at[k0], sems.at[k0 + 1], p.base + j)
+    hb = (p.m // half) * half
+    mm = p.m - hb
+    pltpu.make_async_copy(src2.at[:, :, pl.ds(pl.multiple_of(mm * 128, 128), 128)], r2.at[mm], sems.at[k0 + 3]).start()
+    for k in range(1, half):
+        j = lax.rem(mm + k, half)
+        start_copy(src2.at[:, :, pl.ds(pl.multiple_of(j * 128, 128), 128)], r2.at[mm], sems.at[k0 + 2], sems.at[k0 + 3], p.base + hb + j)
+
+
+def to_tiles_wait(p, r1, r2, sems, k0):
+    wait_bytes(r1.at[pl.ds(0, r1.shape[0] - 1)], sems.at[k0])
+    wait_bytes(r1, sems.at[k0 + 1])
+    wait_bytes(r2.at[pl.ds(0, r2.shape[0] - 1)], sems.at[k0 + 2])
+    wait_bytes(r2, sems.at[k0 + 3])
+
+
+def to_tiles(r1, r2, tiles):
+    layers = r1.shape[1]
+    for l in range(layers):
+        for m in range(r1.shape[0]):
+            tiles[2 * l, 2 * m:2 * m + 2, :] = r1[m, l]
+        for m in range(r2.shape[0]):
+            tiles[2 * l + 1, 4 * m:4 * m + 4, :] = r2[m, l]
+
+def ag_kernel(grid, w1, w2, out, wbuf, r1, r2, tiles, ssem, rsem, tsem, osem):
+    p = Place(grid)
+    units = wbuf.shape[0]
+    enter(p)
+    to_tiles_start(p, w1, w2, r1, r2, tsem, 0)
+    to_tiles_wait(p, r1, r2, tsem, 0)
+    to_tiles(r1, r2, tiles)
+    for u in range(units):
+        wbuf[u, p.z, p.y, p.x, p.c] = tiles[u].astype(BF16)
+    gs = [Gather(p, wbuf, u, ORDERS[u % 3], ssem, rsem) for u in range(units)]
+    todo = []
+    for u, g in enumerate(gs):
+        for k, ev in enumerate(g.events()):
+            todo.append((2.0 * u + 3.0 * k, u, k, ev))
+    todo.sort(key=lambda t: t[:3])
+    for _, u, k, ev in todo:
+        ev()
+        if k == len(gs[u].events()) - 1:
+            pltpu.make_async_copy(wbuf.at[u], out.at[u], osem.at[u]).start()
+    for g in gs:
+        g.drain()
+    for u in range(units):
+        pltpu.make_async_copy(wbuf.at[u], out.at[u], osem.at[u]).wait()
+
+def gather_all(grid, w1, w2, cid):
+    layers = w1.shape[0]
+    units = 2 * layers
+    group = grid[2] * grid[3]
+    ANY = pl.BlockSpec(memory_space=pl.ANY)
+    out = pl.pallas_call(
+        functools.partial(ag_kernel, grid),
+        out_shape=jax.ShapeDtypeStruct((units, *grid, 16, 128), BF16),
+        in_specs=[ANY, ANY], out_specs=ANY,
+        scratch_shapes=[pltpu.VMEM((units, *grid, 16, 128), BF16),
+            pltpu.VMEM((group, layers, 2, 128), F32), pltpu.VMEM((group // 2, layers, 4, 128), F32),
+            pltpu.VMEM((units, 16, 128), F32),
+            pltpu.SemaphoreType.DMA((units, 4)), pltpu.SemaphoreType.DMA((units, 12)), pltpu.SemaphoreType.DMA((4,)),
+            pltpu.SemaphoreType.DMA((units,))],
+        compiler_params=pltpu.CompilerParams(collective_id=cid, has_side_effects=True, vmem_limit_bytes=40 * 2**20),
+        name="weights_gather")(w1, w2)
+    nz, ny, nx, nc = grid
+    out = out.reshape(layers, 2, nz * ny, nx * nc, 16, 128)
+    full1 = out[:, 0].transpose(0, 1, 3, 2, 4).reshape(layers, nz * ny * 16, nx * nc * 128)
+    o2 = out[:, 1].reshape(layers, nz * ny, 2, nx * nc // 2, 16, 128)
+    full2 = o2.transpose(0, 1, 2, 4, 3, 5).reshape(layers, nz * ny * 32, nx * nc // 2 * 128)
+    return full1, full2
 
 
 def run_stack(w_one_b, w_two_b, h_cur):
@@ -37,8 +288,7 @@
     def device_step(w_one, w_two, mom_one, mom_two, x_zero, y_zero, x_one, y_one):
         layers = w_one.shape[0]
         tok_dev, d_model = x_zero.shape
-        w_one_b = lax.all_gather(w_one.astype(jnp.bfloat16), "data", axis=1, tiled=True)
-        w_two_b = lax.all_gather(w_two.astype(jnp.bfloat16), "data", axis=1, tiled=True)
+        w_one_b, w_two_b = gather_all(GRID, w_one, w_two, 0)
         h_end, saved_vals = run_stack(w_one_b, w_two_b, x_zero.astype(jnp.float32))
         d_state = (h_end - y_zero.astype(jnp.float32)) / (n_dev * tok_dev * d_model)
         shard_in = [None] * layers
@@ -53,8 +303,7 @@
         new_mom_two = MOMENTUM * mom_two + jnp.stack(shard_out).astype(jnp.float32)
         new_w_one = w_one - LEARN_RATE * new_mom_one
         new_w_two = w_two - LEARN_RATE * new_mom_two
-        next_one_b = lax.all_gather(new_w_one.astype(jnp.bfloat16), "data", axis=1, tiled=True)
-        next_two_b = lax.all_gather(new_w_two.astype(jnp.bfloat16), "data", axis=1, tiled=True)
+        next_one_b, next_two_b = gather_all(GRID, new_w_one, new_w_two, 1)
         h_last = run_stack(next_one_b, next_two_b, x_one.astype(jnp.float32))[0]
         loss_rows = jnp.sum(jnp.square(h_last - y_one.astype(jnp.float32)), axis=1) / (2 * d_model)
         return new_w_one, new_w_two, new_mom_one, new_mom_two, loss_rows, h_last

time: 989 us -> 624 us (0.63)
  waiting for transfers between devices: 703 us -> 291 us
  Pallas kernels: 0 us -> 149 us
  local copies, waits for them, and re-layouts: 147 us -> 61 us
  matrix products: 113 us -> 103 us
    all_gather x4 -> x0, waiting for transfers between devices: 410 us -> none  [the longest x1 124 us: device_step(): lax.all_gather(w_one.astype(jnp.bfloat16), 'data', axis=1, tiled=True)]
    pallas_call x0 -> x2, Pallas kernels: none -> 149 us  [gather_all(): pl.pallas_call(functools.partial(ag_kernel, grid), out_shape=jax.ShapeDty...]
    slice x2, local copies, waits for them, and re-layouts: 59.8 us -> 3.85 us  [run_stack(): w_one_b[layer_idx]]
    slice x2 -> x14, local copies, waits for them, and re-layouts: 57.1 us -> 16.5 us  [run_stack(): w_two_b[layer_idx]]
    slice x0 -> x2, local copies, waits for them, and re-layouts: none -> 11 us  [the longest x1 5.52 us: gather_all(): out[:, 0].transpose(0, 1, 3, 2, 4)]
    unnamed x110 -> x45, local copies, waits for them, and re-layouts: 19.5 us -> 26 us
    unnamed x6 -> x2, waiting for transfers between devices: 293 us -> 291 us
  transfers between devices with their start and end apart: 5 -> 1, of which waited for: 5 -> 1; matrix products, arithmetic and copies ran while one was open for 7% -> 0% of each run, Pallas kernels for 0% -> 0%
where the time goes in v1:
time: 624 us; the launch traced here: 621 us
  waiting for transfers between devices  291 us (47%)
  Pallas kernels  149 us (24%)
  matrix products  103 us (17%)
  local copies, waits for them, and re-layouts  61 us (10%)
  between operations  14.7 us (2%)
    unnamed x2, waiting for transfers between devices  291 us
    pallas_call x2, Pallas kernels, gather_all(): pl.pallas_call(functools.partial(ag_kernel, grid), out_shape=jax.ShapeDty...  149 us
    dot_general x12, matrix products, run_stack(): jnp.dot(hidden, w_two_b[layer_idx], preferred_element_type=jnp.float32)  48.5 us
    unnamed x45, local copies, waits for them, and re-layouts  26 us
    slice x14, local copies, waits for them, and re-layouts, run_stack(): w_two_b[layer_idx]  16.5 us
    dot_general x6, matrix products, layer_grads(): jnp.einsum('td,tf->df', act_in, d_pre, preferred_element_type=jnp.float32)  15.5 us
    dot_general x5, matrix products, layer_grads(): jnp.einsum('td,fd->tf', d_low, w_out, preferred_element_type=jnp.float32)  14.2 us
    dot_general x6, matrix products, layer_grads(): jnp.einsum('tf,td->fd', hidden, d_low, preferred_element_type=jnp.float32)  13.4 us
  transfers between devices with their start and end apart: 1, of which 1 were waited for; matrix products, arithmetic and copies ran while one was open for 0% of the time, Pallas kernels for 0%

profile of v1, /device:TPU:1, one launch (start us, length us, event | category | flops | bytes accessed | tf_op | source)
XLA Modules:
  0.0 620.8 jit_solution(18244052310668016883)
XLA Ops:
  8.8 75.5 %weights_gather.2 = bf16[12,8,4,4,2,16,128]{6,5,4,3,2,1,0:T(8,128)(2,1)S(1)} custom-call(f32[6,2,1024]{2,1,0:T(2,128)S(1)} %copy-done.2, f32[6,4,512]{2,1,0:T(4,128)S(1)} %copy-done), custom_call_target="tpu_custom_call" | custom-call | tf_op jit(solution)/shard_map/weights_gather/pallas_call | solution.py:242
  84.3 5.5 fusion.318
  89.9 6.0 copy.531
  97.2 2.2 fusion.322
  118.7 2.5 convolution_convert_fusion
  121.2 2.8 fusion.41
  125.0 2.2 convolution_convert_fusion.1
  127.2 2.8 fusion.34
  131.0 2.2 convolution_convert_fusion.2
  133.2 2.8 fusion.27
  137.0 2.2 convolution_convert_fusion.3
  139.2 2.7 fusion.20
  143.0 2.2 convolution_convert_fusion.4
  145.2 3.1 fusion.13
  148.3 2.0 convolution_convert_fusion.6
  150.3 2.0 convolution_convert_fusion.7
  154.3 2.1 convolution_convert_fusion.9
  157.4 2.0 convolution_convert_fusion.10
  159.5 2.1 convolution_convert_fusion.5
  161.6 5.3 fusion.123
  167.0 2.3 copy.295
  172.8 290.8 %all-reduce.15.cloned.1.call-done = (bf16[512,1024]{1,0:T(8,128)(2,1)}, bf16[512,1024]{1,0:T(8,128)(2,1)}, bf16[512,1024]{1,0:T(8,128)(2,1)}, bf16[512,1024]{1,0...) async-done(((bf16[512,1024]{1,0:T(8,128)(2,1)}, ...) | async-done | bytes 12582928
  473.6 73.3 %weights_gather.3 = bf16[12,8,4,4,2,16,128]{6,5,4,3,2,1,0:T(8,128)(2,1)S(1)} custom-call(f32[6,2,1024]{2,1,0:T(2,128)S(1)} %get-tuple-element.44.w1, f32[6,4,512]{2,1,0:T(4,128)S(1)} %get-tuple-element.42.w2), custom_call_target="tpu_custom_call" | custom-call | tf_op jit(solution)/shard_map/weights_gather/pallas_call | solution.py:242
  546.9 5.5 fusion.317
  552.5 6.0 copy.530
  558.5 2.5 fusion.319
  571.9 6.3 %convert_add_fusion = f32[768,512]{0,1:T(8,128)} fusion(bf16[768,512]{0,1:T(8,128)(2,1)} %copy.296, bf16[128,8,4,128]{3,2,1,0:T(4,128)(2,1)} %bitcast.337, bf16[768,512]{1,0:T(8,128)(2,1)} %param.14, bf16[64,8,8,128]{3,2,1,0:T(8,128)(2,1)} %bitcast.319), kind=kOutput, calls=%fused_computation.121 | convolution fusion | flops 1618477056 | bytes 5242880 | tf_op jit(solution)/shard_map/dot_general | solution.py:268
  578.2 7.2 %fusion.108 = f32[768,512]{0,1:T(8,128)} fusion(f32[768,512]{0,1:T(8,128)} %convert_add_fusion, bf16[128,8,4,128]{3,2,1,0:T(4,128)(2,1)} %bitcast.336, bf16[64,8,8,128]{3,2,1,0:T(8,128)(2,1)} %bitcast.318), kind=kOutput, calls=%fused_computation.151 | convolution fusion | flops 1618477056 | bytes 5242880 | tf_op jit(solution)/shard_map/dot_general | solution.py:268
  585.4 6.9 %fusion.111 = f32[768,512]{0,1:T(8,128)} fusion(f32[768,512]{0,1:T(8,128)} %fusion.108, bf16[128,8,4,128]{3,2,1,0:T(4,128)(2,1)} %bitcast.333, bf16[64,8,8,128]{3,2,1,0:T(8,128)(2,1)} %bitcast.317), kind=kOutput, calls=%fused_computation.152 | convolution fusion | flops 1618477056 | bytes 5242880 | tf_op jit(solution)/shard_map/dot_general | solution.py:268
  592.3 6.7 %fusion.114 = f32[768,512]{0,1:T(8,128)} fusion(f32[768,512]{0,1:T(8,128)} %fusion.111, bf16[128,8,4,128]{3,2,1,0:T(4,128)(2,1)} %bitcast.332, bf16[64,8,8,128]{3,2,1,0:T(8,128)(2,1)S(1)} %bitcast.316), kind=kOutput, calls=%fused_computation.153 | convolution fusion | flops 1618477056 | bytes 5242880 | tf_op jit(solution)/shard_map/dot_general | solution.py:268
  599.0 6.9 %fusion.117 = f32[768,512]{0,1:T(8,128)} fusion(f32[768,512]{0,1:T(8,128)} %fusion.114, bf16[128,8,4,128]{3,2,1,0:T(4,128)(2,1)} %bitcast.331, bf16[64,8,8,128]{3,2,1,0:T(8,128)(2,1)S(1)} %bitcast.315), kind=kOutput, calls=%fused_computation.154 | convolution fusion | flops 1618477056 | bytes 5242880 | tf_op jit(solution)/shard_map/dot_general | solution.py:268
  605.9 5.5 multiply_reduce_fusion
  (82 shorter events, 55.9 us)
Async XLA Ops:
  7.2 456.4 %all-reduce.15.cloned.1.call-start = ((), (), s32[]{:S(2)}) async-start(), calls=%async_computation | async-start | bytes 25165824
  7.2 0.8 copy-start
  8.0 0.8 copy-start.2
  100.0 3.9 copy-start.6
  101.2 1.7 copy-start.7
  116.0 1.1 copy-start.13
  157.4 2.1 copy-start.14
  169.2 1.1 copy-start.9
  169.2 2.3 copy-start.8
  169.2 298.6 %copy-start.1 = (f32[6,4,512]{2,1,0:T(4,128)S(1)}, f32[6,4,512]{2,1,0:T(4,128)}, u32[]{:S(2)}) copy-start(f32[6,4,512]{2,1,0:T(4,128)} %w2.1) | copy-start | bytes 147460
  169.3 298.6 %copy-start.11 = (f32[6,4,512]{2,1,0:T(4,128)S(1)}, f32[6,4,512]{2,1,0:T(4,128)}, u32[]{:S(2)}) copy-start(f32[6,4,512]{2,1,0:T(4,128)} %param.11) | copy-start | bytes 147460
  169.3 303.7 %copy-start.3 = (f32[6,2,1024]{2,1,0:T(2,128)S(1)}, f32[6,2,1024]{2,1,0:T(2,128)}, u32[]{:S(2)}) copy-start(f32[6,2,1024]{2,1,0:T(2,128)} %w1.1) | copy-start | bytes 147460
  169.3 303.7 %copy-start.12 = (f32[6,2,1024]{2,1,0:T(2,128)S(1)}, f32[6,2,1024]{2,1,0:T(2,128)}, u32[]{:S(2)}) copy-start(f32[6,2,1024]{2,1,0:T(2,128)} %param.10) | copy-start | bytes 147460
  468.5 78.4 %copy-start.4 = (f32[6,4,512]{2,1,0:T(4,128)}, f32[6,4,512]{2,1,0:T(4,128)S(1)}, u32[]{:S(2)}) copy-start(f32[6,4,512]{2,1,0:T(4,128)S(1)} %get-tuple-element.42.w2) | copy-start | bytes 147460
  473.6 73.3 %copy-start.5 = (f32[6,2,1024]{2,1,0:T(2,128)}, f32[6,2,1024]{2,1,0:T(2,128)S(1)}, u32[]{:S(2)}) copy-start(f32[6,2,1024]{2,1,0:T(2,128)S(1)} %get-tuple-element.44.w1) | copy-start | bytes 147460
  599.0 7.0 %copy-start.10 = (bf16[768,512]{0,1:T(8,128)(2,1)S(1)}, bf16[768,512]{0,1:T(8,128)(2,1)}, u32[]{:S(2)}) copy-start(bf16[768,512]{0,1:T(8,128)(2,1)} %copy.330) | copy-start | bytes 2359300
Sparse Core Ops, SparseCore 0:
  169.4 294.1 all-reduce.14

commit v2 on v0

v2 whole, which is shorter than its diff:
```python
import functools
import jax
import jax.numpy as jnp
from jax import lax
from jax.experimental import pallas as pl
from jax.experimental.pallas import tpu as pltpu
from jax.sharding import PartitionSpec as P

LEARN_RATE = 0.1
MOMENTUM = 0.9
F32, BF16 = jnp.float32, jnp.bfloat16
GRID = (8, 4, 4, 2)
ORDERS = (("z", "x", "y"), ("z", "y", "x"), ("x", "y", "z"))
GELU_SCALE = 0.7978845608028654
GELU_CUBE = 0.044715
ROWS = 256
G_SLOTS = 6
LANES = 128
SPILLED = 4


def start_copy(src, dst, send_sem, recv_sem, dev):
    pltpu.make_async_remote_copy(src_ref=src, dst_ref=dst, send_sem=send_sem, recv_sem=recv_sem,
                                 device_id=(dev,), device_id_type=pl.DeviceIdType.MESH).start()


def wait_bytes(ref, sem):
    pltpu.make_async_copy(ref, ref, sem).wait()


class Place:
    def __init__(self, grid):
        self.grid = grid
        nz, ny, nx, nc = grid
        me = lax.axis_index("data")
        self.me = me
        self.c = lax.rem(me, nc)
        self.x = lax.rem(me // nc, nx)
        self.y = lax.rem(me // (nc * nx), ny)
        self.z = me // (nc * nx * ny)
        self.sign = 1 - 2 * self.c
        self.size = {"z": nz, "y": ny, "x": nx}
        self.pos = {"z": self.z, "y": self.y, "x": self.x}
        self.stride = {"z": ny * nx * nc, "y": nx * nc, "x": nc}
        self.sib = me + 1 - 2 * self.c
        self.m = lax.rem(me, nc * nx)
        self.base = me - self.m

    def wrap(self, v, d):
        n = self.size[d]
        return lax.rem(v + 2 * n, n)

    def dev(self, d, v):
        return self.me + (v - self.pos[d]) * self.stride[d]

    def far(self, d):
        return self.size[d] // 2

    def near(self, d):
        return (self.size[d] - 1) // 2


def block_of(buf, lead, place, done, d, v, tail=()):
    idx = []
    for k in ("z", "y", "x"):
        if k in done:
            idx.append(slice(None))
        elif k == d:
            idx.append(v)
        else:
            idx.append(place.pos[k])
    return buf.at[(*lead, *idx, *tail)]


def ring_sem(place, d, way, step):
    return step - 1 if way == 1 else place.far(d) + step - 1


class Gather:
    def __init__(self, place, buf, u, order, send_sem, recv_sem):
        self.p, self.buf, self.u, self.order = place, buf, u, order
        self.send_sem, self.recv_sem = send_sem, recv_sem
        self.first_sem = {1: 1, 2: 1 + max(place.size[order[1]] - 1, 1)}
        self.last_sem = self.first_sem[2] + max(place.size[order[2]] - 1, 1)

    def block(self, stage, v):
        return block_of(self.buf, (self.u,), self.p, self.order[:stage], self.order[stage], v, (self.p.c,))

    def many(self, stage):
        return self.block(stage, pl.ds(0, self.p.size[self.order[stage]] - 1))

    def direct_start(self):
        p, d = self.p, self.order[0]
        own = self.block(0, p.pos[d])
        for k in range(1, p.size[d]):
            start_copy(own, own, self.send_sem.at[self.u, 0], self.recv_sem.at[self.u, 0], p.dev(d, p.wrap(p.pos[d] + k, d)))

    def direct_wait(self):
        if self.p.size[self.order[0]] > 1:
            wait_bytes(self.many(0), self.recv_sem.at[self.u, 0])

    def ring_send(self, stage, way, step):
        p, d = self.p, self.order[stage]
        s = p.sign * way
        ref = self.block(stage, p.wrap(p.pos[d] - (step - 1) * s, d))
        sem = self.first_sem[stage] + ring_sem(p, d, way, step)
        start_copy(ref, ref, self.send_sem.at[self.u, stage], self.recv_sem.at[self.u, sem], p.dev(d, p.wrap(p.pos[d] + s, d)))

    def ring_wait(self, stage, way, step):
        p, d = self.p, self.order[stage]
        ref = self.block(stage, p.wrap(p.pos[d] - step * p.sign * way, d))
        wait_bytes(ref, self.recv_sem.at[self.u, self.first_sem[stage] + ring_sem(p, d, way, step)])

    def ways(self, stage):
        d = self.order[stage]
        return ((1, self.p.far(d)), (-1, self.p.near(d)))

    def ring_start(self, stage):
        for way, n in self.ways(stage):
            if n:
                self.ring_send(stage, way, 1)

    def ring_step(self, stage, step):
        for way, n in self.ways(stage):
            if step <= n:
                self.ring_wait(stage, way, step)
                if step < n:
                    self.ring_send(stage, way, step + 1)

    def swap_ref(self, c):
        return self.buf.at[self.u, :, :, :, c]

    def swap_start(self):
        ref = self.swap_ref(self.p.c)
        start_copy(ref, ref, self.send_sem.at[self.u, 3], self.recv_sem.at[self.u, self.last_sem], self.p.sib)

    def swap_wait(self):
        wait_bytes(self.swap_ref(1 - self.p.c), self.recv_sem.at[self.u, self.last_sem])

    def events(self):
        out = [[self.direct_start], [self.direct_wait]]
        for stage in (1, 2):
            out[-1].append(functools.partial(self.ring_start, stage))
            for step in range(1, self.p.far(self.order[stage]) + 1):
                out.append([functools.partial(self.ring_step, stage, step)])
        out[-1].append(self.swap_start)
        out.append([self.swap_wait])
        return out

    def drain(self):
        for stage in range(3):
            if self.p.size[self.order[stage]] > 1:
                wait_bytes(self.many(stage), self.send_sem.at[self.u, stage])
        wait_bytes(self.swap_ref(self.p.c), self.send_sem.at[self.u, 3])


def add_into(dst, *srcs):
    total = dst[...].astype(F32)
    for s in srcs:
        total = total + s[...].astype(F32)
    dst[...] = total.astype(BF16)


class Reduce:
    def __init__(self, place, g, gslot, part, rings, rows, tiles, u, order, send_sem, recv_sem):
        self.p, self.g, self.gslot, self.part, self.u, self.order = place, g, gslot, part, u, order
        self.recv = {2: lambda k: rings[0].at[rings[1], k], 1: lambda k: rows.at[u, k, pl.ds(0, place.size[order[0]])]}
        self.tiles = tiles
        self.send_sem, self.recv_sem = send_sem, recv_sem
        self.first_sem = {2: 1, 1: 1 + max(place.size[order[2]] - 1, 1)}
        self.last_sem = self.first_sem[1] + max(place.size[order[1]] - 1, 1)

    def block(self, stage, v):
        return block_of(self.part, (self.u,), self.p, self.order[:stage], self.order[stage], v)

    def swap_start(self):
        start_copy(self.g.at[self.gslot, :, :, :, 1 - self.p.c], self.part.at[self.u],
                   self.send_sem.at[self.u, 3], self.recv_sem.at[self.u, 0], self.p.sib)

    def swap_wait(self):
        wait_bytes(self.part.at[self.u], self.recv_sem.at[self.u, 0])
        p = self.p

        def add(k, _):
            add_into(self.part.at[self.u, k], self.g.at[self.gslot, k, :, :, p.c])
            return 0

        lax.fori_loop(0, p.size["z"], add, 0)
        wait_bytes(self.part.at[self.u], self.send_sem.at[self.u, 3])

    def ways(self, stage):
        d = self.order[stage]
        return ((1, self.p.far(d)), (-1, self.p.near(d)))

    def ring_send(self, stage, way, step, n):
        p, d = self.p, self.order[stage]
        s = p.sign * way
        k = ring_sem(p, d, way, step)
        src = self.block(stage, p.wrap(p.pos[d] + n * s, d)) if step == 1 else self.recv[stage](k - 1)
        start_copy(src, self.recv[stage](k), self.send_sem.at[self.u, stage],
                   self.recv_sem.at[self.u, self.first_sem[stage] + k], p.dev(d, p.wrap(p.pos[d] + s, d)))

    def ring_start(self, stage):
        for way, n in self.ways(stage):
            if n:
                self.ring_send(stage, way, 1, n)

    def ring_step(self, stage, step):
        p, d = self.p, self.order[stage]
        ends = []
        for way, n in self.ways(stage):
            if step <= n:
                k = ring_sem(p, d, way, step)
                ref = self.recv[stage](k)
                wait_bytes(ref, self.recv_sem.at[self.u, self.first_sem[stage] + k])
                if step < n:
                    add_into(ref, self.block(stage, p.wrap(p.pos[d] + (n - step) * p.sign * way, d)))
                    self.ring_send(stage, way, step + 1, n)
        if step == p.far(d):
            for way, n in self.ways(stage):
                if n:
                    ends.append(self.recv[stage](ring_sem(p, d, way, n)))
            add_into(self.block(stage, p.pos[d]), *ends)

    def direct_start(self):
        p, d = self.p, self.order[0]
        for k in range(1, p.size[d]):
            v = p.wrap(p.pos[d] + k, d)
            start_copy(self.block(0, v), self.tiles.at[self.u, k - 1], self.send_sem.at[self.u, 0],
                       self.recv_sem.at[self.u, self.last_sem], p.dev(d, v))

    def direct_sum(self):
        n = self.p.size[self.order[0]]
        if n > 1:
            wait_bytes(self.tiles.at[self.u, pl.ds(0, n - 1)], self.recv_sem.at[self.u, self.last_sem])
        total = self.block(0, self.p.pos[self.order[0]])[...].astype(F32)
        for k in range(n - 1):
            total = total + self.tiles[self.u, k].astype(F32)
        return total.astype(BF16).astype(F32)

    def events(self):
        out = [[self.swap_wait]]
        for stage in (2, 1):
            out[-1].append(functools.partial(self.ring_start, stage))
            for step in range(1, self.p.far(self.order[stage]) + 1):
                out.append([functools.partial(self.ring_step, stage, step)])
        out[-1].append(self.direct_start)
        return out

    def drain(self):
        p = self.p
        for stage in (2, 1):
            n = p.size[self.order[stage]] - 1
            if n:
                wait_bytes(self.block(stage, pl.ds(0, n)), self.send_sem.at[self.u, stage])
        n = p.size[self.order[0]] - 1
        if n:
            wait_bytes(self.tiles.at[self.u, pl.ds(0, n)], self.send_sem.at[self.u, 0])


def enter(p):
    barrier = pltpu.get_barrier_semaphore()
    group = p.grid[2] * p.grid[3]
    peers = [p.base + lax.rem(p.m + k, group) for k in range(1, group)]
    for d in ("y", "z"):
        peers += [p.dev(d, p.wrap(p.pos[d] + k, d)) for k in range(1, p.size[d])]
    for peer in peers:
        pl.semaphore_signal(barrier, inc=1, device_id=(peer,), device_id_type=pl.DeviceIdType.MESH)
    pl.semaphore_wait(barrier, len(peers))


def lanes(ref, j):
    return ref.at[:, :, pl.ds(pl.multiple_of(j * LANES, LANES), LANES)]


class Shuffle:
    def __init__(self, place, one, two, sems, k0):
        self.p, self.one, self.two = place, one, two
        self.sem = lambda k: sems.at[k0 + k]
        self.group = place.grid[2] * place.grid[3]
        self.half = self.group // 2
        self.low = (place.m // self.half) * self.half
        self.mine = place.m - self.low

    def to_tiles_start(self, src1, src2):
        p = self.p
        pltpu.make_async_copy(lanes(src1, p.m), self.one.at[p.m], self.sem(1)).start()
        pltpu.make_async_copy(lanes(src2, self.mine), self.two.at[self.mine], self.sem(3)).start()
        for k in range(1, self.group):
            j = lax.rem(p.m + k, self.group)
            start_copy(lanes(src1, j), self.one.at[p.m], self.sem(0), self.sem(1), p.base + j)
        for k in range(1, self.half):
            j = lax.rem(self.mine + k, self.half)
            start_copy(lanes(src2, j), self.two.at[self.mine], self.sem(2), self.sem(3), p.base + self.low + j)

    def drain_sends(self):
        wait_bytes(self.one.at[pl.ds(0, self.group - 1)], self.sem(0))
        wait_bytes(self.two.at[pl.ds(0, self.half - 1)], self.sem(2))

    def to_tiles_finish(self, tiles):
        wait_bytes(self.one, self.sem(1))
        wait_bytes(self.two, self.sem(3))
        for l in range(self.one.shape[1]):
            for m in range(self.group):
                tiles[2 * l, 2 * m:2 * m + 2, :] = self.one[m, l]
            for m in range(self.half):
                tiles[2 * l + 1, 4 * m:4 * m + 4, :] = self.two[m, l]

    def put_rows(self, u, tile):
        if u % 2 == 0:
            for m in range(self.group):
                self.one[m, u // 2] = tile[2 * m:2 * m + 2, :]
        else:
            for m in range(self.half):
                self.two[m, u // 2] = tile[4 * m:4 * m + 4, :]

    def to_rows_start(self, dst1, dst2):
        p = self.p
        pltpu.make_async_copy(self.one.at[p.m], lanes(dst1, p.m), self.sem(1)).start()
        pltpu.make_async_copy(self.two.at[self.mine], lanes(dst2, self.mine), self.sem(3)).start()
        for k in range(1, self.group):
            j = lax.rem(p.m + k, self.group)
            start_copy(self.one.at[j], lanes(dst1, p.m), self.sem(0), self.sem(1), p.base + j)
        for k in range(1, self.half):
            j = lax.rem(self.mine + k, self.half)
            start_copy(self.two.at[j], lanes(dst2, self.mine), self.sem(2), self.sem(3), p.base + self.low + j)

    def to_rows_finish(self):
        wait_bytes(self.one, self.sem(1))
        wait_bytes(self.two, self.sem(3))
        self.drain_sends()


def w_one_of(wbuf, l):
    nz, ny, nx, nc = wbuf.shape[1:5]
    cols = [wbuf[2 * l, :, :, m // nc, m % nc].reshape(nz * ny * 16, LANES) for m in range(nx * nc)]
    return jnp.concatenate(cols, axis=1)


def w_two_of(wbuf, l):
    nz, ny, nx, nc = wbuf.shape[1:5]
    half = nx * nc // 2
    cols = []
    for b in range(half):
        pair = [wbuf[2 * l + 1, :, :, (r * half + b) // nc, b % nc].reshape(nz * ny, 1, 16, LANES) for r in range(2)]
        cols.append(jnp.concatenate(pair, axis=1).reshape(nz * ny * 32, LANES))
    return jnp.concatenate(cols, axis=1)


def contract(a, b, da, db):
    return lax.dot_general(a, b, (((da,), (db,)), ((), ())), preferred_element_type=F32)


def gelu_and_slope(u):
    u2 = u * u
    t = jnp.tanh(GELU_SCALE * (u + GELU_CUBE * (u * u2)))
    half = 0.5 * (1.0 + t)
    slope = half + (0.5 * u) * (1.0 - t * t) * (GELU_SCALE + (3.0 * GELU_CUBE * GELU_SCALE) * u2)
    return u * half, slope


def gelu(u):
    return u * (0.5 * (1.0 + jnp.tanh(GELU_SCALE * (u + GELU_CUBE * (u * u * u)))))


def row_tiles(total, body):
    size = min(ROWS, total)
    assert total % size == 0

    def step(t, _):
        body(pl.ds(pl.multiple_of(t * size, size), size))
        return 0

    lax.fori_loop(0, total // size, step, 0)


def step_kernel(grid, batch_scale, w1, w2, m1, m2, x0, y0, x1, y1, nw1, nw2, nm1, nm2, loss, hlast, spill,
                wbuf, slope, act, hid, h, dlow, g, part, ring_ab, ring_c, rows, tiles3,
                wone, wtwo, mone, mtwo, wt, mt, lossbuf,
                gsend, grecv, rsend, rrecv, shuf, local):
    p = Place(grid)
    layers = w1.shape[0]
    units = 2 * layers
    nz, ny, nx, nc = grid
    tok, d_model = h.shape
    d_ff = hid.shape[2]

    def load(src, dst, k):
        return pltpu.make_async_copy(src, dst, local.at[k])

    loads = {"x0": load(x0, act.at[0], 0), "y0": load(y0, dlow, 1),
             "x1": load(x1, act.at[layers - 1], 2), "y1": load(y1, act.at[layers - 2], 3)}
    loads["x0"].start()
    loads["y0"].start()
    enter(p)
    wshuf = Shuffle(p, wone, wtwo, shuf, 0)
    mshuf = Shuffle(p, mone, mtwo, shuf, 4)
    wshuf.to_tiles_start(w1, w2)
    mshuf.to_tiles_start(m1, m2)

    def own_tile(u):
        wbuf[u, p.z, p.y, p.x, p.c] = wt[u].astype(BF16)

    wshuf.to_tiles_finish(wt)
    for u in range(units):
        own_tile(u)
    loads["x0"].wait()
    h[...] = act[0].astype(F32)

    def spill_copy(l):
        return load(slope.at[l % 2], spill.at[l], 4 + l)

    def unspill_copy(l):
        return load(spill.at[l], slope.at[l % 2], 4 + l)

    def forward_one(l):
        if 2 <= l < SPILLED + 2 and l - 2 < SPILLED:
            spill_copy(l - 2).wait()

        def body(r):
            a = h[r, :].astype(BF16)
            if l:
                act[l, r, :] = a
            z, s = gelu_and_slope(jnp.dot(a, w_one_of(wbuf, l), preferred_element_type=F32))
            z = z.astype(BF16)
            slope[l % 2, r, :] = s
            hid[l, r, :] = z
            h[r, :] += jnp.dot(z, w_two_of(wbuf, l), preferred_element_type=F32)

        row_tiles(tok, body)
        if l < SPILLED and l + 2 < layers:
            spill_copy(l).start()

    def loss_slope():
        loads["y0"].wait()

        def body(r):
            d = (h[r, :] - dlow[r, :].astype(F32)) * batch_scale
            h[r, :] = d
            dlow[r, :] = d.astype(BF16)

        row_tiles(tok, body)

    gather_args = lambda u: (p, wbuf, u, ORDERS[u % 3], gsend, grecv)
    first = [Gather(*gather_args(u)) for u in range(units)]
    again = [Gather(*gather_args(u)) for u in range(units)]
    red = []
    for u in range(units):
        ring = (ring_c, u // 3) if u % 3 == 2 else (ring_ab, 2 * (u // 3) + u % 3)
        red.append(Reduce(p, g, (units - 1 - u) % G_SLOTS, part, ring, rows, tiles3, u, ORDERS[u % 3], rsend, rrecv))

    def grad_two(l):
        slot = red[2 * l + 1].gslot
        size = min(256, d_ff)
        zs = size // (ny * 32)

        def step(j, _):
            cols = pl.ds(pl.multiple_of(j * size, size), size)
            v = contract(hid[l, :, cols], dlow[...], 0, 0).astype(BF16).reshape(zs, ny, 2, 16, d_model)
            for b in range(nx * nc // 2):
                for r in range(2):
                    g[slot, pl.ds(j * zs, zs), :, (r * nx * nc // 2 + b) // nc, b % nc] = v[:, :, r, :, LANES * b:LANES * b + LANES]
            return 0

        lax.fori_loop(0, d_ff // size, step, 0)
        red[2 * l + 1].swap_start()

    def back_hidden(l):
        if l < SPILLED and l + 2 < layers:
            unspill_copy(l).wait()

        def body(r):
            q = contract(dlow[r, :], w_two_of(wbuf, l), 1, 1)
            v = (slope[l % 2, r, :] * q).astype(BF16)
            hid[l, r, :] = v
            if l:
                d = h[r, :] + contract(v, w_one_of(wbuf, l), 1, 1)
                h[r, :] = d
                dlow[r, :] = d.astype(BF16)

        row_tiles(tok, body)
        if 0 <= l - 2 < SPILLED:
            unspill_copy(l - 2).start()

    def grad_one(l):
        slot = red[2 * l].gslot
        size = min(256, d_model)
        zs = size // (ny * 16)

        def step(j, _):
            cols = pl.ds(pl.multiple_of(j * size, size), size)
            v = contract(act[l, :, cols], hid[l], 0, 0).astype(BF16).reshape(zs, ny, 16, d_ff)
            for m in range(nx * nc):
                g[slot, pl.ds(j * zs, zs), :, m // nc, m % nc] = v[:, :, :, LANES * m:LANES * m + LANES]
            return 0

        lax.fori_loop(0, d_model // size, step, 0)
        red[2 * l].swap_start()
        if l == layers - 1:
            loads["x1"].start()
        if l == layers - 2:
            loads["y1"].start()

    def update(u):
        total = red[u].direct_sum()
        mom = MOMENTUM * mt[u] + total
        w = wt[u] - LEARN_RATE * mom
        wbuf[u, p.z, p.y, p.x, p.c] = w.astype(BF16)
        wt[u] = w
        mt[u] = mom
        again[u].direct_start()

    def moments_ready():
        mshuf.to_tiles_finish(mt)
        mshuf.drain_sends()
        wshuf.drain_sends()

    def second_start():
        loads["x1"].wait()
        h[...] = act[layers - 1].astype(F32)

    def forward_two(l):
        last = l == layers - 1
        if last:
            loads["y1"].wait()

        def body(r):
            a = h[r, :].astype(BF16)
            z = gelu(jnp.dot(a, w_one_of(wbuf, l), preferred_element_type=F32)).astype(BF16)
            v = h[r, :] + jnp.dot(z, w_two_of(wbuf, l), preferred_element_type=F32)
            h[r, :] = v
            if last:
                e = v - act[layers - 2, r, :].astype(F32)
                e = e * e
                s = e[:, :LANES]
                for k in range(1, d_model // LANES):
                    s = s + e[:, LANES * k:LANES * k + LANES]
                lossbuf[:, r] = jnp.sum(s.T, axis=0, keepdims=True) * (1.0 / (2 * d_model))

        row_tiles(tok, body)

    def new_rows():
        for u in range(units):
            wshuf.put_rows(u, wt[u])
            mshuf.put_rows(u, mt[u])
        wshuf.to_rows_start(nw1, nw2)
        mshuf.to_rows_start(nm1, nm2)

    work = {}
    for u in range(units):
        for k, ev in enumerate(first[u].events()):
            work["a", u, k] = ev
        for k, ev in enumerate(red[u].events()):
            work["r", u, k] = ev
        work["u", u, 0] = [functools.partial(update, u)]
        for k, ev in enumerate(again[u].events()[1:]):
            work["b", u, k] = ev
        work["d", u, 0] = [first[u].drain]
    for l in range(layers):
        work["f", l, 0] = [functools.partial(forward_one, l)]
        work["g", l, 0] = [functools.partial(grad_two, l)]
        work["g", l, 1] = [functools.partial(back_hidden, l)]
        work["g", l, 2] = [functools.partial(grad_one, l)]
        work["s", l, 0] = [functools.partial(forward_two, l)]
    work["l", 0, 0] = [loss_slope]
    work["m", 0, 0] = [moments_ready]
    work["h", 0, 0] = [second_start]
    work["n", 0, 0] = [new_rows]
    for name in order_of(work, layers):
        for f in work[name]:
            f()
    out = [load(h, hlast, 0), load(lossbuf, loss, 1)]
    for c in out:
        c.start()
    for u in range(units):
        again[u].drain()
        red[u].drain()
    wshuf.to_rows_finish()
    mshuf.to_rows_finish()
    for c in out:
        c.wait()


def order_of(work, layers):
    units = 2 * layers
    out = []
    n = lambda tag, u: sum(1 for k in work if k[0] == tag and k[1] == u)
    for k in range(12):
        for u in range(units):
            if ("a", u, k) in work and k < n("a", u):
                out.append(("a", u, k))
    for l in range(layers):
        out.append(("f", l, 0))
    for u in range(units):
        out.append(("d", u, 0))
    out += [("m", 0, 0), ("l", 0, 0)]
    for l in reversed(range(layers)):
        out += [("g", l, 0), ("g", l, 1), ("g", l, 2)]
        out += [("r", 2 * l + 1, 0), ("r", 2 * l, 0)]
    for k in range(1, 12):
        for u in reversed(range(units)):
            if ("r", u, k) in work:
                out.append(("r", u, k))
    for u in range(units):
        out.append(("u", u, 0))
    for k in range(12):
        for u in range(units):
            if ("b", u, k) in work:
                out.append(("b", u, k))
    out.append(("h", 0, 0))
    out.append(("n", 0, 0))
    for l in range(layers):
        out.append(("s", l, 0))
    return out


def make_step(grid, layers, tok, d_model, d_ff, n_dev):
    nz, ny, nx, nc = grid
    units = 2 * layers
    group = nx * nc
    hbm = pl.BlockSpec(memory_space=pl.ANY)
    sds = jax.ShapeDtypeStruct
    tile = (16, LANES)
    dma = pltpu.SemaphoreType.DMA
    thirds = (units + 2) // 3
    outs = (sds((layers, 2, d_ff), F32), sds((layers, 4, d_model), F32), sds((layers, 2, d_ff), F32), sds((layers, 4, d_model), F32),
            sds((1, tok), F32), sds((tok, d_model), F32), sds((SPILLED, tok, d_ff), F32))
    shuffled = [pltpu.VMEM((group, layers, 2, LANES), F32), pltpu.VMEM((group // 2, layers, 4, LANES), F32)]
    scratch = [
        pltpu.VMEM((units, *grid, *tile), BF16),
        pltpu.VMEM((2, tok, d_ff), F32),
        pltpu.VMEM((layers, tok, d_model), BF16),
        pltpu.VMEM((layers, tok, d_ff), BF16),
        pltpu.VMEM((tok, d_model), F32),
        pltpu.VMEM((tok, d_model), BF16),
        pltpu.VMEM((G_SLOTS, *grid, *tile), BF16),
        pltpu.VMEM((units, nz, ny, nx, *tile), BF16),
        pltpu.VMEM((2 * thirds, nx - 1, nz, ny, *tile), BF16),
        pltpu.VMEM((thirds, nz - 1, ny, nx, *tile), BF16),
        pltpu.VMEM((units, max(ny, nx) - 1, max(nz, nx), *tile), BF16),
        pltpu.VMEM((units, max(nz, nx) - 1, *tile), BF16),
        *shuffled, *shuffled,
        pltpu.VMEM((units, *tile), F32), pltpu.VMEM((units, *tile), F32),
        pltpu.VMEM((1, tok), F32),
        dma((units, 4)), dma((units, 12)), dma((units, 4)), dma((units, 12)), dma((8,)), dma((4 + SPILLED,)),
    ]
    return pl.pallas_call(
        functools.partial(step_kernel, grid, 1.0 / (n_dev * tok * d_model)),
        out_shape=outs, in_specs=[hbm] * 8, out_specs=[hbm] * 7, scratch_shapes=scratch,
        compiler_params=pltpu.CompilerParams(collective_id=0, has_side_effects=True, vmem_limit_bytes=67043328),
        name="train_step")


def solution(mesh):
    n_dev = mesh.shape["data"]
    w_spec = P(None, "data", None)
    row_spec = P("data", None)

    def device_step(w_one, w_two, mom_one, mom_two, x_zero, y_zero, x_one, y_one):
        tok, d_model = x_zero.shape
        step = make_step(GRID, w_one.shape[0], tok, d_model, w_one.shape[2], n_dev)
        nw1, nw2, nm1, nm2, loss, h_last, _ = step(w_one, w_two, mom_one, mom_two, x_zero, y_zero, x_one, y_one)
        return nw1, nw2, nm1, nm2, loss.reshape(tok), h_last

    return jax.shard_map(device_step, mesh=mesh, in_specs=(w_spec, w_spec, w_spec, w_spec, row_spec, row_spec, row_spec, row_spec),
                         out_specs=(w_spec, w_spec, w_spec, w_spec, P("data"), row_spec), check_vma=False)
```

time: 989 us -> 215 us (0.22)
  waiting for transfers between devices: 703 us -> 0 us
  Pallas kernels: 0 us -> 205 us
  local copies, waits for them, and re-layouts: 147 us -> 8.35 us
  matrix products: 113 us -> 0 us
  between operations: 14.6 us -> 0.65 us
    all_gather x4 -> x0, waiting for transfers between devices: 410 us -> none  [the longest x1 124 us: device_step(): lax.all_gather(w_one.astype(jnp.bfloat16), 'data', axis=1, tiled=True)]
    unnamed x6 -> x0, waiting for transfers between devices: 293 us -> none
    pallas_call x0 -> x1, Pallas kernels: none -> 205 us  [device_step(): step(w_one, w_two, mom_one, mom_two, x_zero, y_zero, x_one, y_one)]
    slice x4 -> x0, local copies, waits for them, and re-layouts: 117 us -> none  [the longest x2 59.8 us: run_stack(): w_one_b[layer_idx]]
    dot_general x40 -> x0, matrix products: 113 us -> none  [the longest x12 47.7 us: run_stack(): jnp.dot(hidden, w_two_b[layer_idx], preferred_element_type=jnp.float32)]
    unnamed x110 -> x5, local copies, waits for them, and re-layouts: 19.5 us -> 8.35 us
  transfers between devices with their start and end apart: 5 -> 0, of which waited for: 5 -> 0; matrix products, arithmetic and copies ran while one was open for 7% -> 0% of each run, Pallas kernels for 0% -> 0%
where the time goes in v2:
time: 215 us
  Pallas kernels  205 us (95%)
  local copies, waits for them, and re-layouts  8.35 us (4%)
    pallas_call x1, Pallas kernels, device_step(): step(w_one, w_two, mom_one, mom_two, x_zero, y_zero, x_one, y_one)  205 us
    unnamed x5, local copies, waits for them, and re-layouts  8.35 us

profile of v2, /device:TPU:1, one launch (start us, length us, event | category | flops | bytes accessed | tf_op | source)
XLA Modules:
  0.0 215.0 jit_solution(9082110867285955246)
XLA Ops:
  0.6 204.8 %train_step.1 = (f32[6,2,1024]{2,1,0:T(2,128)}, f32[6,4,512]{2,1,0:T(4,128)}, f32[6,2,1024]{2,1,0:T(2,128)}, f32[6,4,512]{2,1,0:T(4,128)}, f32[1,768]{1,0:T(1,12...) custom-call(f32[6,2,1024]{2,1,0:T(2,128)} %w1.1, f32[6,4,512]{2,1,0:T(4,128)} %w2.1, f32[6,2,1024]{2,1,0:T(2,128)} %m1.1, ...), custom_call_target="tpu_custom_call" | custom-call | tf_op jit(solution)/shard_map/train_step/pallas_call | solution.py:662
  205.4 1.3 reduce
  206.7 1.4 copy.19
  208.1 1.4 copy.20
  209.5 1.4 copy.21
  211.0 1.4 copy.22
  212.4 2.7 %copy.23 = f32[768,512]{1,0:T(8,128)} copy(f32[768,512]{1,0:T(8,128)} %get-tuple-element.29) | data formatting | bytes 3145728

commit v3 on v2

--- a/solution.py
+++ b/solution.py
@@ -17,6 +17,37 @@
 G_SLOTS = 6
 LANES = 128
 SPILLED = 4
+
+ORDER = (
+    ("a", 4, 0), ("a", 11, 0), ("m", 0, 0), ("a", 2, 0), ("a", 6, 0), ("a", 3, 0), ("a", 0, 0), ("a", 1, 0), ("a", 7, 0), ("a", 5, 0), ("a", 8, 0),
+    ("a", 11, 1), ("a", 9, 0), ("a", 10, 0), ("a", 2, 1), ("a", 5, 1), ("a", 8, 1), ("a", 11, 2), ("a", 4, 1), ("a", 6, 1), ("a", 2, 2), ("a", 3, 1),
+    ("a", 0, 1), ("a", 5, 2), ("a", 8, 2), ("a", 11, 3), ("a", 1, 1), ("a", 7, 1), ("a", 6, 2), ("a", 2, 3), ("a", 9, 1), ("a", 3, 2), ("a", 4, 2),
+    ("a", 5, 3), ("a", 10, 1), ("a", 0, 2), ("a", 8, 3), ("a", 1, 2), ("a", 6, 3), ("a", 11, 4), ("a", 7, 2), ("a", 4, 3), ("a", 2, 4), ("a", 0, 3),
+    ("a", 1, 3), ("a", 5, 4), ("a", 3, 3), ("a", 7, 3), ("a", 11, 5), ("a", 8, 4), ("a", 2, 5), ("a", 10, 2), ("a", 9, 2), ("a", 0, 4), ("a", 1, 4),
+    ("a", 5, 5), ("a", 11, 6), ("a", 6, 4), ("a", 4, 4), ("a", 7, 4), ("a", 3, 4), ("a", 8, 5), ("a", 0, 5), ("a", 1, 5), ("a", 9, 3), ("a", 10, 3),
+    ("a", 2, 6), ("a", 5, 6), ("a", 0, 6), ("d", 0, 0), ("a", 6, 5), ("a", 1, 6), ("d", 1, 0), ("f", 0, 0), ("a", 3, 5), ("a", 11, 7), ("a", 7, 5),
+    ("a", 6, 6), ("d", 6, 0), ("a", 5, 7), ("a", 2, 7), ("a", 4, 5), ("a", 9, 4), ("a", 3, 6), ("d", 3, 0), ("a", 11, 8), ("a", 8, 6), ("d", 11, 0),
+    ("a", 7, 6), ("a", 10, 4), ("a", 5, 8), ("d", 5, 0), ("d", 7, 0), ("a", 2, 8), ("f", 1, 0), ("a", 4, 6), ("a", 9, 5), ("d", 4, 0), ("f", 2, 0),
+    ("a", 9, 6), ("a", 10, 5), ("d", 9, 0), ("d", 2, 0), ("a", 8, 7), ("f", 3, 0), ("a", 10, 6), ("a", 8, 8), ("f", 4, 0), ("f", 5, 0), ("l", 0, 0),
+    ("g", 5, 0), ("g", 5, 1), ("d", 8, 0), ("d", 10, 0), ("g", 5, 2), ("g", 4, 0), ("r", 11, 0), ("g", 4, 1), ("r", 10, 0), ("g", 4, 2), ("g", 3, 0),
+    ("r", 11, 1), ("r", 9, 0), ("g", 3, 1), ("g", 3, 2), ("r", 10, 1), ("r", 8, 0), ("r", 11, 2), ("g", 2, 0), ("r", 7, 0), ("r", 9, 1), ("g", 2, 1),
+    ("r", 8, 1), ("r", 6, 0), ("g", 1, 0), ("r", 11, 3), ("g", 1, 1), ("g", 0, 0), ("r", 11, 4), ("g", 0, 1), ("g", 0, 2), ("r", 11, 5), ("g", 1, 2),
+    ("r", 5, 0), ("r", 6, 1), ("r", 8, 2), ("r", 9, 2), ("r", 1, 0), ("h", 0, 0), ("r", 11, 6), ("r", 0, 0), ("g", 2, 2), ("r", 2, 0), ("r", 7, 1),
+    ("r", 3, 0), ("r", 9, 3), ("r", 5, 1), ("r", 4, 0), ("r", 8, 3), ("r", 2, 1), ("r", 0, 1), ("r", 6, 2), ("u", 11, 0), ("r", 5, 2), ("r", 1, 1),
+    ("r", 7, 2), ("r", 8, 4), ("r", 9, 4), ("r", 3, 1), ("r", 2, 2), ("r", 0, 2), ("r", 10, 2), ("r", 4, 1), ("r", 5, 3), ("r", 7, 3), ("r", 8, 5),
+    ("r", 6, 3), ("b", 11, 0), ("r", 1, 2), ("r", 3, 2), ("r", 2, 3), ("r", 0, 3), ("r", 10, 3), ("r", 5, 4), ("r", 7, 4), ("r", 8, 6), ("u", 9, 0),
+    ("b", 11, 1), ("r", 4, 2), ("r", 6, 4), ("r", 1, 3), ("r", 3, 3), ("r", 2, 4), ("r", 0, 4), ("r", 5, 5), ("b", 11, 2), ("u", 8, 0), ("r", 4, 3),
+    ("r", 1, 4), ("r", 3, 4), ("r", 2, 5), ("r", 5, 6), ("u", 7, 0), ("b", 9, 0), ("r", 4, 4), ("u", 6, 0), ("b", 8, 0), ("r", 2, 6), ("u", 0, 0),
+    ("u", 5, 0), ("b", 11, 3), ("b", 9, 1), ("b", 8, 1), ("u", 1, 0), ("u", 3, 0), ("u", 2, 0), ("b", 7, 0), ("b", 5, 0), ("r", 10, 4), ("u", 4, 0),
+    ("b", 8, 2), ("b", 9, 2), ("b", 6, 0), ("b", 0, 0), ("b", 2, 0), ("b", 5, 1), ("b", 11, 4), ("b", 6, 1), ("b", 1, 0), ("b", 0, 1), ("b", 3, 0),
+    ("b", 7, 1), ("b", 8, 3), ("u", 10, 0), ("n", 0, 0), ("b", 5, 2), ("b", 2, 1), ("b", 4, 0), ("b", 1, 1), ("b", 7, 2), ("b", 0, 2), ("b", 3, 1),
+    ("b", 8, 4), ("b", 2, 2), ("b", 4, 1), ("b", 1, 2), ("b", 5, 3), ("b", 9, 3), ("b", 8, 5), ("b", 10, 0), ("b", 3, 2), ("b", 4, 2), ("b", 0, 3),
+    ("b", 2, 3), ("b", 9, 4), ("b", 5, 4), ("b", 1, 3), ("b", 8, 6), ("b", 9, 5), ("b", 11, 5), ("b", 2, 4), ("b", 8, 7), ("b", 10, 1), ("b", 7, 3),
+    ("b", 6, 2), ("b", 3, 3), ("b", 4, 3), ("b", 5, 5), ("b", 11, 6), ("b", 0, 4), ("b", 1, 4), ("b", 10, 2), ("b", 2, 5), ("b", 11, 7), ("b", 7, 4),
+    ("b", 0, 5), ("b", 1, 5), ("s", 0, 0), ("b", 5, 6), ("b", 4, 4), ("b", 2, 6), ("b", 7, 5), ("b", 3, 4), ("b", 6, 3), ("b", 5, 7), ("b", 10, 3),
+    ("b", 4, 5), ("b", 2, 7), ("b", 3, 5), ("s", 1, 0), ("b", 6, 4), ("s", 2, 0), ("b", 6, 5), ("b", 10, 4), ("s", 3, 0), ("b", 10, 5), ("s", 4, 0),
+    ("s", 5, 0),
+)
 
 
 def start_copy(src, dst, send_sem, recv_sem, dev):
@@ -119,6 +150,8 @@
         for way, n in self.ways(stage):
             if n:
                 self.ring_send(stage, way, 1)
+        if stage == 2:
+            self.swap_start(0)
 
     def ring_step(self, stage, step):
         for way, n in self.ways(stage):
@@ -126,12 +159,15 @@
                 self.ring_wait(stage, way, step)
                 if step < n:
                     self.ring_send(stage, way, step + 1)
+                if stage == 2:
+                    self.swap_start(step * way)
 
     def swap_ref(self, c):
         return self.buf.at[self.u, :, :, :, c]
 
-    def swap_start(self):
-        ref = self.swap_ref(self.p.c)
+    def swap_start(self, k):
+        d = self.order[2]
+        ref = self.block(2, self.p.wrap(self.p.pos[d] - k * self.p.sign, d))
         start_copy(ref, ref, self.send_sem.at[self.u, 3], self.recv_sem.at[self.u, self.last_sem], self.p.sib)
 
     def swap_wait(self):
@@ -143,7 +179,6 @@
             out[-1].append(functools.partial(self.ring_start, stage))
             for step in range(1, self.p.far(self.order[stage]) + 1):
                 out.append([functools.partial(self.ring_step, stage, step)])
-        out[-1].append(self.swap_start)
         out.append([self.swap_wait])
         return out
 
@@ -284,14 +319,17 @@
 
     def to_tiles_start(self, src1, src2):
         p = self.p
-        pltpu.make_async_copy(lanes(src1, p.m), self.one.at[p.m], self.sem(1)).start()
-        pltpu.make_async_copy(lanes(src2, self.mine), self.two.at[self.mine], self.sem(3)).start()
         for k in range(1, self.group):
             j = lax.rem(p.m + k, self.group)
             start_copy(lanes(src1, j), self.one.at[p.m], self.sem(0), self.sem(1), p.base + j)
         for k in range(1, self.half):
             j = lax.rem(self.mine + k, self.half)
             start_copy(lanes(src2, j), self.two.at[self.mine], self.sem(2), self.sem(3), p.base + self.low + j)
+
+    def to_tiles_own(self, src1, src2):
+        p = self.p
+        pltpu.make_async_copy(lanes(src1, p.m), self.one.at[p.m], self.sem(1)).start()
+        pltpu.make_async_copy(lanes(src2, self.mine), self.two.at[self.mine], self.sem(3)).start()
 
     def drain_sends(self):
         wait_bytes(self.one.at[pl.ds(0, self.group - 1)], self.sem(0))
@@ -376,7 +414,7 @@
 
 def step_kernel(grid, batch_scale, w1, w2, m1, m2, x0, y0, x1, y1, nw1, nw2, nm1, nm2, loss, hlast, spill,
                 wbuf, slope, act, hid, h, dlow, g, part, ring_ab, ring_c, rows, tiles3,
-                wone, wtwo, mone, mtwo, wt, mt, lossbuf,
+                wone, wtwo, mone, mtwo, wrow1, wrow2, wt, mt, lossbuf,
                 gsend, grecv, rsend, rrecv, shuf, local):
     p = Place(grid)
     layers = w1.shape[0]
@@ -390,12 +428,19 @@
 
     loads = {"x0": load(x0, act.at[0], 0), "y0": load(y0, dlow, 1),
              "x1": load(x1, act.at[layers - 1], 2), "y1": load(y1, act.at[layers - 2], 3)}
+    stage = [load(w1, wrow1, 2), load(w2, wrow2, 3)]
+    wshuf = Shuffle(p, wone, wtwo, shuf, 0)
+    mshuf = Shuffle(p, mone, mtwo, shuf, 4)
+    for c in stage:
+        c.start()
+    wshuf.to_tiles_own(w1, w2)
+    mshuf.to_tiles_own(m1, m2)
     loads["x0"].start()
     loads["y0"].start()
     enter(p)
-    wshuf = Shuffle(p, wone, wtwo, shuf, 0)
-    mshuf = Shuffle(p, mone, mtwo, shuf, 4)
-    wshuf.to_tiles_start(w1, w2)
+    for c in stage:
+        c.wait()
+    wshuf.to_tiles_start(wrow1, wrow2)
     mshuf.to_tiles_start(m1, m2)
 
     def own_tile(u):
@@ -442,12 +487,13 @@
         row_tiles(tok, body)
 
     gather_args = lambda u: (p, wbuf, u, ORDERS[u % 3], gsend, grecv)
+    slots = gradient_slots()
     first = [Gather(*gather_args(u)) for u in range(units)]
     again = [Gather(*gather_args(u)) for u in range(units)]
     red = []
     for u in range(units):
         ring = (ring_c, u // 3) if u % 3 == 2 else (ring_ab, 2 * (u // 3) + u % 3)
-        red.append(Reduce(p, g, (units - 1 - u) % G_SLOTS, part, ring, rows, tiles3, u, ORDERS[u % 3], rsend, rrecv))
+        red.append(Reduce(p, g, slots[u], part, ring, rows, tiles3, u, ORDERS[u % 3], rsend, rrecv))
 
     def grad_two(l):
         slot = red[2 * l + 1].gslot
@@ -463,7 +509,6 @@
             return 0
 
         lax.fori_loop(0, d_ff // size, step, 0)
-        red[2 * l + 1].swap_start()
 
     def back_hidden(l):
         if l < SPILLED and l + 2 < layers:
@@ -479,6 +524,7 @@
                 dlow[r, :] = d.astype(BF16)
 
         row_tiles(tok, body)
+        red[2 * l + 1].swap_start()
         if 0 <= l - 2 < SPILLED:
             unspill_copy(l - 2).start()
 
@@ -566,9 +612,10 @@
     work["m", 0, 0] = [moments_ready]
     work["h", 0, 0] = [second_start]
     work["n", 0, 0] = [new_rows]
-    for name in order_of(work, layers):
-        for f in work[name]:
+    for name in ORDER:
+        for f in work.pop(name):
             f()
+    assert not work
     out = [load(h, hlast, 0), load(lossbuf, loss, 1)]
     for c in out:
         c.start()
@@ -581,37 +628,14 @@
         c.wait()
 
 
-def order_of(work, layers):
-    units = 2 * layers
-    out = []
-    n = lambda tag, u: sum(1 for k in work if k[0] == tag and k[1] == u)
-    for k in range(12):
-        for u in range(units):
-            if ("a", u, k) in work and k < n("a", u):
-                out.append(("a", u, k))
-    for l in range(layers):
-        out.append(("f", l, 0))
-    for u in range(units):
-        out.append(("d", u, 0))
-    out += [("m", 0, 0), ("l", 0, 0)]
-    for l in reversed(range(layers)):
-        out += [("g", l, 0), ("g", l, 1), ("g", l, 2)]
-        out += [("r", 2 * l + 1, 0), ("r", 2 * l, 0)]
-    for k in range(1, 12):
-        for u in reversed(range(units)):
-            if ("r", u, k) in work:
-                out.append(("r", u, k))
-    for u in range(units):
-        out.append(("u", u, 0))
-    for k in range(12):
-        for u in range(units):
-            if ("b", u, k) in work:
-                out.append(("b", u, k))
-    out.append(("h", 0, 0))
-    out.append(("n", 0, 0))
-    for l in range(layers):
-        out.append(("s", l, 0))
-    return out
+def gradient_slots():
+    free, held = list(range(G_SLOTS)), {}
+    for tag, n, k in ORDER:
+        if tag == "g" and k != 1:
+            held[2 * n + (k == 0)] = free.pop(0)
+        if tag == "r" and k == 0:
+            free.append(held[n])
+    return held
 
 
 def make_step(grid, layers, tok, d_model, d_ff, n_dev):
@@ -640,6 +664,7 @@
         pltpu.VMEM((units, max(ny, nx) - 1, max(nz, nx), *tile), BF16),
         pltpu.VMEM((units, max(nz, nx) - 1, *tile), BF16),
         *shuffled, *shuffled,
+        pltpu.VMEM((layers, 2, d_ff), F32), pltpu.VMEM((layers, 4, d_model), F32),
         pltpu.VMEM((units, *tile), F32), pltpu.VMEM((units, *tile), F32),
         pltpu.VMEM((1, tok), F32),
         dma((units, 4)), dma((units, 12)), dma((units, 4)), dma((units, 12)), dma((8,)), dma((4 + SPILLED,)),
@@ -651,6 +676,15 @@
         name="train_step")
 
 
+def hand_over(*refs):
+    n = len(refs) // 2
+    for src, dst in zip(refs[:n], refs[n:]):
+        if len(dst.shape) < len(src.shape):
+            dst[...] = src[0, :]
+        else:
+            dst[...] = src[...]
+
+
 def solution(mesh):
     n_dev = mesh.shape["data"]
     w_spec = P(None, "data", None)
@@ -659,8 +693,11 @@
     def device_step(w_one, w_two, mom_one, mom_two, x_zero, y_zero, x_one, y_one):
         tok, d_model = x_zero.shape
         step = make_step(GRID, w_one.shape[0], tok, d_model, w_one.shape[2], n_dev)
-        nw1, nw2, nm1, nm2, loss, h_last, _ = step(w_one, w_two, mom_one, mom_two, x_zero, y_zero, x_one, y_one)
-        return nw1, nw2, nm1, nm2, loss.reshape(tok), h_last
+        made = step(w_one, w_two, mom_one, mom_two, x_zero, y_zero, x_one, y_one)[:6]
+        outs = [jax.ShapeDtypeStruct(v.shape, v.dtype) for v in made]
+        outs[4] = jax.ShapeDtypeStruct((tok,), F32)
+        vmem = pl.BlockSpec(memory_space=pltpu.VMEM)
+        return pl.pallas_call(hand_over, out_shape=tuple(outs), in_specs=[vmem] * 6, out_specs=[vmem] * 6, name="hand_over")(*made)
 
     return jax.shard_map(device_step, mesh=mesh, in_specs=(w_spec, w_spec, w_spec, w_spec, row_spec, row_spec, row_spec, row_spec),
                          out_specs=(w_spec, w_spec, w_spec, w_spec, P("data"), row_spec), check_vma=False)

time: 215 us -> 174 us (0.81)
  Pallas kernels: 205 us -> 173 us
  local copies, waits for them, and re-layouts: 8.35 us -> 0 us
    pallas_call x1 -> x2, Pallas kernels: 205 us -> 173 us  [the longest x1 171 us: device_step(): step(w_one, w_two, mom_one, mom_two, x_zero, y_zero, x_one, y_one)[:6]]
    unnamed x5 -> x0, local copies, waits for them, and re-layouts: 8.35 us -> none
where the time goes in v3:
time: 174 us
  Pallas kernels  173 us (99%)
    pallas_call x1, Pallas kernels, device_step(): step(w_one, w_two, mom_one, mom_two, x_zero, y_zero, x_one, y_one)[:6]  171 us

profile of v3, /device:TPU:1, one launch (start us, length us, event | category | flops | bytes accessed | tf_op | source)
XLA Modules:
  0.0 174.0 jit_solution(14709702107535884672)
XLA Ops:
  0.6 170.6 %train_step.1 = (f32[6,2,1024]{2,1,0:T(2,128)}, f32[6,4,512]{2,1,0:T(4,128)}, f32[6,2,1024]{2,1,0:T(2,128)}, f32[6,4,512]{2,1,0:T(4,128)}, f32[1,768]{1,0:T(1,12...) custom-call(f32[6,2,1024]{2,1,0:T(2,128)} %w1.1, f32[6,4,512]{2,1,0:T(4,128)} %w2.1, f32[6,2,1024]{2,1,0:T(2,128)} %m1.1, ...), custom_call_target="tpu_custom_call" | custom-call | tf_op jit(solution)/shard_map/train_step/pallas_call | solution.py:696
  171.2 2.8 %hand_over.1 = (f32[6,2,1024]{2,1,0:T(2,128)}, f32[6,4,512]{2,1,0:T(4,128)}, f32[6,2,1024]{2,1,0:T(2,128)}, f32[6,4,512]{2,1,0:T(4,128)}, f32[768]{0:T(1024)}, /*index=5*/f32[768,512]{1,0:T(8,128)}) custom-call(f32[6,2,1024]{2,1,0:T(2,128)} %get-tuple-element.12.refs_0_, f32[6,4,512]{2,1,0:T(4,128)} %get-tuple-element.13.refs_1_, ...), custom_call_target="tpu_custom_call" | custom-call | tf_op jit(solution)/shard_map/hand_over/pallas_call | solution.py:700

commit v4 on v3

v4 whole, which is shorter than its diff:
```python
import functools
import jax
import jax.numpy as jnp
from jax import lax
from jax.experimental import pallas as pl
from jax.experimental.pallas import tpu as pltpu
from jax.sharding import PartitionSpec as P

LEARN_RATE = 0.1
MOMENTUM = 0.9
F32, BF16 = jnp.float32, jnp.bfloat16
GRID = (8, 4, 4, 2)
ORDERS = (("z", "x", "y"), ("z", "y", "x"), ("x", "y", "z"))
GELU_SCALE = 0.7978845608028654
GELU_CUBE = 0.044715
G_SLOTS = 6
LANES = 128
SPILLED = 4

ORDER = (
    ("a", 8, 0), ("a", 9, 0), ("a", 1, 0), ("a", 0, 0), ("a", 2, 0), ("a", 4, 0), ("a", 3, 0), ("m", 0, 0), ("a", 5, 0), ("a", 11, 0), ("a", 7, 0),
    ("a", 8, 1), ("a", 10, 0), ("a", 6, 0), ("a", 2, 1), ("a", 5, 1), ("a", 11, 1), ("a", 9, 1), ("a", 1, 1), ("a", 0, 1), ("a", 8, 2), ("a", 4, 1),
    ("a", 2, 2), ("a", 3, 1), ("a", 5, 2), ("a", 7, 1), ("a", 11, 2), ("a", 10, 1), ("a", 6, 1), ("a", 1, 2), ("a", 8, 3), ("a", 0, 2), ("a", 2, 3),
    ("a", 4, 2), ("a", 3, 2), ("a", 5, 3), ("a", 7, 2), ("a", 11, 3), ("a", 1, 3), ("a", 0, 3), ("a", 2, 4), ("a", 8, 4), ("a", 6, 2), ("a", 5, 4),
    ("a", 4, 3), ("a", 3, 3), ("a", 11, 4), ("a", 0, 4), ("a", 2, 5), ("a", 7, 3), ("a", 0, 5), ("d", 0, 0), ("a", 9, 2), ("a", 1, 4), ("a", 8, 5),
    ("a", 10, 2), ("a", 5, 5), ("a", 6, 3), ("a", 4, 4), ("a", 1, 5), ("f", 0, 0), ("a", 2, 6), ("a", 3, 4), ("a", 7, 4), ("a", 4, 5), ("a", 11, 5),
    ("d", 1, 0), ("d", 4, 0), ("a", 5, 6), ("a", 8, 6), ("a", 9, 3), ("a", 2, 7), ("d", 2, 0), ("a", 3, 5), ("f", 1, 0), ("a", 8, 7), ("a", 6, 4),
    ("a", 7, 5), ("d", 7, 0), ("a", 10, 3), ("a", 5, 7), ("f", 2, 0), ("a", 9, 4), ("a", 6, 5), ("d", 6, 0), ("d", 3, 0), ("a", 11, 6), ("d", 8, 0),
    ("f", 3, 0), ("a", 9, 5), ("a", 10, 4), ("d", 9, 0), ("a", 11, 7), ("d", 11, 0), ("f", 4, 0), ("a", 10, 5), ("d", 10, 0), ("d", 5, 0),
    ("f", 5, 0), ("l", 0, 0), ("g", 5, 0), ("g", 5, 1), ("g", 4, 0), ("g", 4, 1), ("g", 4, 2), ("g", 5, 2), ("r", 11, 0), ("g", 3, 0), ("r", 8, 0),
    ("g", 3, 1), ("g", 3, 2), ("r", 11, 1), ("r", 10, 0), ("r", 9, 0), ("r", 8, 1), ("g", 2, 0), ("r", 7, 0), ("r", 6, 0), ("g", 2, 1), ("r", 11, 2),
    ("g", 1, 0), ("r", 8, 2), ("g", 1, 1), ("r", 10, 1), ("r", 5, 0), ("g", 0, 0), ("r", 6, 1), ("r", 7, 1), ("r", 8, 3), ("g", 1, 2), ("r", 3, 0),
    ("r", 11, 3), ("g", 0, 1), ("r", 5, 1), ("r", 6, 2), ("r", 8, 4), ("r", 7, 2), ("r", 2, 0), ("g", 0, 2), ("g", 2, 2), ("r", 1, 0), ("r", 10, 2),
    ("h", 0, 0), ("r", 5, 2), ("r", 3, 1), ("r", 8, 5), ("r", 6, 3), ("r", 2, 1), ("r", 4, 0), ("r", 0, 0), ("r", 7, 3), ("r", 5, 3), ("r", 1, 1),
    ("r", 10, 3), ("r", 11, 4), ("u", 8, 0), ("r", 2, 2), ("r", 9, 1), ("r", 3, 2), ("u", 6, 0), ("r", 5, 4), ("r", 4, 1), ("r", 0, 1), ("u", 7, 0),
    ("r", 1, 2), ("r", 2, 3), ("r", 11, 5), ("r", 9, 2), ("b", 8, 0), ("u", 10, 0), ("r", 3, 3), ("r", 5, 5), ("r", 4, 2), ("r", 0, 2), ("r", 2, 4),
    ("b", 6, 0), ("u", 11, 0), ("b", 7, 0), ("r", 1, 3), ("b", 8, 1), ("u", 5, 0), ("b", 10, 0), ("r", 4, 3), ("u", 3, 0), ("r", 0, 3), ("r", 2, 5),
    ("b", 6, 1), ("b", 5, 0), ("b", 7, 1), ("b", 8, 2), ("u", 1, 0), ("b", 11, 0), ("u", 2, 0), ("r", 9, 3), ("b", 10, 1), ("u", 4, 0), ("b", 8, 3),
    ("b", 6, 2), ("b", 3, 0), ("u", 0, 0), ("b", 5, 1), ("b", 2, 0), ("b", 11, 1), ("b", 1, 0), ("b", 7, 2), ("b", 8, 4), ("b", 6, 3), ("b", 10, 2),
    ("b", 4, 0), ("u", 9, 0), ("n", 0, 0), ("b", 2, 1), ("b", 5, 2), ("b", 6, 4), ("b", 3, 1), ("b", 0, 0), ("b", 7, 3), ("b", 1, 1), ("b", 11, 2),
    ("b", 8, 5), ("b", 7, 4), ("b", 10, 3), ("b", 8, 6), ("b", 10, 4), ("b", 2, 2), ("b", 4, 1), ("b", 9, 0), ("b", 0, 1), ("b", 5, 3), ("b", 3, 2),
    ("b", 11, 3), ("b", 1, 2), ("b", 2, 3), ("b", 5, 4), ("b", 0, 2), ("b", 4, 2), ("b", 11, 4), ("b", 3, 3), ("b", 2, 4), ("b", 9, 1), ("b", 1, 3),
    ("b", 5, 5), ("b", 3, 4), ("b", 0, 3), ("b", 11, 5), ("b", 4, 3), ("b", 1, 4), ("b", 5, 6), ("b", 2, 5), ("b", 0, 4), ("s", 0, 0), ("b", 2, 6),
    ("b", 11, 6), ("b", 4, 4), ("b", 9, 2), ("s", 1, 0), ("s", 2, 0), ("b", 9, 3), ("s", 3, 0), ("b", 9, 4), ("s", 4, 0), ("s", 5, 0),
)


def start_copy(src, dst, send_sem, recv_sem, dev):
    pltpu.make_async_remote_copy(src_ref=src, dst_ref=dst, send_sem=send_sem, recv_sem=recv_sem,
                                 device_id=(dev,), device_id_type=pl.DeviceIdType.MESH).start()


def wait_bytes(ref, sem):
    pltpu.make_async_copy(ref, ref, sem).wait()


class Place:
    def __init__(self, grid):
        self.grid = grid
        nz, ny, nx, nc = grid
        me = lax.axis_index("data")
        self.me = me
        self.c = lax.rem(me, nc)
        self.x = lax.rem(me // nc, nx)
        self.y = lax.rem(me // (nc * nx), ny)
        self.z = me // (nc * nx * ny)
        self.sign = 1 - 2 * self.c
        self.size = {"z": nz, "y": ny, "x": nx}
        self.pos = {"z": self.z, "y": self.y, "x": self.x}
        self.stride = {"z": ny * nx * nc, "y": nx * nc, "x": nc}
        self.sib = me + 1 - 2 * self.c
        self.m = lax.rem(me, nc * nx)
        self.base = me - self.m

    def wrap(self, v, d):
        n = self.size[d]
        return lax.rem(v + 2 * n, n)

    def dev(self, d, v):
        return self.me + (v - self.pos[d]) * self.stride[d]

    def far(self, d):
        return self.size[d] // 2

    def near(self, d):
        return (self.size[d] - 1) // 2


def block_of(buf, lead, place, done, d, v, tail=()):
    idx = []
    for k in ("z", "y", "x"):
        if k in done:
            idx.append(slice(None))
        elif k == d:
            idx.append(v)
        else:
            idx.append(place.pos[k])
    return buf.at[(*lead, *idx, *tail)]


def ring_sem(place, d, way, step):
    return step - 1 if way == 1 else place.far(d) + step - 1


class Gather:
    def __init__(self, place, buf, u, order, send_sem, recv_sem):
        self.p, self.buf, self.u, self.order = place, buf, u, order
        self.send_sem, self.recv_sem = send_sem, recv_sem
        self.last_sem = 2 + max(place.size[order[2]] - 1, 1)

    def block(self, stage, v):
        return block_of(self.buf, (self.u,), self.p, self.order[:stage], self.order[stage], v, (self.p.c,))

    def many(self, stage):
        return self.block(stage, pl.ds(0, self.p.size[self.order[stage]] - 1))

    def direct_start(self, stage):
        p, d = self.p, self.order[stage]
        own = self.block(stage, p.pos[d])
        for k in range(1, p.size[d]):
            start_copy(own, own, self.send_sem.at[self.u, stage], self.recv_sem.at[self.u, stage], p.dev(d, p.wrap(p.pos[d] + k, d)))

    def direct_wait(self, stage):
        if self.p.size[self.order[stage]] > 1:
            wait_bytes(self.many(stage), self.recv_sem.at[self.u, stage])

    def ring_send(self, way, step):
        p, d = self.p, self.order[2]
        s = p.sign * way
        ref = self.block(2, p.wrap(p.pos[d] - (step - 1) * s, d))
        start_copy(ref, ref, self.send_sem.at[self.u, 2], self.recv_sem.at[self.u, 2 + ring_sem(p, d, way, step)], p.dev(d, p.wrap(p.pos[d] + s, d)))

    def ways(self):
        d = self.order[2]
        return ((1, self.p.far(d)), (-1, self.p.near(d)))

    def ring_start(self):
        for way, n in self.ways():
            if n:
                self.ring_send(way, 1)
        self.swap_start(0)

    def ring_step(self, step):
        p, d = self.p, self.order[2]
        for way, n in self.ways():
            if step <= n:
                ref = self.block(2, p.wrap(p.pos[d] - step * p.sign * way, d))
                wait_bytes(ref, self.recv_sem.at[self.u, 2 + ring_sem(p, d, way, step)])
                if step < n:
                    self.ring_send(way, step + 1)
                self.swap_start(step * way)

    def swap_ref(self, c):
        return self.buf.at[self.u, :, :, :, c]

    def swap_start(self, k):
        d = self.order[2]
        ref = self.block(2, self.p.wrap(self.p.pos[d] - k * self.p.sign, d))
        start_copy(ref, ref, self.send_sem.at[self.u, 3], self.recv_sem.at[self.u, self.last_sem], self.p.sib)

    def swap_wait(self):
        wait_bytes(self.swap_ref(1 - self.p.c), self.recv_sem.at[self.u, self.last_sem])

    def events(self):
        part = functools.partial
        out = [[part(self.direct_start, 0)],
               [part(self.direct_wait, 0), part(self.direct_start, 1)],
               [part(self.direct_wait, 1), self.ring_start]]
        out += [[part(self.ring_step, step)] for step in range(1, self.p.far(self.order[2]) + 1)]
        return out + [[self.swap_wait]]

    def drain(self):
        for stage in range(3):
            if self.p.size[self.order[stage]] > 1:
                wait_bytes(self.many(stage), self.send_sem.at[self.u, stage])
        wait_bytes(self.swap_ref(self.p.c), self.send_sem.at[self.u, 3])


def add_into(dst, *srcs):
    total = dst[...].astype(F32)
    for s in srcs:
        total = total + s[...].astype(F32)
    dst[...] = total.astype(BF16)


class Reduce:
    def __init__(self, place, g, gslot, part, rings, rows, tiles, u, order, send_sem, recv_sem):
        self.p, self.g, self.gslot, self.part, self.u, self.order = place, g, gslot, part, u, order
        self.ring = lambda k: rings[0].at[rings[1], k]
        n0 = place.size[order[0]]
        self.rows = lambda k: rows.at[u, k, pl.ds(0, n0)]
        self.tiles = lambda k: tiles.at[u, k]
        self.send_sem, self.recv_sem = send_sem, recv_sem
        self.first_sem = 3

    def block(self, stage, v):
        return block_of(self.part, (self.u,), self.p, self.order[:stage], self.order[stage], v)

    def swap_start(self):
        start_copy(self.g.at[self.gslot, :, :, :, 1 - self.p.c], self.part.at[self.u],
                   self.send_sem.at[self.u, 3], self.recv_sem.at[self.u, 0], self.p.sib)

    def swap_wait(self):
        wait_bytes(self.part.at[self.u], self.recv_sem.at[self.u, 0])
        p = self.p

        def add(k, _):
            add_into(self.part.at[self.u, k], self.g.at[self.gslot, k, :, :, p.c])
            return 0

        lax.fori_loop(0, p.size["z"], add, 0)
        wait_bytes(self.part.at[self.u], self.send_sem.at[self.u, 3])

    def ways(self):
        d = self.order[2]
        return ((1, self.p.far(d)), (-1, self.p.near(d)))

    def ring_send(self, way, step, n):
        p, d = self.p, self.order[2]
        s = p.sign * way
        k = ring_sem(p, d, way, step)
        src = self.block(2, p.wrap(p.pos[d] + n * s, d)) if step == 1 else self.ring(k - 1)
        start_copy(src, self.ring(k), self.send_sem.at[self.u, 2], self.recv_sem.at[self.u, self.first_sem + k],
                   p.dev(d, p.wrap(p.pos[d] + s, d)))

    def ring_start(self):
        for way, n in self.ways():
            if n:
                self.ring_send(way, 1, n)

    def ring_step(self, step):
        p, d = self.p, self.order[2]
        for way, n in self.ways():
            if step <= n:
                k = ring_sem(p, d, way, step)
                wait_bytes(self.ring(k), self.recv_sem.at[self.u, self.first_sem + k])
                if step < n:
                    add_into(self.ring(k), self.block(2, p.wrap(p.pos[d] + (n - step) * p.sign * way, d)))
                    self.ring_send(way, step + 1, n)
        if step == p.far(d):
            add_into(self.block(2, p.pos[d]), *[self.ring(ring_sem(p, d, way, n)) for way, n in self.ways() if n])

    def direct_start(self, stage):
        p, d = self.p, self.order[stage]
        land = self.rows if stage == 1 else self.tiles
        for k in range(1, p.size[d]):
            v = p.wrap(p.pos[d] + k, d)
            start_copy(self.block(stage, v), land(k - 1), self.send_sem.at[self.u, stage], self.recv_sem.at[self.u, 1 + stage], p.dev(d, v))

    def direct_wait(self, stage, sems, first):
        n = self.p.size[self.order[stage]]
        if n > 1:
            wait_bytes((self.rows if stage == 1 else self.tiles)(pl.ds(0, n - 1)), sems.at[self.u, first])

    def row_sum(self):
        self.direct_wait(1, self.recv_sem, 2)
        n = self.p.size[self.order[1]]
        if n > 1:
            add_into(self.block(1, self.p.pos[self.order[1]]), *[self.rows(k) for k in range(n - 1)])

    def tile_sum(self):
        self.direct_wait(0, self.recv_sem, 1)
        total = self.block(0, self.p.pos[self.order[0]])[...].astype(F32)
        for k in range(self.p.size[self.order[0]] - 1):
            total = total + self.tiles(k)[...].astype(F32)
        return total.astype(BF16).astype(F32)

    def events(self):
        part = functools.partial
        out = [[self.swap_wait, self.ring_start]]
        out += [[part(self.ring_step, step)] for step in range(1, self.p.far(self.order[2]) + 1)]
        out[-1].append(part(self.direct_start, 1))
        return out + [[self.row_sum, part(self.direct_start, 0)]]

    def drain(self):
        n = self.p.size[self.order[2]] - 1
        if n:
            wait_bytes(self.block(2, pl.ds(0, n)), self.send_sem.at[self.u, 2])
        self.direct_wait(1, self.send_sem, 1)
        self.direct_wait(0, self.send_sem, 0)


def enter(p):
    barrier = pltpu.get_barrier_semaphore()
    group = p.grid[2] * p.grid[3]
    peers = [p.base + lax.rem(p.m + k, group) for k in range(1, group)]
    for d in ("y", "z"):
        peers += [p.dev(d, p.wrap(p.pos[d] + k, d)) for k in range(1, p.size[d])]
    for peer in peers:
        pl.semaphore_signal(barrier, inc=1, device_id=(peer,), device_id_type=pl.DeviceIdType.MESH)
    pl.semaphore_wait(barrier, len(peers))


def lanes(ref, j):
    return ref.at[:, :, pl.ds(pl.multiple_of(j * LANES, LANES), LANES)]


class Shuffle:
    def __init__(self, place, one, two, sems, k0):
        self.p, self.one, self.two = place, one, two
        self.sem = lambda k: sems.at[k0 + k]
        self.group = place.grid[2] * place.grid[3]
        self.half = self.group // 2
        self.low = (place.m // self.half) * self.half
        self.mine = place.m - self.low

    def to_tiles_start(self, src1, src2):
        p = self.p
        for k in range(1, self.group):
            j = lax.rem(p.m + k, self.group)
            start_copy(lanes(src1, j), self.one.at[p.m], self.sem(0), self.sem(1), p.base + j)
        for k in range(1, self.half):
            j = lax.rem(self.mine + k, self.half)
            start_copy(lanes(src2, j), self.two.at[self.mine], self.sem(2), self.sem(3), p.base + self.low + j)

    def to_tiles_own(self, src1, src2):
        p = self.p
        pltpu.make_async_copy(lanes(src1, p.m), self.one.at[p.m], self.sem(1)).start()
        pltpu.make_async_copy(lanes(src2, self.mine), self.two.at[self.mine], self.sem(3)).start()

    def drain_sends(self):
        wait_bytes(self.one.at[pl.ds(0, self.group - 1)], self.sem(0))
        wait_bytes(self.two.at[pl.ds(0, self.half - 1)], self.sem(2))

    def to_tiles_finish(self, tiles):
        wait_bytes(self.one, self.sem(1))
        wait_bytes(self.two, self.sem(3))
        for l in range(self.one.shape[1]):
            for m in range(self.group):
                tiles[2 * l, 2 * m:2 * m + 2, :] = self.one[m, l]
            for m in range(self.half):
                tiles[2 * l + 1, 4 * m:4 * m + 4, :] = self.two[m, l]

    def put_rows(self, u, tile):
        if u % 2 == 0:
            for m in range(self.group):
                self.one[m, u // 2] = tile[2 * m:2 * m + 2, :]
        else:
            for m in range(self.half):
                self.two[m, u // 2] = tile[4 * m:4 * m + 4, :]

    def to_rows_start(self, dst1, dst2):
        p = self.p
        pltpu.make_async_copy(self.one.at[p.m], lanes(dst1, p.m), self.sem(1)).start()
        pltpu.make_async_copy(self.two.at[self.mine], lanes(dst2, self.mine), self.sem(3)).start()
        for k in range(1, self.group):
            j = lax.rem(p.m + k, self.group)
            start_copy(self.one.at[j], lanes(dst1, p.m), self.sem(0), self.sem(1), p.base + j)
        for k in range(1, self.half):
            j = lax.rem(self.mine + k, self.half)
            start_copy(self.two.at[j], lanes(dst2, self.mine), self.sem(2), self.sem(3), p.base + self.low + j)

    def to_rows_finish(self):
        wait_bytes(self.one, self.sem(1))
        wait_bytes(self.two, self.sem(3))
        self.drain_sends()


def w_one_of(wbuf, l):
    nz, ny, nx, nc = wbuf.shape[1:5]
    cols = [wbuf[2 * l, :, :, m // nc, m % nc].reshape(nz * ny * 16, LANES) for m in range(nx * nc)]
    return jnp.concatenate(cols, axis=1)


def w_two_of(wbuf, l):
    nz, ny, nx, nc = wbuf.shape[1:5]
    half = nx * nc // 2
    cols = []
    for b in range(half):
        pair = [wbuf[2 * l + 1, :, :, (r * half + b) // nc, b % nc].reshape(nz * ny, 1, 16, LANES) for r in range(2)]
        cols.append(jnp.concatenate(pair, axis=1).reshape(nz * ny * 32, LANES))
    return jnp.concatenate(cols, axis=1)


def contract(a, b, da, db):
    return lax.dot_general(a, b, (((da,), (db,)), ((), ())), preferred_element_type=F32)


def gelu_and_slope(u):
    u2 = u * u
    t = jnp.tanh(GELU_SCALE * (u + GELU_CUBE * (u * u2)))
    half = 0.5 * (1.0 + t)
    slope = half + (0.5 * u) * (1.0 - t * t) * (GELU_SCALE + (3.0 * GELU_CUBE * GELU_SCALE) * u2)
    return u * half, slope


def gelu(u):
    return u * (0.5 * (1.0 + jnp.tanh(GELU_SCALE * (u + GELU_CUBE * (u * u * u)))))


def step_kernel(grid, batch_scale, w1, w2, m1, m2, x0, y0, x1, y1, nw1, nw2, nm1, nm2, loss, hlast, spill,
                wbuf, slope, act, hid, h, dlow, g, part, ring_ab, ring_c, rows, tiles3,
                wone, wtwo, mone, mtwo, wrow1, wrow2, wt, mt, lossbuf,
                gsend, grecv, rsend, rrecv, shuf, local):
    p = Place(grid)
    layers = w1.shape[0]
    units = 2 * layers
    nz, ny, nx, nc = grid
    tok, d_model = h.shape
    d_ff = hid.shape[2]

    def load(src, dst, k):
        return pltpu.make_async_copy(src, dst, local.at[k])

    loads = {"x0": load(x0, act.at[0], 0), "y0": load(y0, dlow, 1),
             "x1": load(x1, act.at[layers - 1], 2), "y1": load(y1, act.at[layers - 2], 3)}
    stage = [load(w1, wrow1, 2), load(w2, wrow2, 3)]
    wshuf = Shuffle(p, wone, wtwo, shuf, 0)
    mshuf = Shuffle(p, mone, mtwo, shuf, 4)
    for c in stage:
        c.start()
    wshuf.to_tiles_own(w1, w2)
    mshuf.to_tiles_own(m1, m2)
    loads["x0"].start()
    loads["y0"].start()
    enter(p)
    for c in stage:
        c.wait()
    wshuf.to_tiles_start(wrow1, wrow2)
    mshuf.to_tiles_start(m1, m2)

    def own_tile(u):
        wbuf[u, p.z, p.y, p.x, p.c] = wt[u].astype(BF16)

    wshuf.to_tiles_finish(wt)
    for u in range(units):
        own_tile(u)
    loads["x0"].wait()
    h[...] = act[0].astype(F32)

    def spill_copy(l):
        return load(slope.at[lax.rem(l, 2)], spill.at[l], 4 + l)

    def unspill_copy(l):
        return load(spill.at[l], slope.at[l % 2], 4 + l)

    def forward_one(l):
        @pl.when(jnp.logical_and(l >= 2, l < SPILLED + 2))
        def _():
            spill_copy(l - 2).wait()

        a = h[...].astype(BF16)
        act[l] = a
        z, s = gelu_and_slope(jnp.dot(a, w_one_of(wbuf, l), preferred_element_type=F32))
        z = z.astype(BF16)
        slope[lax.rem(l, 2)] = s
        hid[l] = z
        h[...] += jnp.dot(z, w_two_of(wbuf, l), preferred_element_type=F32)

        @pl.when(l < SPILLED)
        def _():
            spill_copy(l).start()

    def loss_slope():
        loads["y0"].wait()
        d = (h[...] - dlow[...].astype(F32)) * batch_scale
        h[...] = d
        dlow[...] = d.astype(BF16)

    gather_args = lambda u: (p, wbuf, u, ORDERS[u % 3], gsend, grecv)
    slots = gradient_slots()
    first = [Gather(*gather_args(u)) for u in range(units)]
    again = [Gather(*gather_args(u)) for u in range(units)]
    red = []
    for u in range(units):
        ring = (ring_c, u // 3) if u % 3 == 2 else (ring_ab, 2 * (u // 3) + u % 3)
        red.append(Reduce(p, g, slots[u], part, ring, rows, tiles3, u, ORDERS[u % 3], rsend, rrecv))

    def grad_two(l):
        slot = red[2 * l + 1].gslot
        half = nx * nc // 2
        v = contract(hid[l], dlow[...], 0, 0).astype(BF16).reshape(nz, ny, 2, 16, d_model)
        for b in range(half):
            for r in range(2):
                g[slot, :, :, (r * half + b) // nc, b % nc] = v[:, :, r, :, LANES * b:LANES * b + LANES]

    def back_hidden(l):
        if l + 2 < layers:
            unspill_copy(l).wait()
        q = contract(dlow[...], w_two_of(wbuf, l), 1, 1)
        v = (slope[l % 2] * q).astype(BF16)
        hid[l] = v
        if l:
            d = h[...] + contract(v, w_one_of(wbuf, l), 1, 1)
            h[...] = d
            dlow[...] = d.astype(BF16)
        red[2 * l + 1].swap_start()
        if l >= 2:
            unspill_copy(l - 2).start()

    def grad_one(l):
        slot = red[2 * l].gslot
        v = contract(act[l], hid[l], 0, 0).astype(BF16).reshape(nz, ny, 16, d_ff)
        for m in range(nx * nc):
            g[slot, :, :, m // nc, m % nc] = v[:, :, :, LANES * m:LANES * m + LANES]
        red[2 * l].swap_start()
        if l == layers - 1:
            loads["x1"].start()
        if l == layers - 2:
            loads["y1"].start()

    def update(u):
        total = red[u].tile_sum()
        mom = MOMENTUM * mt[u] + total
        w = wt[u] - LEARN_RATE * mom
        wbuf[u, p.z, p.y, p.x, p.c] = w.astype(BF16)
        wt[u] = w
        mt[u] = mom
        again[u].direct_start(0)

    def moments_ready():
        mshuf.to_tiles_finish(mt)
        mshuf.drain_sends()
        wshuf.drain_sends()

    def second_start():
        loads["x1"].wait()
        h[...] = act[layers - 1].astype(F32)

    def forward_two(l):
        z = gelu(jnp.dot(h[...].astype(BF16), w_one_of(wbuf, l), preferred_element_type=F32)).astype(BF16)
        v = h[...] + jnp.dot(z, w_two_of(wbuf, l), preferred_element_type=F32)
        h[...] = v
        return v

    def forward_last():
        loads["y1"].wait()
        e = forward_two(layers - 1) - act[layers - 2].astype(F32)
        e = e * e
        s = e[:, :LANES]
        for k in range(1, d_model // LANES):
            s = s + e[:, LANES * k:LANES * k + LANES]
        lossbuf[...] = jnp.sum(s.T, axis=0, keepdims=True) * (1.0 / (2 * d_model))

    def new_rows():
        for u in range(units):
            wshuf.put_rows(u, wt[u])
            mshuf.put_rows(u, mt[u])
        wshuf.to_rows_start(nw1, nw2)
        mshuf.to_rows_start(nm1, nm2)

    work = {}
    for u in range(units):
        for k, ev in enumerate(first[u].events()):
            work["a", u, k] = ev
        for k, ev in enumerate(red[u].events()):
            work["r", u, k] = ev
        work["u", u, 0] = [functools.partial(update, u)]
        for k, ev in enumerate(again[u].events()[1:]):
            work["b", u, k] = ev
        work["d", u, 0] = [first[u].drain]
    for l in range(layers):
        work["g", l, 0] = [functools.partial(grad_two, l)]
        work["g", l, 1] = [functools.partial(back_hidden, l)]
        work["g", l, 2] = [functools.partial(grad_one, l)]
    work["s", layers - 1, 0] = [forward_last]
    work["l", 0, 0] = [loss_slope]
    work["m", 0, 0] = [moments_ready]
    work["h", 0, 0] = [second_start]
    work["n", 0, 0] = [new_rows]

    def do(names):
        for name in names:
            for f in work.pop(name):
                f()

    def layer_loop(tag, n, body):
        first = ORDER.index((tag, 0, 0))
        do(ORDER[done[0]:first])
        ends = [ORDER.index((tag, l, 0)) for l in range(n)]

        def step(l, _):
            for k in range(1, n):
                names = ORDER[ends[k - 1] + 1:ends[k]]
                if names:
                    pl.when(l == k)(functools.partial(do, names))
            body(l)
            return 0

        lax.fori_loop(0, n, step, 0)
        done[0] = ends[-1] + 1

    done = [0]
    layer_loop("f", layers, forward_one)

    def forward_step(l):
        forward_two(l)

    layer_loop("s", layers - 1, forward_step)
    do(ORDER[done[0]:])
    assert not work
    out = [load(h, hlast, 0), load(lossbuf, loss, 1)]
    for c in out:
        c.start()
    for u in range(units):
        again[u].drain()
        red[u].drain()
    wshuf.to_rows_finish()
    mshuf.to_rows_finish()
    for c in out:
        c.wait()


def gradient_slots():
    free, held = list(range(G_SLOTS)), {}
    for tag, n, k in ORDER:
        if tag == "g" and k != 1:
            held[2 * n + (k == 0)] = free.pop(0)
        if tag == "r" and k == 0:
            free.append(held[n])
    return held


def make_step(grid, layers, tok, d_model, d_ff, n_dev):
    nz, ny, nx, nc = grid
    units = 2 * layers
    group = nx * nc
    hbm = pl.BlockSpec(memory_space=pl.ANY)
    sds = jax.ShapeDtypeStruct
    tile = (16, LANES)
    dma = pltpu.SemaphoreType.DMA
    thirds = (units + 2) // 3
    outs = (sds((layers, 2, d_ff), F32), sds((layers, 4, d_model), F32), sds((layers, 2, d_ff), F32), sds((layers, 4, d_model), F32),
            sds((1, tok), F32), sds((tok, d_model), F32), sds((SPILLED, tok, d_ff), F32))
    shuffled = [pltpu.VMEM((group, layers, 2, LANES), F32), pltpu.VMEM((group // 2, layers, 4, LANES), F32)]
    scratch = [
        pltpu.VMEM((units, *grid, *tile), BF16),
        pltpu.VMEM((2, tok, d_ff), F32),
        pltpu.VMEM((layers, tok, d_model), BF16),
        pltpu.VMEM((layers, tok, d_ff), BF16),
        pltpu.VMEM((tok, d_model), F32),
        pltpu.VMEM((tok, d_model), BF16),
        pltpu.VMEM((G_SLOTS, *grid, *tile), BF16),
        pltpu.VMEM((units, nz, ny, nx, *tile), BF16),
        pltpu.VMEM((2 * thirds, nx - 1, nz, ny, *tile), BF16),
        pltpu.VMEM((thirds, nz - 1, ny, nx, *tile), BF16),
        pltpu.VMEM((units, max(ny, nx) - 1, max(nz, nx), *tile), BF16),
        pltpu.VMEM((units, max(nz, nx) - 1, *tile), BF16),
        *shuffled, *shuffled,
        pltpu.VMEM((layers, 2, d_ff), F32), pltpu.VMEM((layers, 4, d_model), F32),
        pltpu.VMEM((units, *tile), F32), pltpu.VMEM((units, *tile), F32),
        pltpu.VMEM((1, tok), F32),
        dma((units, 4)), dma((units, 10)), dma((units, 4)), dma((units, 10)), dma((8,)), dma((4 + SPILLED,)),
    ]
    return pl.pallas_call(
        functools.partial(step_kernel, grid, 1.0 / (n_dev * tok * d_model)),
        out_shape=outs, in_specs=[hbm] * 8, out_specs=[hbm] * 7, scratch_shapes=scratch,
        compiler_params=pltpu.CompilerParams(collective_id=0, has_side_effects=True, vmem_limit_bytes=67043328),
        name="train_step")


def hand_over(*refs):
    n = len(refs) // 2
    for src, dst in zip(refs[:n], refs[n:]):
        if len(dst.shape) < len(src.shape):
            dst[...] = src[0, :]
        else:
            dst[...] = src[...]


def solution(mesh):
    n_dev = mesh.shape["data"]
    w_spec = P(None, "data", None)
    row_spec = P("data", None)

    def device_step(w_one, w_two, mom_one, mom_two, x_zero, y_zero, x_one, y_one):
        tok, d_model = x_zero.shape
        step = make_step(GRID, w_one.shape[0], tok, d_model, w_one.shape[2], n_dev)
        made = step(w_one, w_two, mom_one, mom_two, x_zero, y_zero, x_one, y_one)[:6]
        outs = [jax.ShapeDtypeStruct(v.shape, v.dtype) for v in made]
        outs[4] = jax.ShapeDtypeStruct((tok,), F32)
        vmem = pl.BlockSpec(memory_space=pltpu.VMEM)
        return pl.pallas_call(hand_over, out_shape=tuple(outs), in_specs=[vmem] * 6, out_specs=[vmem] * 6, name="hand_over")(*made)

    return jax.shard_map(device_step, mesh=mesh, in_specs=(w_spec, w_spec, w_spec, w_spec, row_spec, row_spec, row_spec, row_spec),
                         out_specs=(w_spec, w_spec, w_spec, w_spec, P("data"), row_spec), check_vma=False)
```

time: 174 us -> 155 us (0.89)
  Pallas kernels: 173 us -> 155 us
    pallas_call x1, Pallas kernels: 171 us -> 152 us  [device_step(): step(w_one, w_two, mom_one, mom_two, x_zero, y_zero, x_one, y_one)[:6]]
where the time goes in v4:
time: 155 us
  Pallas kernels  155 us (100%)
    pallas_call x1, Pallas kernels, device_step(): step(w_one, w_two, mom_one, mom_two, x_zero, y_zero, x_one, y_one)[:6]  152 us

profile of v4, /device:TPU:1, one launch (start us, length us, event | category | flops | bytes accessed | tf_op | source)
XLA Modules:
  0.0 155.4 jit_solution(9953294015321204715)
XLA Ops:
  0.6 151.9 %train_step.1 = (f32[6,2,1024]{2,1,0:T(2,128)}, f32[6,4,512]{2,1,0:T(4,128)}, f32[6,2,1024]{2,1,0:T(2,128)}, f32[6,4,512]{2,1,0:T(4,128)}, f32[1,768]{1,0:T(1,12...) custom-call(f32[6,2,1024]{2,1,0:T(2,128)} %w1.1, f32[6,4,512]{2,1,0:T(4,128)} %w2.1, f32[6,2,1024]{2,1,0:T(2,128)} %m1.1, ...), custom_call_target="tpu_custom_call" | custom-call | tf_op jit(solution)/shard_map/train_step/pallas_call | solution.py:669
  152.6 2.8 %hand_over.1 = (f32[6,2,1024]{2,1,0:T(2,128)}, f32[6,4,512]{2,1,0:T(4,128)}, f32[6,2,1024]{2,1,0:T(2,128)}, f32[6,4,512]{2,1,0:T(4,128)}, f32[768]{0:T(1024)}, /*index=5*/f32[768,512]{1,0:T(8,128)}) custom-call(f32[6,2,1024]{2,1,0:T(2,128)} %get-tuple-element.12.refs_0_, f32[6,4,512]{2,1,0:T(4,128)} %get-tuple-element.13.refs_1_, ...), custom_call_target="tpu_custom_call" | custom-call | tf_op jit(solution)/shard_map/hand_over/pallas_call | solution.py:673

commit v5 on v4

--- a/solution.py
+++ b/solution.py
@@ -10,7 +10,8 @@
 MOMENTUM = 0.9
 F32, BF16 = jnp.float32, jnp.bfloat16
 GRID = (8, 4, 4, 2)
-ORDERS = (("z", "x", "y"), ("z", "y", "x"), ("x", "y", "z"))
+ORDERS = (("z", "x", "y"), ("z", "y", "x"), ("x", "y", "z"), ("y", "x", "z"))
+COLOURS = (0, 1, 2, 0, 1, 3, 0, 1, 2, 0, 1, 3)
 GELU_SCALE = 0.7978845608028654
 GELU_CUBE = 0.044715
 G_SLOTS = 6
@@ -18,30 +19,29 @@
 SPILLED = 4
 
 ORDER = (
-    ("a", 8, 0), ("a", 9, 0), ("a", 1, 0), ("a", 0, 0), ("a", 2, 0), ("a", 4, 0), ("a", 3, 0), ("m", 0, 0), ("a", 5, 0), ("a", 11, 0), ("a", 7, 0),
-    ("a", 8, 1), ("a", 10, 0), ("a", 6, 0), ("a", 2, 1), ("a", 5, 1), ("a", 11, 1), ("a", 9, 1), ("a", 1, 1), ("a", 0, 1), ("a", 8, 2), ("a", 4, 1),
-    ("a", 2, 2), ("a", 3, 1), ("a", 5, 2), ("a", 7, 1), ("a", 11, 2), ("a", 10, 1), ("a", 6, 1), ("a", 1, 2), ("a", 8, 3), ("a", 0, 2), ("a", 2, 3),
-    ("a", 4, 2), ("a", 3, 2), ("a", 5, 3), ("a", 7, 2), ("a", 11, 3), ("a", 1, 3), ("a", 0, 3), ("a", 2, 4), ("a", 8, 4), ("a", 6, 2), ("a", 5, 4),
-    ("a", 4, 3), ("a", 3, 3), ("a", 11, 4), ("a", 0, 4), ("a", 2, 5), ("a", 7, 3), ("a", 0, 5), ("d", 0, 0), ("a", 9, 2), ("a", 1, 4), ("a", 8, 5),
-    ("a", 10, 2), ("a", 5, 5), ("a", 6, 3), ("a", 4, 4), ("a", 1, 5), ("f", 0, 0), ("a", 2, 6), ("a", 3, 4), ("a", 7, 4), ("a", 4, 5), ("a", 11, 5),
-    ("d", 1, 0), ("d", 4, 0), ("a", 5, 6), ("a", 8, 6), ("a", 9, 3), ("a", 2, 7), ("d", 2, 0), ("a", 3, 5), ("f", 1, 0), ("a", 8, 7), ("a", 6, 4),
-    ("a", 7, 5), ("d", 7, 0), ("a", 10, 3), ("a", 5, 7), ("f", 2, 0), ("a", 9, 4), ("a", 6, 5), ("d", 6, 0), ("d", 3, 0), ("a", 11, 6), ("d", 8, 0),
-    ("f", 3, 0), ("a", 9, 5), ("a", 10, 4), ("d", 9, 0), ("a", 11, 7), ("d", 11, 0), ("f", 4, 0), ("a", 10, 5), ("d", 10, 0), ("d", 5, 0),
-    ("f", 5, 0), ("l", 0, 0), ("g", 5, 0), ("g", 5, 1), ("g", 4, 0), ("g", 4, 1), ("g", 4, 2), ("g", 5, 2), ("r", 11, 0), ("g", 3, 0), ("r", 8, 0),
-    ("g", 3, 1), ("g", 3, 2), ("r", 11, 1), ("r", 10, 0), ("r", 9, 0), ("r", 8, 1), ("g", 2, 0), ("r", 7, 0), ("r", 6, 0), ("g", 2, 1), ("r", 11, 2),
-    ("g", 1, 0), ("r", 8, 2), ("g", 1, 1), ("r", 10, 1), ("r", 5, 0), ("g", 0, 0), ("r", 6, 1), ("r", 7, 1), ("r", 8, 3), ("g", 1, 2), ("r", 3, 0),
-    ("r", 11, 3), ("g", 0, 1), ("r", 5, 1), ("r", 6, 2), ("r", 8, 4), ("r", 7, 2), ("r", 2, 0), ("g", 0, 2), ("g", 2, 2), ("r", 1, 0), ("r", 10, 2),
-    ("h", 0, 0), ("r", 5, 2), ("r", 3, 1), ("r", 8, 5), ("r", 6, 3), ("r", 2, 1), ("r", 4, 0), ("r", 0, 0), ("r", 7, 3), ("r", 5, 3), ("r", 1, 1),
-    ("r", 10, 3), ("r", 11, 4), ("u", 8, 0), ("r", 2, 2), ("r", 9, 1), ("r", 3, 2), ("u", 6, 0), ("r", 5, 4), ("r", 4, 1), ("r", 0, 1), ("u", 7, 0),
-    ("r", 1, 2), ("r", 2, 3), ("r", 11, 5), ("r", 9, 2), ("b", 8, 0), ("u", 10, 0), ("r", 3, 3), ("r", 5, 5), ("r", 4, 2), ("r", 0, 2), ("r", 2, 4),
-    ("b", 6, 0), ("u", 11, 0), ("b", 7, 0), ("r", 1, 3), ("b", 8, 1), ("u", 5, 0), ("b", 10, 0), ("r", 4, 3), ("u", 3, 0), ("r", 0, 3), ("r", 2, 5),
-    ("b", 6, 1), ("b", 5, 0), ("b", 7, 1), ("b", 8, 2), ("u", 1, 0), ("b", 11, 0), ("u", 2, 0), ("r", 9, 3), ("b", 10, 1), ("u", 4, 0), ("b", 8, 3),
-    ("b", 6, 2), ("b", 3, 0), ("u", 0, 0), ("b", 5, 1), ("b", 2, 0), ("b", 11, 1), ("b", 1, 0), ("b", 7, 2), ("b", 8, 4), ("b", 6, 3), ("b", 10, 2),
-    ("b", 4, 0), ("u", 9, 0), ("n", 0, 0), ("b", 2, 1), ("b", 5, 2), ("b", 6, 4), ("b", 3, 1), ("b", 0, 0), ("b", 7, 3), ("b", 1, 1), ("b", 11, 2),
-    ("b", 8, 5), ("b", 7, 4), ("b", 10, 3), ("b", 8, 6), ("b", 10, 4), ("b", 2, 2), ("b", 4, 1), ("b", 9, 0), ("b", 0, 1), ("b", 5, 3), ("b", 3, 2),
-    ("b", 11, 3), ("b", 1, 2), ("b", 2, 3), ("b", 5, 4), ("b", 0, 2), ("b", 4, 2), ("b", 11, 4), ("b", 3, 3), ("b", 2, 4), ("b", 9, 1), ("b", 1, 3),
-    ("b", 5, 5), ("b", 3, 4), ("b", 0, 3), ("b", 11, 5), ("b", 4, 3), ("b", 1, 4), ("b", 5, 6), ("b", 2, 5), ("b", 0, 4), ("s", 0, 0), ("b", 2, 6),
-    ("b", 11, 6), ("b", 4, 4), ("b", 9, 2), ("s", 1, 0), ("s", 2, 0), ("b", 9, 3), ("s", 3, 0), ("b", 9, 4), ("s", 4, 0), ("s", 5, 0),
+    ("a", 11, 0), ("a", 10, 0), ("a", 3, 0), ("a", 2, 0), ("a", 1, 0), ("a", 4, 0), ("a", 8, 0), ("a", 0, 0), ("a", 5, 0), ("m", 0, 0), ("a", 6, 0),
+    ("a", 7, 0), ("a", 11, 1), ("a", 2, 1), ("a", 5, 1), ("a", 8, 1), ("a", 9, 0), ("a", 10, 1), ("a", 3, 1), ("a", 1, 1), ("a", 11, 2), ("a", 2, 2),
+    ("a", 4, 1), ("a", 5, 2), ("a", 8, 2), ("a", 0, 1), ("a", 6, 1), ("a", 7, 1), ("a", 3, 2), ("a", 9, 1), ("a", 11, 3), ("a", 1, 2), ("a", 2, 3),
+    ("a", 4, 2), ("a", 0, 2), ("a", 5, 3), ("a", 6, 2), ("a", 8, 3), ("a", 3, 3), ("a", 7, 2), ("a", 11, 4), ("a", 2, 4), ("a", 0, 3), ("a", 1, 3),
+    ("a", 5, 4), ("a", 4, 3), ("a", 8, 4), ("a", 6, 3), ("a", 11, 5), ("a", 3, 4), ("a", 7, 3), ("a", 2, 5), ("a", 9, 2), ("a", 0, 4), ("a", 3, 5),
+    ("a", 1, 4), ("a", 10, 2), ("a", 5, 5), ("a", 6, 4), ("a", 4, 4), ("a", 0, 5), ("a", 1, 5), ("f", 0, 0), ("a", 2, 6), ("a", 11, 6), ("a", 6, 5),
+    ("a", 4, 5), ("a", 8, 5), ("m", 0, 1), ("a", 5, 6), ("a", 7, 4), ("a", 9, 3), ("a", 2, 7), ("f", 1, 0), ("a", 11, 7), ("a", 10, 3), ("a", 5, 7),
+    ("f", 2, 0), ("a", 7, 5), ("a", 9, 4), ("a", 8, 6), ("f", 3, 0), ("a", 10, 4), ("a", 9, 5), ("a", 8, 7), ("f", 4, 0), ("a", 10, 5), ("d", 0, 0),
+    ("f", 5, 0), ("l", 0, 0), ("g", 5, 0), ("g", 5, 1), ("g", 4, 0), ("g", 4, 1), ("g", 4, 2), ("r", 11, 0), ("g", 3, 0), ("g", 3, 1), ("r", 8, 0),
+    ("g", 3, 2), ("r", 11, 1), ("r", 9, 0), ("g", 5, 2), ("r", 7, 0), ("g", 2, 0), ("r", 6, 0), ("g", 2, 1), ("r", 8, 1), ("r", 10, 0), ("r", 11, 2),
+    ("g", 1, 0), ("r", 9, 1), ("g", 1, 1), ("r", 5, 0), ("r", 7, 1), ("g", 1, 2), ("r", 8, 2), ("r", 6, 1), ("g", 0, 0), ("r", 3, 0), ("r", 10, 1),
+    ("r", 11, 3), ("g", 0, 1), ("h", 0, 0), ("r", 2, 0), ("r", 9, 2), ("r", 5, 1), ("g", 0, 2), ("r", 7, 2), ("g", 2, 2), ("r", 8, 3), ("r", 11, 4),
+    ("r", 1, 0), ("r", 10, 2), ("r", 6, 2), ("r", 0, 0), ("r", 2, 1), ("r", 3, 1), ("r", 4, 0), ("r", 9, 3), ("r", 5, 2), ("r", 7, 3), ("r", 11, 5),
+    ("r", 10, 3), ("r", 8, 4), ("r", 2, 2), ("r", 1, 1), ("r", 0, 1), ("r", 5, 3), ("r", 6, 3), ("r", 3, 2), ("u", 9, 0), ("r", 4, 1), ("u", 11, 0),
+    ("r", 2, 3), ("u", 7, 0), ("r", 0, 2), ("u", 10, 0), ("r", 1, 2), ("r", 8, 5), ("r", 5, 4), ("r", 2, 4), ("b", 11, 0), ("r", 3, 3), ("u", 6, 0),
+    ("b", 9, 0), ("r", 4, 2), ("r", 1, 3), ("b", 7, 0), ("r", 0, 3), ("u", 8, 0), ("r", 2, 5), ("r", 5, 5), ("b", 11, 1), ("b", 10, 0), ("u", 3, 0),
+    ("b", 9, 1), ("r", 4, 3), ("b", 6, 0), ("u", 2, 0), ("b", 7, 1), ("u", 5, 0), ("u", 1, 0), ("b", 11, 2), ("b", 8, 0), ("u", 0, 0), ("b", 10, 1),
+    ("b", 9, 2), ("b", 2, 0), ("u", 4, 0), ("n", 0, 0), ("b", 5, 0), ("b", 11, 3), ("b", 6, 1), ("b", 3, 0), ("b", 8, 1), ("b", 7, 2), ("b", 9, 3),
+    ("b", 1, 0), ("b", 0, 0), ("b", 2, 1), ("b", 9, 4), ("b", 11, 4), ("b", 4, 0), ("b", 5, 1), ("b", 10, 2), ("b", 3, 1), ("b", 8, 2), ("b", 7, 3),
+    ("b", 2, 2), ("b", 1, 1), ("b", 11, 5), ("b", 7, 4), ("b", 0, 1), ("b", 10, 3), ("b", 5, 2), ("b", 4, 1), ("b", 11, 6), ("b", 10, 4), ("b", 8, 3),
+    ("b", 3, 2), ("b", 2, 3), ("b", 6, 2), ("b", 5, 3), ("b", 1, 2), ("b", 0, 2), ("b", 8, 4), ("b", 3, 3), ("b", 4, 2), ("b", 2, 4), ("b", 6, 3),
+    ("b", 3, 4), ("b", 1, 3), ("b", 5, 4), ("b", 0, 3), ("b", 6, 4), ("b", 8, 5), ("b", 1, 4), ("b", 2, 5), ("b", 4, 3), ("b", 0, 4), ("s", 0, 0),
+    ("b", 8, 6), ("b", 5, 5), ("b", 2, 6), ("s", 1, 0), ("b", 5, 6), ("b", 4, 4), ("s", 2, 0), ("s", 3, 0), ("s", 4, 0), ("s", 5, 0),
 )
 
 
@@ -102,11 +102,32 @@
     return step - 1 if way == 1 else place.far(d) + step - 1
 
 
+class Sems:
+    def __init__(self, place, colours, send, recv, per_unit):
+        self.send, self.recv = send, recv
+        self.kind = [int(ORDERS[c][2] == "z") for c in colours]
+        self.base, n = [], 0
+        for c in colours:
+            self.base.append(n)
+            n += self.count(place.grid, c)
+        self.swaps = per_unit
+
+    @staticmethod
+    def count(grid, c):
+        return 3 + grid["zyx".index(ORDERS[c][2])] - 1
+
+    def r(self, u, k):
+        return self.recv.at[self.base[u] + k]
+
+    def s(self, u, stage):
+        if stage == 3:
+            return self.send.at[6 + (u if self.swaps else 0)]
+        return self.send.at[2 * stage + self.kind[u]]
+
+
 class Gather:
-    def __init__(self, place, buf, u, order, send_sem, recv_sem):
-        self.p, self.buf, self.u, self.order = place, buf, u, order
-        self.send_sem, self.recv_sem = send_sem, recv_sem
-        self.last_sem = 2 + max(place.size[order[2]] - 1, 1)
+    def __init__(self, place, buf, u, order, sems):
+        self.p, self.buf, self.u, self.order, self.sems = place, buf, u, order, sems
 
     def block(self, stage, v):
         return block_of(self.buf, (self.u,), self.p, self.order[:stage], self.order[stage], v, (self.p.c,))
@@ -118,17 +139,17 @@
         p, d = self.p, self.order[stage]
         own = self.block(stage, p.pos[d])
         for k in range(1, p.size[d]):
-            start_copy(own, own, self.send_sem.at[self.u, stage], self.recv_sem.at[self.u, stage], p.dev(d, p.wrap(p.pos[d] + k, d)))
+            start_copy(own, own, self.sems.s(self.u, stage), self.sems.r(self.u, stage), p.dev(d, p.wrap(p.pos[d] + k, d)))
 
     def direct_wait(self, stage):
         if self.p.size[self.order[stage]] > 1:
-            wait_bytes(self.many(stage), self.recv_sem.at[self.u, stage])
+            wait_bytes(self.many(stage), self.sems.r(self.u, stage))
 
     def ring_send(self, way, step):
         p, d = self.p, self.order[2]
         s = p.sign * way
         ref = self.block(2, p.wrap(p.pos[d] - (step - 1) * s, d))
-        start_copy(ref, ref, self.send_sem.at[self.u, 2], self.recv_sem.at[self.u, 2 + ring_sem(p, d, way, step)], p.dev(d, p.wrap(p.pos[d] + s, d)))
+        start_copy(ref, ref, self.sems.s(self.u, 2), self.sems.r(self.u, 3 + ring_sem(p, d, way, step)), p.dev(d, p.wrap(p.pos[d] + s, d)))
 
     def ways(self):
         d = self.order[2]
@@ -145,7 +166,7 @@
         for way, n in self.ways():
             if step <= n:
                 ref = self.block(2, p.wrap(p.pos[d] - step * p.sign * way, d))
-                wait_bytes(ref, self.recv_sem.at[self.u, 2 + ring_sem(p, d, way, step)])
+                wait_bytes(ref, self.sems.r(self.u, 3 + ring_sem(p, d, way, step)))
                 if step < n:
                     self.ring_send(way, step + 1)
                 self.swap_start(step * way)
@@ -156,10 +177,10 @@
     def swap_start(self, k):
         d = self.order[2]
         ref = self.block(2, self.p.wrap(self.p.pos[d] - k * self.p.sign, d))
-        start_copy(ref, ref, self.send_sem.at[self.u, 3], self.recv_sem.at[self.u, self.last_sem], self.p.sib)
+        start_copy(ref, ref, self.sems.s(self.u, 3), self.sems.r(self.u, 2), self.p.sib)
 
     def swap_wait(self):
-        wait_bytes(self.swap_ref(1 - self.p.c), self.recv_sem.at[self.u, self.last_sem])
+        wait_bytes(self.swap_ref(1 - self.p.c), self.sems.r(self.u, 2))
 
     def events(self):
         part = functools.partial
@@ -169,11 +190,16 @@
         out += [[part(self.ring_step, step)] for step in range(1, self.p.far(self.order[2]) + 1)]
         return out + [[self.swap_wait]]
 
-    def drain(self):
-        for stage in range(3):
-            if self.p.size[self.order[stage]] > 1:
-                wait_bytes(self.many(stage), self.send_sem.at[self.u, stage])
-        wait_bytes(self.swap_ref(self.p.c), self.send_sem.at[self.u, 3])
+
+def drain_gather(place, buf, sems):
+    nz, ny, nx, nc = place.grid
+    heavy = sum(sems.kind)
+    light = len(sems.kind) - heavy
+    sent = (buf.at[0:light, 0:nz - 1, 0, 0, 0], buf.at[0:heavy, 0, 0, 0:nx - 1, 0],
+            buf.at[0:light, :, 0:nx - 1, 0, 0], buf.at[0:heavy, 0, 0:nx - 1, :, 0],
+            buf.at[0:light, :, 0:ny - 1, :, 0], buf.at[0:heavy, 0:nz - 1, :, :, 0], buf.at[:, :, :, :, 0])
+    for k, ref in enumerate(sent):
+        wait_bytes(ref, sems.send.at[k])
 
 
 def add_into(dst, *srcs):
@@ -184,24 +210,22 @@
 
 
 class Reduce:
-    def __init__(self, place, g, gslot, part, rings, rows, tiles, u, order, send_sem, recv_sem):
-        self.p, self.g, self.gslot, self.part, self.u, self.order = place, g, gslot, part, u, order
-        self.ring = lambda k: rings[0].at[rings[1], k]
+    def __init__(self, place, g, gslot, part, ring, rows, tiles, u, order, sems):
+        self.p, self.g, self.gslot, self.part, self.u, self.order, self.sems = place, g, gslot, part, u, order, sems
+        self.ring = ring
         n0 = place.size[order[0]]
-        self.rows = lambda k: rows.at[u, k, pl.ds(0, n0)]
-        self.tiles = lambda k: tiles.at[u, k]
-        self.send_sem, self.recv_sem = send_sem, recv_sem
-        self.first_sem = 3
+        self.rows = lambda k: rows.at[k, pl.ds(0, n0)]
+        self.tiles = lambda k: tiles.at[k]
 
     def block(self, stage, v):
         return block_of(self.part, (self.u,), self.p, self.order[:stage], self.order[stage], v)
 
     def swap_start(self):
         start_copy(self.g.at[self.gslot, :, :, :, 1 - self.p.c], self.part.at[self.u],
-                   self.send_sem.at[self.u, 3], self.recv_sem.at[self.u, 0], self.p.sib)
+                   self.sems.s(self.u, 3), self.sems.r(self.u, 2), self.p.sib)
 
     def swap_wait(self):
-        wait_bytes(self.part.at[self.u], self.recv_sem.at[self.u, 0])
+        wait_bytes(self.part.at[self.u], self.sems.r(self.u, 2))
         p = self.p
 
         def add(k, _):
@@ -209,7 +233,7 @@
             return 0
 
         lax.fori_loop(0, p.size["z"], add, 0)
-        wait_bytes(self.part.at[self.u], self.send_sem.at[self.u, 3])
+        wait_bytes(self.part.at[self.u], self.sems.s(self.u, 3))
 
     def ways(self):
         d = self.order[2]
@@ -220,8 +244,7 @@
         s = p.sign * way
         k = ring_sem(p, d, way, step)
         src = self.block(2, p.wrap(p.pos[d] + n * s, d)) if step == 1 else self.ring(k - 1)
-        start_copy(src, self.ring(k), self.send_sem.at[self.u, 2], self.recv_sem.at[self.u, self.first_sem + k],
-                   p.dev(d, p.wrap(p.pos[d] + s, d)))
+        start_copy(src, self.ring(k), self.sems.s(self.u, 2), self.sems.r(self.u, 3 + k), p.dev(d, p.wrap(p.pos[d] + s, d)))
 
     def ring_start(self):
         for way, n in self.ways():
@@ -233,7 +256,7 @@
         for way, n in self.ways():
             if step <= n:
                 k = ring_sem(p, d, way, step)
-                wait_bytes(self.ring(k), self.recv_sem.at[self.u, self.first_sem + k])
+                wait_bytes(self.ring(k), self.sems.r(self.u, 3 + k))
                 if step < n:
                     add_into(self.ring(k), self.block(2, p.wrap(p.pos[d] + (n - step) * p.sign * way, d)))
                     self.ring_send(way, step + 1, n)
@@ -245,21 +268,21 @@
         land = self.rows if stage == 1 else self.tiles
         for k in range(1, p.size[d]):
             v = p.wrap(p.pos[d] + k, d)
-            start_copy(self.block(stage, v), land(k - 1), self.send_sem.at[self.u, stage], self.recv_sem.at[self.u, 1 + stage], p.dev(d, v))
-
-    def direct_wait(self, stage, sems, first):
+            start_copy(self.block(stage, v), land(k - 1), self.sems.s(self.u, stage), self.sems.r(self.u, stage), p.dev(d, v))
+
+    def direct_wait(self, stage):
         n = self.p.size[self.order[stage]]
         if n > 1:
-            wait_bytes((self.rows if stage == 1 else self.tiles)(pl.ds(0, n - 1)), sems.at[self.u, first])
+            wait_bytes((self.rows if stage == 1 else self.tiles)(pl.ds(0, n - 1)), self.sems.r(self.u, stage))
 
     def row_sum(self):
-        self.direct_wait(1, self.recv_sem, 2)
+        self.direct_wait(1)
         n = self.p.size[self.order[1]]
         if n > 1:
             add_into(self.block(1, self.p.pos[self.order[1]]), *[self.rows(k) for k in range(n - 1)])
 
     def tile_sum(self):
-        self.direct_wait(0, self.recv_sem, 1)
+        self.direct_wait(0)
         total = self.block(0, self.p.pos[self.order[0]])[...].astype(F32)
         for k in range(self.p.size[self.order[0]] - 1):
             total = total + self.tiles(k)[...].astype(F32)
@@ -272,12 +295,14 @@
         out[-1].append(part(self.direct_start, 1))
         return out + [[self.row_sum, part(self.direct_start, 0)]]
 
-    def drain(self):
-        n = self.p.size[self.order[2]] - 1
-        if n:
-            wait_bytes(self.block(2, pl.ds(0, n)), self.send_sem.at[self.u, 2])
-        self.direct_wait(1, self.send_sem, 1)
-        self.direct_wait(0, self.send_sem, 0)
+
+def drain_reduce(place, ring_ab, ring_c, rows, tiles, sems):
+    nz, ny, nx, nc = place.grid
+    heavy = sum(sems.kind)
+    light = len(sems.kind) - heavy
+    sent = (tiles.at[0:light, 0:nz - 1], tiles.at[0:heavy, 0:nx - 1], rows.at[0:light, :, 0:nz], rows.at[0:heavy, :, 0:nx], ring_ab, ring_c)
+    for k, ref in enumerate(sent):
+        wait_bytes(ref, sems.send.at[k])
 
 
 def enter(p):
@@ -376,16 +401,19 @@
     return lax.dot_general(a, b, (((da,), (db,)), ((), ())), preferred_element_type=F32)
 
 
+def gelu_parts(u):
+    w = GELU_SCALE + (GELU_SCALE * GELU_CUBE) * (u * u)
+    gate = 0.5 + 0.5 * jnp.tanh(u * w)
+    return u * gate, gate, w
+
+
+def gelu(u):
+    return gelu_parts(u)[0]
+
+
 def gelu_and_slope(u):
-    u2 = u * u
-    t = jnp.tanh(GELU_SCALE * (u + GELU_CUBE * (u * u2)))
-    half = 0.5 * (1.0 + t)
-    slope = half + (0.5 * u) * (1.0 - t * t) * (GELU_SCALE + (3.0 * GELU_CUBE * GELU_SCALE) * u2)
-    return u * half, slope
-
-
-def gelu(u):
-    return u * (0.5 * (1.0 + jnp.tanh(GELU_SCALE * (u + GELU_CUBE * (u * u * u)))))
+    z, gate, w = gelu_parts(u)
+    return z, gate + (z - z * gate) * (6.0 * w - 4.0 * GELU_SCALE)
 
 
 def step_kernel(grid, batch_scale, w1, w2, m1, m2, x0, y0, x1, y1, nw1, nw2, nm1, nm2, loss, hlast, spill,
@@ -417,7 +445,6 @@
     for c in stage:
         c.wait()
     wshuf.to_tiles_start(wrow1, wrow2)
-    mshuf.to_tiles_start(m1, m2)
 
     def own_tile(u):
         wbuf[u, p.z, p.y, p.x, p.c] = wt[u].astype(BF16)
@@ -457,14 +484,16 @@
         h[...] = d
         dlow[...] = d.astype(BF16)
 
-    gather_args = lambda u: (p, wbuf, u, ORDERS[u % 3], gsend, grecv)
+    gsems = Sems(p, COLOURS, gsend, grecv, False)
+    rsems = Sems(p, COLOURS, rsend, rrecv, True)
     slots = gradient_slots()
-    first = [Gather(*gather_args(u)) for u in range(units)]
-    again = [Gather(*gather_args(u)) for u in range(units)]
+    first = [Gather(p, wbuf, u, ORDERS[COLOURS[u]], gsems) for u in range(units)]
+    again = [Gather(p, wbuf, u, ORDERS[COLOURS[u]], gsems) for u in range(units)]
     red = []
     for u in range(units):
-        ring = (ring_c, u // 3) if u % 3 == 2 else (ring_ab, 2 * (u // 3) + u % 3)
-        red.append(Reduce(p, g, slots[u], part, ring, rows, tiles3, u, ORDERS[u % 3], rsend, rrecv))
+        n = sum(k == rsems.kind[u] for k in rsems.kind[:u])
+        ring = functools.partial(lambda buf, n, k: buf.at[n, k], ring_c if rsems.kind[u] else ring_ab, n)
+        red.append(Reduce(p, g, slots[u], part, ring, rows.at[u], tiles3.at[u], u, ORDERS[COLOURS[u]], rsems))
 
     def grad_two(l):
         slot = red[2 * l + 1].gslot
@@ -508,6 +537,9 @@
         mt[u] = mom
         again[u].direct_start(0)
 
+    def moments_start():
+        mshuf.to_tiles_start(m1, m2)
+
     def moments_ready():
         mshuf.to_tiles_finish(mt)
         mshuf.drain_sends()
@@ -548,14 +580,15 @@
         work["u", u, 0] = [functools.partial(update, u)]
         for k, ev in enumerate(again[u].events()[1:]):
             work["b", u, k] = ev
-        work["d", u, 0] = [first[u].drain]
     for l in range(layers):
         work["g", l, 0] = [functools.partial(grad_two, l)]
         work["g", l, 1] = [functools.partial(back_hidden, l)]
         work["g", l, 2] = [functools.partial(grad_one, l)]
     work["s", layers - 1, 0] = [forward_last]
+    work["d", 0, 0] = [functools.partial(drain_gather, p, wbuf, gsems)]
     work["l", 0, 0] = [loss_slope]
-    work["m", 0, 0] = [moments_ready]
+    work["m", 0, 0] = [moments_start]
+    work["m", 0, 1] = [moments_ready]
     work["h", 0, 0] = [second_start]
     work["n", 0, 0] = [new_rows]
 
@@ -592,9 +625,8 @@
     out = [load(h, hlast, 0), load(lossbuf, loss, 1)]
     for c in out:
         c.start()
-    for u in range(units):
-        again[u].drain()
-        red[u].drain()
+    drain_gather(p, wbuf, gsems)
+    drain_reduce(p, ring_ab, ring_c, rows, tiles3, rsems)
     wshuf.to_rows_finish()
     mshuf.to_rows_finish()
     for c in out:
@@ -619,7 +651,8 @@
     sds = jax.ShapeDtypeStruct
     tile = (16, LANES)
     dma = pltpu.SemaphoreType.DMA
-    thirds = (units + 2) // 3
+    heavy = sum(ORDERS[c][2] == "z" for c in COLOURS)
+    recvs = sum(Sems.count(grid, c) for c in COLOURS)
     outs = (sds((layers, 2, d_ff), F32), sds((layers, 4, d_model), F32), sds((layers, 2, d_ff), F32), sds((layers, 4, d_model), F32),
             sds((1, tok), F32), sds((tok, d_model), F32), sds((SPILLED, tok, d_ff), F32))
     shuffled = [pltpu.VMEM((group, layers, 2, LANES), F32), pltpu.VMEM((group // 2, layers, 4, LANES), F32)]
@@ -632,15 +665,15 @@
         pltpu.VMEM((tok, d_model), BF16),
         pltpu.VMEM((G_SLOTS, *grid, *tile), BF16),
         pltpu.VMEM((units, nz, ny, nx, *tile), BF16),
-        pltpu.VMEM((2 * thirds, nx - 1, nz, ny, *tile), BF16),
-        pltpu.VMEM((thirds, nz - 1, ny, nx, *tile), BF16),
+        pltpu.VMEM((units - heavy, nx - 1, nz, ny, *tile), BF16),
+        pltpu.VMEM((heavy, nz - 1, ny, nx, *tile), BF16),
         pltpu.VMEM((units, max(ny, nx) - 1, max(nz, nx), *tile), BF16),
         pltpu.VMEM((units, max(nz, nx) - 1, *tile), BF16),
         *shuffled, *shuffled,
         pltpu.VMEM((layers, 2, d_ff), F32), pltpu.VMEM((layers, 4, d_model), F32),
         pltpu.VMEM((units, *tile), F32), pltpu.VMEM((units, *tile), F32),
         pltpu.VMEM((1, tok), F32),
-        dma((units, 4)), dma((units, 10)), dma((units, 4)), dma((units, 10)), dma((8,)), dma((4 + SPILLED,)),
+        dma((7,)), dma((recvs,)), dma((6 + units,)), dma((recvs,)), dma((8,)), dma((4 + SPILLED,)),
     ]
     return pl.pallas_call(
         functools.partial(step_kernel, grid, 1.0 / (n_dev * tok * d_model)),

time: 155 us -> 149 us (0.961)
  Pallas kernels: 155 us -> 148 us
    pallas_call x1, Pallas kernels: 152 us -> 146 us  [device_step(): step(w_one, w_two, mom_one, mom_two, x_zero, y_zero, x_one, y_one)[:6]]
where the time goes in v5:
time: 149 us
  Pallas kernels  148 us (99%)
    pallas_call x1, Pallas kernels, device_step(): step(w_one, w_two, mom_one, mom_two, x_zero, y_zero, x_one, y_one)[:6]  146 us

profile of v5, /device:TPU:1, one launch (start us, length us, event | category | flops | bytes accessed | tf_op | source)
XLA Modules:
  0.0 149.0 jit_solution(15336870839598074126)
XLA Ops:
  0.6 145.5 %train_step.1 = (f32[6,2,1024]{2,1,0:T(2,128)}, f32[6,4,512]{2,1,0:T(4,128)}, f32[6,2,1024]{2,1,0:T(2,128)}, f32[6,4,512]{2,1,0:T(4,128)}, f32[1,768]{1,0:T(1,12...) custom-call(f32[6,2,1024]{2,1,0:T(2,128)} %w1.1, f32[6,4,512]{2,1,0:T(4,128)} %w2.1, f32[6,2,1024]{2,1,0:T(2,128)} %m1.1, ...), custom_call_target="tpu_custom_call" | custom-call | tf_op jit(solution)/shard_map/train_step/pallas_call | solution.py:702
  146.2 2.8 %hand_over.1 = (f32[6,2,1024]{2,1,0:T(2,128)}, f32[6,4,512]{2,1,0:T(4,128)}, f32[6,2,1024]{2,1,0:T(2,128)}, f32[6,4,512]{2,1,0:T(4,128)}, f32[768]{0:T(1024)}, /*index=5*/f32[768,512]{1,0:T(8,128)}) custom-call(f32[6,2,1024]{2,1,0:T(2,128)} %get-tuple-element.12.refs_0_, f32[6,4,512]{2,1,0:T(4,128)} %get-tuple-element.13.refs_1_, ...), custom_call_target="tpu_custom_call" | custom-call | tf_op jit(solution)/shard_map/hand_over/pallas_call | solution.py:706

commit v6 on v5

--- a/solution.py
+++ b/solution.py
@@ -14,34 +14,41 @@
 COLOURS = (0, 1, 2, 0, 1, 3, 0, 1, 2, 0, 1, 3)
 GELU_SCALE = 0.7978845608028654
 GELU_CUBE = 0.044715
-G_SLOTS = 6
+G_SLOTS = 5
 LANES = 128
 SPILLED = 4
+LATER = (2, 3)
 
 ORDER = (
-    ("a", 11, 0), ("a", 10, 0), ("a", 3, 0), ("a", 2, 0), ("a", 1, 0), ("a", 4, 0), ("a", 8, 0), ("a", 0, 0), ("a", 5, 0), ("m", 0, 0), ("a", 6, 0),
-    ("a", 7, 0), ("a", 11, 1), ("a", 2, 1), ("a", 5, 1), ("a", 8, 1), ("a", 9, 0), ("a", 10, 1), ("a", 3, 1), ("a", 1, 1), ("a", 11, 2), ("a", 2, 2),
-    ("a", 4, 1), ("a", 5, 2), ("a", 8, 2), ("a", 0, 1), ("a", 6, 1), ("a", 7, 1), ("a", 3, 2), ("a", 9, 1), ("a", 11, 3), ("a", 1, 2), ("a", 2, 3),
-    ("a", 4, 2), ("a", 0, 2), ("a", 5, 3), ("a", 6, 2), ("a", 8, 3), ("a", 3, 3), ("a", 7, 2), ("a", 11, 4), ("a", 2, 4), ("a", 0, 3), ("a", 1, 3),
-    ("a", 5, 4), ("a", 4, 3), ("a", 8, 4), ("a", 6, 3), ("a", 11, 5), ("a", 3, 4), ("a", 7, 3), ("a", 2, 5), ("a", 9, 2), ("a", 0, 4), ("a", 3, 5),
-    ("a", 1, 4), ("a", 10, 2), ("a", 5, 5), ("a", 6, 4), ("a", 4, 4), ("a", 0, 5), ("a", 1, 5), ("f", 0, 0), ("a", 2, 6), ("a", 11, 6), ("a", 6, 5),
-    ("a", 4, 5), ("a", 8, 5), ("m", 0, 1), ("a", 5, 6), ("a", 7, 4), ("a", 9, 3), ("a", 2, 7), ("f", 1, 0), ("a", 11, 7), ("a", 10, 3), ("a", 5, 7),
-    ("f", 2, 0), ("a", 7, 5), ("a", 9, 4), ("a", 8, 6), ("f", 3, 0), ("a", 10, 4), ("a", 9, 5), ("a", 8, 7), ("f", 4, 0), ("a", 10, 5), ("d", 0, 0),
-    ("f", 5, 0), ("l", 0, 0), ("g", 5, 0), ("g", 5, 1), ("g", 4, 0), ("g", 4, 1), ("g", 4, 2), ("r", 11, 0), ("g", 3, 0), ("g", 3, 1), ("r", 8, 0),
-    ("g", 3, 2), ("r", 11, 1), ("r", 9, 0), ("g", 5, 2), ("r", 7, 0), ("g", 2, 0), ("r", 6, 0), ("g", 2, 1), ("r", 8, 1), ("r", 10, 0), ("r", 11, 2),
-    ("g", 1, 0), ("r", 9, 1), ("g", 1, 1), ("r", 5, 0), ("r", 7, 1), ("g", 1, 2), ("r", 8, 2), ("r", 6, 1), ("g", 0, 0), ("r", 3, 0), ("r", 10, 1),
-    ("r", 11, 3), ("g", 0, 1), ("h", 0, 0), ("r", 2, 0), ("r", 9, 2), ("r", 5, 1), ("g", 0, 2), ("r", 7, 2), ("g", 2, 2), ("r", 8, 3), ("r", 11, 4),
-    ("r", 1, 0), ("r", 10, 2), ("r", 6, 2), ("r", 0, 0), ("r", 2, 1), ("r", 3, 1), ("r", 4, 0), ("r", 9, 3), ("r", 5, 2), ("r", 7, 3), ("r", 11, 5),
-    ("r", 10, 3), ("r", 8, 4), ("r", 2, 2), ("r", 1, 1), ("r", 0, 1), ("r", 5, 3), ("r", 6, 3), ("r", 3, 2), ("u", 9, 0), ("r", 4, 1), ("u", 11, 0),
-    ("r", 2, 3), ("u", 7, 0), ("r", 0, 2), ("u", 10, 0), ("r", 1, 2), ("r", 8, 5), ("r", 5, 4), ("r", 2, 4), ("b", 11, 0), ("r", 3, 3), ("u", 6, 0),
-    ("b", 9, 0), ("r", 4, 2), ("r", 1, 3), ("b", 7, 0), ("r", 0, 3), ("u", 8, 0), ("r", 2, 5), ("r", 5, 5), ("b", 11, 1), ("b", 10, 0), ("u", 3, 0),
-    ("b", 9, 1), ("r", 4, 3), ("b", 6, 0), ("u", 2, 0), ("b", 7, 1), ("u", 5, 0), ("u", 1, 0), ("b", 11, 2), ("b", 8, 0), ("u", 0, 0), ("b", 10, 1),
-    ("b", 9, 2), ("b", 2, 0), ("u", 4, 0), ("n", 0, 0), ("b", 5, 0), ("b", 11, 3), ("b", 6, 1), ("b", 3, 0), ("b", 8, 1), ("b", 7, 2), ("b", 9, 3),
-    ("b", 1, 0), ("b", 0, 0), ("b", 2, 1), ("b", 9, 4), ("b", 11, 4), ("b", 4, 0), ("b", 5, 1), ("b", 10, 2), ("b", 3, 1), ("b", 8, 2), ("b", 7, 3),
-    ("b", 2, 2), ("b", 1, 1), ("b", 11, 5), ("b", 7, 4), ("b", 0, 1), ("b", 10, 3), ("b", 5, 2), ("b", 4, 1), ("b", 11, 6), ("b", 10, 4), ("b", 8, 3),
-    ("b", 3, 2), ("b", 2, 3), ("b", 6, 2), ("b", 5, 3), ("b", 1, 2), ("b", 0, 2), ("b", 8, 4), ("b", 3, 3), ("b", 4, 2), ("b", 2, 4), ("b", 6, 3),
-    ("b", 3, 4), ("b", 1, 3), ("b", 5, 4), ("b", 0, 3), ("b", 6, 4), ("b", 8, 5), ("b", 1, 4), ("b", 2, 5), ("b", 4, 3), ("b", 0, 4), ("s", 0, 0),
-    ("b", 8, 6), ("b", 5, 5), ("b", 2, 6), ("s", 1, 0), ("b", 5, 6), ("b", 4, 4), ("s", 2, 0), ("s", 3, 0), ("s", 4, 0), ("s", 5, 0),
+    ("a", 3, 0), ("a", 1, 0), ("a", 0, 0), ("a", 6, 0), ("a", 10, 0), ("a", 4, 0), ("a", 8, 0), ("a", 2, 0), ("m", 0, 0), ("a", 11, 0), ("a", 7, 0),
+    ("a", 5, 0), ("a", 8, 1), ("a", 9, 0), ("a", 11, 1), ("a", 2, 1), ("a", 5, 1), ("a", 3, 1), ("a", 1, 1), ("a", 0, 1), ("a", 6, 1), ("a", 8, 2),
+    ("a", 11, 2), ("a", 10, 1), ("a", 2, 2), ("a", 4, 1), ("a", 5, 2), ("a", 7, 1), ("a", 9, 1), ("a", 8, 3), ("a", 1, 2), ("a", 3, 2), ("a", 8, 4),
+    ("a", 0, 2), ("a", 6, 2), ("a", 10, 2), ("a", 11, 3), ("a", 2, 3), ("a", 2, 4), ("a", 4, 2), ("a", 5, 3), ("a", 1, 3), ("a", 5, 4), ("a", 7, 2),
+    ("a", 8, 5), ("a", 1, 4), ("a", 8, 6), ("a", 11, 4), ("a", 2, 5), ("a", 10, 3), ("a", 0, 3), ("a", 2, 6), ("a", 10, 4), ("a", 5, 5), ("a", 0, 4),
+    ("a", 5, 6), ("a", 3, 3), ("a", 3, 4), ("a", 4, 3), ("a", 8, 7), ("a", 6, 3), ("a", 8, 8), ("a", 11, 5), ("a", 4, 4), ("a", 11, 6), ("a", 6, 4),
+    ("a", 2, 7), ("a", 9, 2), ("a", 1, 5), ("a", 2, 8), ("a", 0, 5), ("a", 5, 7), ("a", 7, 3), ("a", 5, 8), ("a", 1, 6), ("a", 3, 5), ("a", 8, 9),
+    ("a", 0, 6), ("f", 0, 0), ("a", 3, 6), ("a", 2, 9), ("a", 8, 10), ("a", 7, 4), ("a", 6, 5), ("m", 0, 1), ("a", 11, 7), ("a", 10, 5), ("a", 9, 3),
+    ("a", 11, 8), ("a", 5, 9), ("a", 4, 5), ("a", 2, 10), ("f", 1, 0), ("a", 9, 4), ("a", 4, 6), ("a", 7, 5), ("a", 5, 10), ("f", 2, 0), ("a", 9, 5),
+    ("a", 6, 6), ("a", 7, 6), ("f", 3, 0), ("a", 9, 6), ("a", 11, 9), ("a", 10, 6), ("f", 4, 0), ("a", 11, 10), ("d", 0, 0), ("f", 5, 0), ("l", 0, 0),
+    ("g", 5, 0), ("g", 5, 1), ("g", 5, 2), ("g", 4, 0), ("g", 4, 1), ("r", 11, 0), ("g", 3, 1), ("g", 3, 2), ("r", 9, 0), ("r", 10, 0), ("r", 11, 1),
+    ("g", 4, 2), ("r", 11, 2), ("g", 2, 1), ("g", 2, 0), ("r", 8, 0), ("r", 11, 3), ("r", 6, 0), ("r", 11, 4), ("r", 9, 1), ("g", 2, 2), ("r", 10, 1),
+    ("r", 10, 2), ("r", 9, 2), ("g", 1, 0), ("r", 5, 0), ("g", 1, 1), ("r", 8, 1), ("r", 8, 2), ("r", 4, 0), ("r", 6, 1), ("g", 1, 2), ("r", 5, 1),
+    ("r", 6, 2), ("r", 11, 5), ("r", 11, 6), ("g", 0, 0), ("r", 5, 2), ("r", 3, 0), ("r", 9, 3), ("g", 0, 1), ("r", 8, 3), ("r", 8, 4), ("r", 2, 0),
+    ("r", 4, 1), ("h", 0, 0), ("g", 3, 0), ("r", 5, 3), ("r", 11, 7), ("r", 6, 3), ("r", 4, 2), ("r", 10, 3), ("g", 0, 2), ("r", 5, 4), ("r", 3, 1),
+    ("r", 1, 0), ("r", 8, 5), ("r", 7, 0), ("r", 8, 6), ("r", 9, 4), ("r", 3, 2), ("r", 4, 3), ("r", 2, 1), ("r", 0, 0), ("r", 2, 2), ("r", 5, 5),
+    ("r", 11, 8), ("r", 10, 4), ("r", 5, 6), ("r", 8, 7), ("r", 6, 4), ("r", 1, 1), ("r", 2, 3), ("r", 1, 2), ("r", 4, 4), ("r", 2, 4), ("r", 0, 1),
+    ("r", 3, 3), ("r", 5, 7), ("u", 9, 0), ("r", 7, 1), ("r", 0, 2), ("r", 7, 2), ("r", 2, 5), ("u", 11, 0), ("r", 8, 8), ("u", 10, 0), ("r", 1, 3),
+    ("r", 0, 3), ("r", 2, 6), ("u", 6, 0), ("r", 2, 7), ("u", 4, 0), ("b", 11, 0), ("r", 3, 4), ("r", 5, 8), ("b", 9, 0), ("r", 7, 3), ("u", 8, 0),
+    ("r", 1, 4), ("b", 10, 0), ("r", 2, 8), ("r", 0, 4), ("b", 6, 0), ("b", 11, 1), ("u", 5, 0), ("b", 4, 0), ("b", 9, 1), ("r", 7, 4), ("u", 3, 0),
+    ("u", 2, 0), ("b", 11, 2), ("b", 10, 1), ("u", 1, 0), ("b", 11, 3), ("u", 0, 0), ("b", 5, 0), ("b", 8, 0), ("b", 4, 1), ("b", 6, 1), ("b", 11, 4),
+    ("b", 2, 0), ("u", 7, 0), ("n", 0, 0), ("b", 11, 5), ("b", 3, 0), ("b", 9, 2), ("b", 9, 3), ("b", 8, 1), ("b", 11, 6), ("b", 1, 0), ("b", 5, 1),
+    ("b", 0, 0), ("b", 4, 2), ("b", 11, 7), ("b", 6, 2), ("b", 6, 3), ("b", 4, 3), ("b", 8, 2), ("b", 7, 0), ("b", 2, 1), ("b", 9, 4), ("b", 11, 8),
+    ("b", 10, 2), ("b", 10, 3), ("b", 5, 2), ("b", 3, 1), ("b", 9, 5), ("b", 11, 9), ("b", 5, 3), ("b", 1, 1), ("b", 6, 4), ("b", 0, 1), ("b", 4, 4),
+    ("b", 2, 2), ("b", 2, 3), ("b", 6, 5), ("b", 10, 4), ("b", 5, 4), ("b", 4, 5), ("b", 7, 1), ("b", 5, 5), ("b", 3, 2), ("b", 8, 3), ("b", 10, 5),
+    ("b", 1, 2), ("b", 2, 4), ("b", 3, 3), ("b", 2, 5), ("b", 1, 3), ("b", 5, 6), ("b", 0, 2), ("b", 5, 7), ("b", 8, 4), ("b", 7, 2), ("b", 8, 5),
+    ("b", 0, 3), ("b", 2, 6), ("b", 7, 3), ("b", 2, 7), ("b", 3, 4), ("b", 5, 8), ("b", 1, 4), ("b", 8, 6), ("b", 0, 4), ("b", 3, 5), ("b", 5, 9),
+    ("b", 8, 7), ("b", 7, 4), ("b", 1, 5), ("b", 2, 8), ("b", 0, 5), ("s", 0, 0), ("b", 2, 9), ("b", 8, 8), ("b", 7, 5), ("s", 1, 0), ("s", 2, 0),
+    ("s", 3, 0), ("b", 8, 9), ("s", 4, 0), ("s", 5, 0),
 )
 
 
@@ -64,7 +71,6 @@
         self.x = lax.rem(me // nc, nx)
         self.y = lax.rem(me // (nc * nx), ny)
         self.z = me // (nc * nx * ny)
-        self.sign = 1 - 2 * self.c
         self.size = {"z": nz, "y": ny, "x": nx}
         self.pos = {"z": self.z, "y": self.y, "x": self.x}
         self.stride = {"z": ny * nx * nc, "y": nx * nc, "x": nc}
@@ -98,8 +104,24 @@
     return buf.at[(*lead, *idx, *tail)]
 
 
+def half_of(buf, lead, place, d, v, h, tail=()):
+    cut = "y" if d == "z" else "z"
+    n = place.size[cut] // 2
+    idx = [v if k == d else pl.ds(h * n, n) if k == cut else slice(None) for k in ("z", "y", "x")]
+    return buf.at[(*lead, *idx, *tail)]
+
+
 def ring_sem(place, d, way, step):
     return step - 1 if way == 1 else place.far(d) + step - 1
+
+
+def ring_steps(place, d):
+    out = []
+    for step in range(1, place.far(d) + 1):
+        out.append((1, step))
+        if step <= place.near(d):
+            out.append((-1, step))
+    return out
 
 
 class Sems:
@@ -147,36 +169,36 @@
 
     def ring_send(self, way, step):
         p, d = self.p, self.order[2]
-        s = p.sign * way
-        ref = self.block(2, p.wrap(p.pos[d] - (step - 1) * s, d))
-        start_copy(ref, ref, self.sems.s(self.u, 2), self.sems.r(self.u, 3 + ring_sem(p, d, way, step)), p.dev(d, p.wrap(p.pos[d] + s, d)))
-
-    def ways(self):
+        for h in range(2):
+            s = way * (1 - 2 * h)
+            ref = half_of(self.buf, (self.u,), p, d, p.wrap(p.pos[d] - (step - 1) * s, d), h, (p.c,))
+            start_copy(ref, ref, self.sems.s(self.u, 2), self.sems.r(self.u, 3 + ring_sem(p, d, way, step)), p.dev(d, p.wrap(p.pos[d] + s, d)))
+
+    def ring_start(self):
         d = self.order[2]
-        return ((1, self.p.far(d)), (-1, self.p.near(d)))
-
-    def ring_start(self):
-        for way, n in self.ways():
+        for way, n in ((1, self.p.far(d)), (-1, self.p.near(d))):
             if n:
                 self.ring_send(way, 1)
         self.swap_start(0)
 
-    def ring_step(self, step):
+    def ring_step(self, way, step):
         p, d = self.p, self.order[2]
-        for way, n in self.ways():
-            if step <= n:
-                ref = self.block(2, p.wrap(p.pos[d] - step * p.sign * way, d))
-                wait_bytes(ref, self.sems.r(self.u, 3 + ring_sem(p, d, way, step)))
-                if step < n:
-                    self.ring_send(way, step + 1)
-                self.swap_start(step * way)
+        n = p.far(d) if way == 1 else p.near(d)
+        wait_bytes(self.block(2, 0), self.sems.r(self.u, 3 + ring_sem(p, d, way, step)))
+        if step < n:
+            self.ring_send(way, step + 1)
+        if way == -1:
+            self.swap_start(step)
+            self.swap_start(-step)
+        elif step > p.near(d):
+            self.swap_start(step)
 
     def swap_ref(self, c):
         return self.buf.at[self.u, :, :, :, c]
 
     def swap_start(self, k):
         d = self.order[2]
-        ref = self.block(2, self.p.wrap(self.p.pos[d] - k * self.p.sign, d))
+        ref = self.block(2, self.p.wrap(self.p.pos[d] - k, d))
         start_copy(ref, ref, self.sems.s(self.u, 3), self.sems.r(self.u, 2), self.p.sib)
 
     def swap_wait(self):
@@ -187,7 +209,7 @@
         out = [[part(self.direct_start, 0)],
                [part(self.direct_wait, 0), part(self.direct_start, 1)],
                [part(self.direct_wait, 1), self.ring_start]]
-        out += [[part(self.ring_step, step)] for step in range(1, self.p.far(self.order[2]) + 1)]
+        out += [[part(self.ring_step, way, step)] for way, step in ring_steps(self.p, self.order[2])]
         return out + [[self.swap_wait]]
 
 
@@ -235,33 +257,43 @@
         lax.fori_loop(0, p.size["z"], add, 0)
         wait_bytes(self.part.at[self.u], self.sems.s(self.u, 3))
 
-    def ways(self):
+    def count(self, way):
         d = self.order[2]
-        return ((1, self.p.far(d)), (-1, self.p.near(d)))
-
-    def ring_send(self, way, step, n):
+        return self.p.far(d) if way == 1 else self.p.near(d)
+
+    def half(self, k, h):
+        ref = self.ring(k)
+        n = ref.shape[0] // 2
+        return ref.at[pl.ds(h * n, n)]
+
+    def own_half(self, way, ahead, h):
         p, d = self.p, self.order[2]
-        s = p.sign * way
+        return half_of(self.part, (self.u,), p, d, p.wrap(p.pos[d] + ahead * way * (1 - 2 * h), d), h)
+
+    def ring_send(self, way, step):
+        p, d = self.p, self.order[2]
         k = ring_sem(p, d, way, step)
-        src = self.block(2, p.wrap(p.pos[d] + n * s, d)) if step == 1 else self.ring(k - 1)
-        start_copy(src, self.ring(k), self.sems.s(self.u, 2), self.sems.r(self.u, 3 + k), p.dev(d, p.wrap(p.pos[d] + s, d)))
+        for h in range(2):
+            src = self.own_half(way, self.count(way), h) if step == 1 else self.half(k - 1, h)
+            start_copy(src, self.half(k, h), self.sems.s(self.u, 2), self.sems.r(self.u, 3 + k),
+                       p.dev(d, p.wrap(p.pos[d] + way * (1 - 2 * h), d)))
 
     def ring_start(self):
-        for way, n in self.ways():
-            if n:
-                self.ring_send(way, 1, n)
-
-    def ring_step(self, step):
+        for way in (1, -1):
+            if self.count(way):
+                self.ring_send(way, 1)
+
+    def ring_step(self, way, step):
         p, d = self.p, self.order[2]
-        for way, n in self.ways():
-            if step <= n:
-                k = ring_sem(p, d, way, step)
-                wait_bytes(self.ring(k), self.sems.r(self.u, 3 + k))
-                if step < n:
-                    add_into(self.ring(k), self.block(2, p.wrap(p.pos[d] + (n - step) * p.sign * way, d)))
-                    self.ring_send(way, step + 1, n)
-        if step == p.far(d):
-            add_into(self.block(2, p.pos[d]), *[self.ring(ring_sem(p, d, way, n)) for way, n in self.ways() if n])
+        n = self.count(way)
+        k = ring_sem(p, d, way, step)
+        wait_bytes(self.ring(k), self.sems.r(self.u, 3 + k))
+        if step < n:
+            for h in range(2):
+                add_into(self.half(k, h), self.own_half(way, n - step, h))
+            self.ring_send(way, step + 1)
+        if way == 1 and step == n:
+            add_into(self.block(2, p.pos[d]), *[self.ring(ring_sem(p, d, w, self.count(w))) for w in (1, -1) if self.count(w)])
 
     def direct_start(self, stage):
         p, d = self.p, self.order[stage]
@@ -291,7 +323,7 @@
     def events(self):
         part = functools.partial
         out = [[self.swap_wait, self.ring_start]]
-        out += [[part(self.ring_step, step)] for step in range(1, self.p.far(self.order[2]) + 1)]
+        out += [[part(self.ring_step, way, step)] for way, step in ring_steps(self.p, self.order[2])]
         out[-1].append(part(self.direct_start, 1))
         return out + [[self.row_sum, part(self.direct_start, 0)]]
 
@@ -430,7 +462,7 @@
     def load(src, dst, k):
         return pltpu.make_async_copy(src, dst, local.at[k])
 
-    loads = {"x0": load(x0, act.at[0], 0), "y0": load(y0, dlow, 1),
+    loads = {"x0": load(x0, act.at[0], 0), "y0": load(y0, dlow.at[0], 1),
              "x1": load(x1, act.at[layers - 1], 2), "y1": load(y1, act.at[layers - 2], 3)}
     stage = [load(w1, wrow1, 2), load(w2, wrow2, 3)]
     wshuf = Shuffle(p, wone, wtwo, shuf, 0)
@@ -480,9 +512,9 @@
 
     def loss_slope():
         loads["y0"].wait()
-        d = (h[...] - dlow[...].astype(F32)) * batch_scale
+        d = (h[...] - dlow[0].astype(F32)) * batch_scale
         h[...] = d
-        dlow[...] = d.astype(BF16)
+        dlow[0] = d.astype(BF16)
 
     gsems = Sems(p, COLOURS, gsend, grecv, False)
     rsems = Sems(p, COLOURS, rsend, rrecv, True)
@@ -495,31 +527,40 @@
         ring = functools.partial(lambda buf, n, k: buf.at[n, k], ring_c if rsems.kind[u] else ring_ab, n)
         red.append(Reduce(p, g, slots[u], part, ring, rows.at[u], tiles3.at[u], u, ORDERS[COLOURS[u]], rsems))
 
+    def slope_of(l):
+        return dlow.at[1 + LATER.index(l) if l in LATER else 0]
+
+    def hidden_slope_of(l):
+        return hid.at[l + len(LATER) if l in LATER else l]
+
     def grad_two(l):
         slot = red[2 * l + 1].gslot
         half = nx * nc // 2
-        v = contract(hid[l], dlow[...], 0, 0).astype(BF16).reshape(nz, ny, 2, 16, d_model)
+        v = contract(hid[l], slope_of(l)[...], 0, 0).astype(BF16).reshape(nz, ny, 2, 16, d_model)
         for b in range(half):
             for r in range(2):
                 g[slot, :, :, (r * half + b) // nc, b % nc] = v[:, :, r, :, LANES * b:LANES * b + LANES]
+        if l in LATER:
+            red[2 * l + 1].swap_start()
 
     def back_hidden(l):
         if l + 2 < layers:
             unspill_copy(l).wait()
-        q = contract(dlow[...], w_two_of(wbuf, l), 1, 1)
+        q = contract(slope_of(l)[...], w_two_of(wbuf, l), 1, 1)
         v = (slope[l % 2] * q).astype(BF16)
-        hid[l] = v
+        hidden_slope_of(l)[...] = v
         if l:
             d = h[...] + contract(v, w_one_of(wbuf, l), 1, 1)
             h[...] = d
-            dlow[...] = d.astype(BF16)
-        red[2 * l + 1].swap_start()
+            slope_of(l - 1)[...] = d.astype(BF16)
+        if l not in LATER:
+            red[2 * l + 1].swap_start()
         if l >= 2:
             unspill_copy(l - 2).start()
 
     def grad_one(l):
         slot = red[2 * l].gslot
-        v = contract(act[l], hid[l], 0, 0).astype(BF16).reshape(nz, ny, 16, d_ff)
+        v = contract(act[l], hidden_slope_of(l)[...], 0, 0).astype(BF16).reshape(nz, ny, 16, d_ff)
         for m in range(nx * nc):
             g[slot, :, :, m // nc, m % nc] = v[:, :, :, LANES * m:LANES * m + LANES]
         red[2 * l].swap_start()
@@ -662,7 +703,7 @@
         pltpu.VMEM((layers, tok, d_model), BF16),
         pltpu.VMEM((layers, tok, d_ff), BF16),
         pltpu.VMEM((tok, d_model), F32),
-        pltpu.VMEM((tok, d_model), BF16),
+        pltpu.VMEM((len(LATER) + 1, tok, d_model), BF16),
         pltpu.VMEM((G_SLOTS, *grid, *tile), BF16),
         pltpu.VMEM((units, nz, ny, nx, *tile), BF16),
         pltpu.VMEM((units - heavy, nx - 1, nz, ny, *tile), BF16),

time: 149 us -> 149 us (level)
  no operation moved by 1% of the time
where the time goes in v6:
time: 149 us
  Pallas kernels  148 us (99%)
    pallas_call x1, Pallas kernels, device_step(): step(w_one, w_two, mom_one, mom_two, x_zero, y_zero, x_one, y_one)[:6]  145 us

profile of v6, /device:TPU:1, one launch (start us, length us, event | category | flops | bytes accessed | tf_op | source)
XLA Modules:
  0.0 148.6 jit_solution(14677107754977968782)
XLA Ops:
  0.6 145.1 %train_step.1 = (f32[6,2,1024]{2,1,0:T(2,128)}, f32[6,4,512]{2,1,0:T(4,128)}, f32[6,2,1024]{2,1,0:T(2,128)}, f32[6,4,512]{2,1,0:T(4,128)}, f32[1,768]{1,0:T(1,12...) custom-call(f32[6,2,1024]{2,1,0:T(2,128)} %w1.1, f32[6,4,512]{2,1,0:T(4,128)} %w2.1, f32[6,2,1024]{2,1,0:T(2,128)} %m1.1, ...), custom_call_target="tpu_custom_call" | custom-call | tf_op jit(solution)/shard_map/train_step/pallas_call | solution.py:743
  145.8 2.8 %hand_over.1 = (f32[6,2,1024]{2,1,0:T(2,128)}, f32[6,4,512]{2,1,0:T(4,128)}, f32[6,2,1024]{2,1,0:T(2,128)}, f32[6,4,512]{2,1,0:T(4,128)}, f32[768]{0:T(1024)}, /*index=5*/f32[768,512]{1,0:T(8,128)}) custom-call(f32[6,2,1024]{2,1,0:T(2,128)} %get-tuple-element.12.refs_0_, f32[6,4,512]{2,1,0:T(4,128)} %get-tuple-element.13.refs_1_, ...), custom_call_target="tpu_custom_call" | custom-call | tf_op jit(solution)/shard_map/hand_over/pallas_call | solution.py:747

commit v7 on v6

--- a/solution.py
+++ b/solution.py
@@ -11,7 +11,7 @@
 F32, BF16 = jnp.float32, jnp.bfloat16
 GRID = (8, 4, 4, 2)
 ORDERS = (("z", "x", "y"), ("z", "y", "x"), ("x", "y", "z"), ("y", "x", "z"))
-COLOURS = (0, 1, 2, 0, 1, 3, 0, 1, 2, 0, 1, 3)
+COLOURS = (0, 1, 0, 1, 2, 3, 0, 1, 2, 0, 1, 3)
 GELU_SCALE = 0.7978845608028654
 GELU_CUBE = 0.044715
 G_SLOTS = 5
@@ -20,35 +20,35 @@
 LATER = (2, 3)
 
 ORDER = (
-    ("a", 3, 0), ("a", 1, 0), ("a", 0, 0), ("a", 6, 0), ("a", 10, 0), ("a", 4, 0), ("a", 8, 0), ("a", 2, 0), ("m", 0, 0), ("a", 11, 0), ("a", 7, 0),
-    ("a", 5, 0), ("a", 8, 1), ("a", 9, 0), ("a", 11, 1), ("a", 2, 1), ("a", 5, 1), ("a", 3, 1), ("a", 1, 1), ("a", 0, 1), ("a", 6, 1), ("a", 8, 2),
-    ("a", 11, 2), ("a", 10, 1), ("a", 2, 2), ("a", 4, 1), ("a", 5, 2), ("a", 7, 1), ("a", 9, 1), ("a", 8, 3), ("a", 1, 2), ("a", 3, 2), ("a", 8, 4),
-    ("a", 0, 2), ("a", 6, 2), ("a", 10, 2), ("a", 11, 3), ("a", 2, 3), ("a", 2, 4), ("a", 4, 2), ("a", 5, 3), ("a", 1, 3), ("a", 5, 4), ("a", 7, 2),
-    ("a", 8, 5), ("a", 1, 4), ("a", 8, 6), ("a", 11, 4), ("a", 2, 5), ("a", 10, 3), ("a", 0, 3), ("a", 2, 6), ("a", 10, 4), ("a", 5, 5), ("a", 0, 4),
-    ("a", 5, 6), ("a", 3, 3), ("a", 3, 4), ("a", 4, 3), ("a", 8, 7), ("a", 6, 3), ("a", 8, 8), ("a", 11, 5), ("a", 4, 4), ("a", 11, 6), ("a", 6, 4),
-    ("a", 2, 7), ("a", 9, 2), ("a", 1, 5), ("a", 2, 8), ("a", 0, 5), ("a", 5, 7), ("a", 7, 3), ("a", 5, 8), ("a", 1, 6), ("a", 3, 5), ("a", 8, 9),
-    ("a", 0, 6), ("f", 0, 0), ("a", 3, 6), ("a", 2, 9), ("a", 8, 10), ("a", 7, 4), ("a", 6, 5), ("m", 0, 1), ("a", 11, 7), ("a", 10, 5), ("a", 9, 3),
-    ("a", 11, 8), ("a", 5, 9), ("a", 4, 5), ("a", 2, 10), ("f", 1, 0), ("a", 9, 4), ("a", 4, 6), ("a", 7, 5), ("a", 5, 10), ("f", 2, 0), ("a", 9, 5),
-    ("a", 6, 6), ("a", 7, 6), ("f", 3, 0), ("a", 9, 6), ("a", 11, 9), ("a", 10, 6), ("f", 4, 0), ("a", 11, 10), ("d", 0, 0), ("f", 5, 0), ("l", 0, 0),
-    ("g", 5, 0), ("g", 5, 1), ("g", 5, 2), ("g", 4, 0), ("g", 4, 1), ("r", 11, 0), ("g", 3, 1), ("g", 3, 2), ("r", 9, 0), ("r", 10, 0), ("r", 11, 1),
-    ("g", 4, 2), ("r", 11, 2), ("g", 2, 1), ("g", 2, 0), ("r", 8, 0), ("r", 11, 3), ("r", 6, 0), ("r", 11, 4), ("r", 9, 1), ("g", 2, 2), ("r", 10, 1),
-    ("r", 10, 2), ("r", 9, 2), ("g", 1, 0), ("r", 5, 0), ("g", 1, 1), ("r", 8, 1), ("r", 8, 2), ("r", 4, 0), ("r", 6, 1), ("g", 1, 2), ("r", 5, 1),
-    ("r", 6, 2), ("r", 11, 5), ("r", 11, 6), ("g", 0, 0), ("r", 5, 2), ("r", 3, 0), ("r", 9, 3), ("g", 0, 1), ("r", 8, 3), ("r", 8, 4), ("r", 2, 0),
-    ("r", 4, 1), ("h", 0, 0), ("g", 3, 0), ("r", 5, 3), ("r", 11, 7), ("r", 6, 3), ("r", 4, 2), ("r", 10, 3), ("g", 0, 2), ("r", 5, 4), ("r", 3, 1),
-    ("r", 1, 0), ("r", 8, 5), ("r", 7, 0), ("r", 8, 6), ("r", 9, 4), ("r", 3, 2), ("r", 4, 3), ("r", 2, 1), ("r", 0, 0), ("r", 2, 2), ("r", 5, 5),
-    ("r", 11, 8), ("r", 10, 4), ("r", 5, 6), ("r", 8, 7), ("r", 6, 4), ("r", 1, 1), ("r", 2, 3), ("r", 1, 2), ("r", 4, 4), ("r", 2, 4), ("r", 0, 1),
-    ("r", 3, 3), ("r", 5, 7), ("u", 9, 0), ("r", 7, 1), ("r", 0, 2), ("r", 7, 2), ("r", 2, 5), ("u", 11, 0), ("r", 8, 8), ("u", 10, 0), ("r", 1, 3),
-    ("r", 0, 3), ("r", 2, 6), ("u", 6, 0), ("r", 2, 7), ("u", 4, 0), ("b", 11, 0), ("r", 3, 4), ("r", 5, 8), ("b", 9, 0), ("r", 7, 3), ("u", 8, 0),
-    ("r", 1, 4), ("b", 10, 0), ("r", 2, 8), ("r", 0, 4), ("b", 6, 0), ("b", 11, 1), ("u", 5, 0), ("b", 4, 0), ("b", 9, 1), ("r", 7, 4), ("u", 3, 0),
-    ("u", 2, 0), ("b", 11, 2), ("b", 10, 1), ("u", 1, 0), ("b", 11, 3), ("u", 0, 0), ("b", 5, 0), ("b", 8, 0), ("b", 4, 1), ("b", 6, 1), ("b", 11, 4),
-    ("b", 2, 0), ("u", 7, 0), ("n", 0, 0), ("b", 11, 5), ("b", 3, 0), ("b", 9, 2), ("b", 9, 3), ("b", 8, 1), ("b", 11, 6), ("b", 1, 0), ("b", 5, 1),
-    ("b", 0, 0), ("b", 4, 2), ("b", 11, 7), ("b", 6, 2), ("b", 6, 3), ("b", 4, 3), ("b", 8, 2), ("b", 7, 0), ("b", 2, 1), ("b", 9, 4), ("b", 11, 8),
-    ("b", 10, 2), ("b", 10, 3), ("b", 5, 2), ("b", 3, 1), ("b", 9, 5), ("b", 11, 9), ("b", 5, 3), ("b", 1, 1), ("b", 6, 4), ("b", 0, 1), ("b", 4, 4),
-    ("b", 2, 2), ("b", 2, 3), ("b", 6, 5), ("b", 10, 4), ("b", 5, 4), ("b", 4, 5), ("b", 7, 1), ("b", 5, 5), ("b", 3, 2), ("b", 8, 3), ("b", 10, 5),
-    ("b", 1, 2), ("b", 2, 4), ("b", 3, 3), ("b", 2, 5), ("b", 1, 3), ("b", 5, 6), ("b", 0, 2), ("b", 5, 7), ("b", 8, 4), ("b", 7, 2), ("b", 8, 5),
-    ("b", 0, 3), ("b", 2, 6), ("b", 7, 3), ("b", 2, 7), ("b", 3, 4), ("b", 5, 8), ("b", 1, 4), ("b", 8, 6), ("b", 0, 4), ("b", 3, 5), ("b", 5, 9),
-    ("b", 8, 7), ("b", 7, 4), ("b", 1, 5), ("b", 2, 8), ("b", 0, 5), ("s", 0, 0), ("b", 2, 9), ("b", 8, 8), ("b", 7, 5), ("s", 1, 0), ("s", 2, 0),
-    ("s", 3, 0), ("b", 8, 9), ("s", 4, 0), ("s", 5, 0),
+    ("a", 0, 0), ("a", 4, 0), ("a", 5, 0), ("a", 1, 0), ("a", 3, 0), ("m", 0, 0), ("a", 2, 0), ("a", 11, 0), ("a", 8, 0), ("a", 9, 0), ("a", 7, 0),
+    ("a", 6, 0), ("a", 4, 1), ("a", 10, 0), ("a", 5, 1), ("a", 8, 1), ("a", 11, 1), ("a", 0, 1), ("a", 1, 1), ("a", 3, 1), ("a", 2, 1), ("a", 4, 2),
+    ("a", 5, 2), ("a", 9, 1), ("a", 8, 2), ("a", 11, 2), ("a", 7, 1), ("a", 6, 1), ("a", 10, 1), ("a", 0, 2), ("a", 4, 3), ("a", 1, 2), ("a", 4, 4),
+    ("a", 5, 3), ("a", 3, 2), ("a", 2, 2), ("a", 5, 4), ("a", 8, 3), ("a", 8, 4), ("a", 11, 3), ("a", 1, 3), ("a", 11, 4), ("a", 0, 3), ("a", 4, 5),
+    ("a", 0, 4), ("a", 1, 4), ("a", 4, 6), ("a", 5, 5), ("a", 7, 2), ("a", 6, 2), ("a", 3, 3), ("a", 2, 3), ("a", 5, 6), ("a", 8, 5), ("a", 3, 4),
+    ("a", 2, 4), ("a", 8, 6), ("a", 11, 5), ("a", 1, 5), ("a", 11, 6), ("a", 0, 5), ("a", 9, 2), ("a", 4, 7), ("a", 10, 2), ("a", 1, 6), ("a", 4, 8),
+    ("a", 0, 6), ("f", 0, 0), ("a", 5, 7), ("a", 5, 8), ("m", 0, 1), ("a", 3, 5), ("a", 7, 3), ("a", 2, 5), ("a", 6, 3), ("a", 8, 7), ("a", 8, 8),
+    ("a", 7, 4), ("a", 11, 7), ("a", 6, 4), ("a", 9, 3), ("a", 10, 3), ("a", 3, 6), ("a", 11, 8), ("a", 2, 6), ("f", 1, 0), ("a", 5, 9), ("a", 4, 9),
+    ("a", 8, 9), ("a", 10, 4), ("a", 6, 5), ("a", 11, 9), ("a", 7, 5), ("a", 5, 10), ("a", 9, 4), ("a", 4, 10), ("f", 2, 0), ("a", 6, 6), ("a", 7, 6),
+    ("a", 9, 5), ("a", 11, 10), ("f", 3, 0), ("a", 9, 6), ("a", 10, 5), ("a", 8, 10), ("f", 4, 0), ("a", 10, 6), ("f", 5, 0), ("d", 0, 0),
+    ("l", 0, 0), ("g", 5, 0), ("g", 5, 1), ("g", 4, 0), ("g", 5, 2), ("g", 4, 1), ("g", 3, 1), ("g", 3, 2), ("g", 3, 0), ("r", 9, 0), ("r", 11, 0),
+    ("r", 10, 0), ("g", 4, 2), ("g", 2, 1), ("r", 7, 0), ("r", 11, 1), ("r", 6, 0), ("g", 2, 2), ("r", 11, 2), ("r", 9, 1), ("r", 10, 1), ("g", 2, 0),
+    ("r", 9, 2), ("r", 10, 2), ("r", 8, 0), ("g", 1, 0), ("r", 4, 0), ("r", 11, 3), ("g", 1, 1), ("r", 7, 1), ("r", 7, 2), ("r", 6, 1), ("r", 6, 2),
+    ("r", 11, 4), ("r", 5, 0), ("g", 0, 0), ("r", 4, 1), ("r", 9, 3), ("r", 10, 3), ("g", 0, 1), ("r", 3, 0), ("h", 0, 0), ("r", 4, 2), ("g", 0, 2),
+    ("r", 7, 3), ("r", 11, 5), ("r", 11, 6), ("r", 5, 1), ("r", 8, 1), ("g", 1, 2), ("r", 5, 2), ("r", 6, 3), ("r", 4, 3), ("r", 9, 4), ("r", 0, 0),
+    ("r", 4, 4), ("r", 10, 4), ("r", 1, 0), ("r", 3, 1), ("r", 5, 3), ("r", 2, 0), ("r", 3, 2), ("r", 11, 7), ("r", 7, 4), ("r", 5, 4), ("r", 4, 5),
+    ("r", 0, 1), ("r", 1, 1), ("r", 6, 4), ("r", 4, 6), ("r", 0, 2), ("r", 8, 2), ("r", 1, 2), ("r", 5, 5), ("r", 2, 1), ("r", 8, 3), ("u", 9, 0),
+    ("r", 3, 3), ("r", 5, 6), ("r", 2, 2), ("u", 10, 0), ("r", 4, 7), ("r", 11, 8), ("r", 0, 3), ("r", 1, 3), ("u", 7, 0), ("r", 8, 4), ("r", 5, 7),
+    ("r", 2, 3), ("r", 8, 5), ("u", 6, 0), ("r", 3, 4), ("r", 4, 8), ("u", 11, 0), ("r", 8, 6), ("r", 0, 4), ("b", 9, 0), ("r", 8, 7), ("r", 5, 8),
+    ("r", 1, 4), ("b", 10, 0), ("r", 2, 4), ("b", 7, 0), ("u", 4, 0), ("b", 11, 0), ("b", 6, 0), ("u", 3, 0), ("r", 8, 8), ("u", 5, 0), ("b", 9, 1),
+    ("u", 0, 0), ("b", 10, 1), ("u", 1, 0), ("b", 11, 1), ("u", 2, 0), ("b", 4, 0), ("b", 5, 0), ("b", 6, 1), ("u", 8, 0), ("n", 0, 0), ("b", 7, 1),
+    ("b", 3, 0), ("b", 11, 2), ("b", 11, 3), ("b", 0, 0), ("b", 9, 2), ("b", 9, 3), ("b", 4, 1), ("b", 5, 1), ("b", 1, 0), ("b", 8, 0), ("b", 10, 2),
+    ("b", 10, 3), ("b", 2, 0), ("b", 11, 4), ("b", 6, 2), ("b", 6, 3), ("b", 4, 2), ("b", 4, 3), ("b", 3, 1), ("b", 5, 2), ("b", 9, 4), ("b", 0, 1),
+    ("b", 5, 3), ("b", 10, 4), ("b", 9, 5), ("b", 11, 5), ("b", 11, 6), ("b", 1, 1), ("b", 10, 5), ("b", 4, 4), ("b", 8, 1), ("b", 2, 1), ("b", 6, 4),
+    ("b", 5, 4), ("b", 3, 2), ("b", 5, 5), ("b", 11, 7), ("b", 6, 5), ("b", 3, 3), ("b", 0, 2), ("b", 11, 8), ("b", 0, 3), ("b", 1, 2), ("b", 4, 5),
+    ("b", 8, 2), ("b", 11, 9), ("b", 8, 3), ("b", 2, 2), ("b", 1, 3), ("b", 7, 2), ("b", 5, 6), ("b", 7, 3), ("b", 5, 7), ("b", 2, 3), ("b", 3, 4),
+    ("b", 4, 6), ("b", 4, 7), ("b", 0, 4), ("b", 1, 4), ("b", 8, 4), ("b", 3, 5), ("b", 8, 5), ("b", 2, 4), ("b", 0, 5), ("b", 7, 4), ("b", 1, 5),
+    ("s", 0, 0), ("b", 2, 5), ("b", 4, 8), ("b", 7, 5), ("b", 8, 6), ("b", 5, 8), ("s", 1, 0), ("b", 4, 9), ("b", 8, 7), ("b", 5, 9), ("s", 2, 0),
+    ("b", 8, 8), ("s", 3, 0), ("b", 8, 9), ("s", 4, 0), ("s", 5, 0),
 )
 
 
@@ -443,13 +443,13 @@
     return gelu_parts(u)[0]
 
 
-def gelu_and_slope(u):
+def gelu_slope(u):
     z, gate, w = gelu_parts(u)
-    return z, gate + (z - z * gate) * (6.0 * w - 4.0 * GELU_SCALE)
+    return gate + (z - z * gate) * (6.0 * w - 4.0 * GELU_SCALE)
 
 
 def step_kernel(grid, batch_scale, w1, w2, m1, m2, x0, y0, x1, y1, nw1, nw2, nm1, nm2, loss, hlast, spill,
-                wbuf, slope, act, hid, h, dlow, g, part, ring_ab, ring_c, rows, tiles3,
+                wbuf, before, act, hid, h, dlow, g, part, ring_ab, ring_c, rows, tiles3,
                 wone, wtwo, mone, mtwo, wrow1, wrow2, wt, mt, lossbuf,
                 gsend, grecv, rsend, rrecv, shuf, local):
     p = Place(grid)
@@ -488,10 +488,10 @@
     h[...] = act[0].astype(F32)
 
     def spill_copy(l):
-        return load(slope.at[lax.rem(l, 2)], spill.at[l], 4 + l)
+        return load(before.at[lax.rem(l, 2)], spill.at[l], 4 + l)
 
     def unspill_copy(l):
-        return load(spill.at[l], slope.at[l % 2], 4 + l)
+        return load(spill.at[l], before.at[l % 2], 4 + l)
 
     def forward_one(l):
         @pl.when(jnp.logical_and(l >= 2, l < SPILLED + 2))
@@ -500,9 +500,9 @@
 
         a = h[...].astype(BF16)
         act[l] = a
-        z, s = gelu_and_slope(jnp.dot(a, w_one_of(wbuf, l), preferred_element_type=F32))
-        z = z.astype(BF16)
-        slope[lax.rem(l, 2)] = s
+        u = jnp.dot(a, w_one_of(wbuf, l), preferred_element_type=F32)
+        before[lax.rem(l, 2)] = u
+        z = gelu(u).astype(BF16)
         hid[l] = z
         h[...] += jnp.dot(z, w_two_of(wbuf, l), preferred_element_type=F32)
 
@@ -547,7 +547,7 @@
         if l + 2 < layers:
             unspill_copy(l).wait()
         q = contract(slope_of(l)[...], w_two_of(wbuf, l), 1, 1)
-        v = (slope[l % 2] * q).astype(BF16)
+        v = (gelu_slope(before[l % 2]) * q).astype(BF16)
         hidden_slope_of(l)[...] = v
         if l:
             d = h[...] + contract(v, w_one_of(wbuf, l), 1, 1)

time: 149 us -> 146 us (0.980)
  Pallas kernels: 148 us -> 145 us
    pallas_call x1, Pallas kernels: 145 us -> 142 us  [device_step(): step(w_one, w_two, mom_one, mom_two, x_zero, y_zero, x_one, y_one)[:6]]
where the time goes in v7:
time: 146 us
  Pallas kernels  145 us (99%)
    pallas_call x1, Pallas kernels, device_step(): step(w_one, w_two, mom_one, mom_two, x_zero, y_zero, x_one, y_one)[:6]  142 us

profile of v7, /device:TPU:1, one launch (start us, length us, event | category | flops | bytes accessed | tf_op | source)
XLA Modules:
  0.0 145.7 jit_solution(2629153563396415879)
XLA Ops:
  0.6 142.3 %train_step.1 = (f32[6,2,1024]{2,1,0:T(2,128)}, f32[6,4,512]{2,1,0:T(4,128)}, f32[6,2,1024]{2,1,0:T(2,128)}, f32[6,4,512]{2,1,0:T(4,128)}, f32[1,768]{1,0:T(1,12...) custom-call(f32[6,2,1024]{2,1,0:T(2,128)} %w1.1, f32[6,4,512]{2,1,0:T(4,128)} %w2.1, f32[6,2,1024]{2,1,0:T(2,128)} %m1.1, ...), custom_call_target="tpu_custom_call" | custom-call | tf_op jit(solution)/shard_map/train_step/pallas_call | solution.py:743
  142.9 2.8 %hand_over.1 = (f32[6,2,1024]{2,1,0:T(2,128)}, f32[6,4,512]{2,1,0:T(4,128)}, f32[6,2,1024]{2,1,0:T(2,128)}, f32[6,4,512]{2,1,0:T(4,128)}, f32[768]{0:T(1024)}, /*index=5*/f32[768,512]{1,0:T(8,128)}) custom-call(f32[6,2,1024]{2,1,0:T(2,128)} %get-tuple-element.12.refs_0_, f32[6,4,512]{2,1,0:T(4,128)} %get-tuple-element.13.refs_1_, ...), custom_call_target="tpu_custom_call" | custom-call | tf_op jit(solution)/shard_map/hand_over/pallas_call | solution.py:747

commit v8 on v7

--- a/solution.py
+++ b/solution.py
@@ -47,7 +47,7 @@
     ("b", 5, 4), ("b", 3, 2), ("b", 5, 5), ("b", 11, 7), ("b", 6, 5), ("b", 3, 3), ("b", 0, 2), ("b", 11, 8), ("b", 0, 3), ("b", 1, 2), ("b", 4, 5),
     ("b", 8, 2), ("b", 11, 9), ("b", 8, 3), ("b", 2, 2), ("b", 1, 3), ("b", 7, 2), ("b", 5, 6), ("b", 7, 3), ("b", 5, 7), ("b", 2, 3), ("b", 3, 4),
     ("b", 4, 6), ("b", 4, 7), ("b", 0, 4), ("b", 1, 4), ("b", 8, 4), ("b", 3, 5), ("b", 8, 5), ("b", 2, 4), ("b", 0, 5), ("b", 7, 4), ("b", 1, 5),
-    ("s", 0, 0), ("b", 2, 5), ("b", 4, 8), ("b", 7, 5), ("b", 8, 6), ("b", 5, 8), ("s", 1, 0), ("b", 4, 9), ("b", 8, 7), ("b", 5, 9), ("s", 2, 0),
+    ("s", 0, 0), ("b", 2, 5), ("b", 4, 8), ("b", 7, 5), ("b", 8, 6), ("b", 5, 8), ("s", 1, 0), ("n", 0, 1), ("b", 4, 9), ("b", 8, 7), ("b", 5, 9), ("s", 2, 0),
     ("b", 8, 8), ("s", 3, 0), ("b", 8, 9), ("s", 4, 0), ("s", 5, 0),
 )
 
@@ -609,6 +609,8 @@
         for u in range(units):
             wshuf.put_rows(u, wt[u])
             mshuf.put_rows(u, mt[u])
+
+    def send_rows():
         wshuf.to_rows_start(nw1, nw2)
         mshuf.to_rows_start(nm1, nm2)
 
@@ -632,6 +634,7 @@
     work["m", 0, 1] = [moments_ready]
     work["h", 0, 0] = [second_start]
     work["n", 0, 0] = [new_rows]
+    work["n", 0, 1] = [send_rows]
 
     def do(names):
         for name in names:

time: 146 us -> 145 us (level)
  no operation moved by 1% of the time
where the time goes in v8:
time: 145 us
  Pallas kernels  144 us (99%)
    pallas_call x1, Pallas kernels, device_step(): step(w_one, w_two, mom_one, mom_two, x_zero, y_zero, x_one, y_one)[:6]  142 us

profile of v8, /device:TPU:1, one launch (start us, length us, event | category | flops | bytes accessed | tf_op | source)
XLA Modules:
  0.0 145.1 jit_solution(1469160811729201349)
XLA Ops:
  0.6 141.7 %train_step.1 = (f32[6,2,1024]{2,1,0:T(2,128)}, f32[6,4,512]{2,1,0:T(4,128)}, f32[6,2,1024]{2,1,0:T(2,128)}, f32[6,4,512]{2,1,0:T(4,128)}, f32[1,768]{1,0:T(1,12...) custom-call(f32[6,2,1024]{2,1,0:T(2,128)} %w1.1, f32[6,4,512]{2,1,0:T(4,128)} %w2.1, f32[6,2,1024]{2,1,0:T(2,128)} %m1.1, ...), custom_call_target="tpu_custom_call" | custom-call | tf_op jit(solution)/shard_map/train_step/pallas_call | solution.py:746
  142.3 2.8 %hand_over.1 = (f32[6,2,1024]{2,1,0:T(2,128)}, f32[6,4,512]{2,1,0:T(4,128)}, f32[6,2,1024]{2,1,0:T(2,128)}, f32[6,4,512]{2,1,0:T(4,128)}, f32[768]{0:T(1024)}, /*index=5*/f32[768,512]{1,0:T(8,128)}) custom-call(f32[6,2,1024]{2,1,0:T(2,128)} %get-tuple-element.12.refs_0_, f32[6,4,512]{2,1,0:T(4,128)} %get-tuple-element.13.refs_1_, ...), custom_call_target="tpu_custom_call" | custom-call | tf_op jit(solution)/shard_map/hand_over/pallas_call | solution.py:750

commit v9 on v8

--- a/solution.py
+++ b/solution.py
@@ -20,35 +20,35 @@
 LATER = (2, 3)
 
 ORDER = (
-    ("a", 0, 0), ("a", 4, 0), ("a", 5, 0), ("a", 1, 0), ("a", 3, 0), ("m", 0, 0), ("a", 2, 0), ("a", 11, 0), ("a", 8, 0), ("a", 9, 0), ("a", 7, 0),
-    ("a", 6, 0), ("a", 4, 1), ("a", 10, 0), ("a", 5, 1), ("a", 8, 1), ("a", 11, 1), ("a", 0, 1), ("a", 1, 1), ("a", 3, 1), ("a", 2, 1), ("a", 4, 2),
-    ("a", 5, 2), ("a", 9, 1), ("a", 8, 2), ("a", 11, 2), ("a", 7, 1), ("a", 6, 1), ("a", 10, 1), ("a", 0, 2), ("a", 4, 3), ("a", 1, 2), ("a", 4, 4),
-    ("a", 5, 3), ("a", 3, 2), ("a", 2, 2), ("a", 5, 4), ("a", 8, 3), ("a", 8, 4), ("a", 11, 3), ("a", 1, 3), ("a", 11, 4), ("a", 0, 3), ("a", 4, 5),
-    ("a", 0, 4), ("a", 1, 4), ("a", 4, 6), ("a", 5, 5), ("a", 7, 2), ("a", 6, 2), ("a", 3, 3), ("a", 2, 3), ("a", 5, 6), ("a", 8, 5), ("a", 3, 4),
-    ("a", 2, 4), ("a", 8, 6), ("a", 11, 5), ("a", 1, 5), ("a", 11, 6), ("a", 0, 5), ("a", 9, 2), ("a", 4, 7), ("a", 10, 2), ("a", 1, 6), ("a", 4, 8),
-    ("a", 0, 6), ("f", 0, 0), ("a", 5, 7), ("a", 5, 8), ("m", 0, 1), ("a", 3, 5), ("a", 7, 3), ("a", 2, 5), ("a", 6, 3), ("a", 8, 7), ("a", 8, 8),
-    ("a", 7, 4), ("a", 11, 7), ("a", 6, 4), ("a", 9, 3), ("a", 10, 3), ("a", 3, 6), ("a", 11, 8), ("a", 2, 6), ("f", 1, 0), ("a", 5, 9), ("a", 4, 9),
-    ("a", 8, 9), ("a", 10, 4), ("a", 6, 5), ("a", 11, 9), ("a", 7, 5), ("a", 5, 10), ("a", 9, 4), ("a", 4, 10), ("f", 2, 0), ("a", 6, 6), ("a", 7, 6),
-    ("a", 9, 5), ("a", 11, 10), ("f", 3, 0), ("a", 9, 6), ("a", 10, 5), ("a", 8, 10), ("f", 4, 0), ("a", 10, 6), ("f", 5, 0), ("d", 0, 0),
-    ("l", 0, 0), ("g", 5, 0), ("g", 5, 1), ("g", 4, 0), ("g", 5, 2), ("g", 4, 1), ("g", 3, 1), ("g", 3, 2), ("g", 3, 0), ("r", 9, 0), ("r", 11, 0),
-    ("r", 10, 0), ("g", 4, 2), ("g", 2, 1), ("r", 7, 0), ("r", 11, 1), ("r", 6, 0), ("g", 2, 2), ("r", 11, 2), ("r", 9, 1), ("r", 10, 1), ("g", 2, 0),
-    ("r", 9, 2), ("r", 10, 2), ("r", 8, 0), ("g", 1, 0), ("r", 4, 0), ("r", 11, 3), ("g", 1, 1), ("r", 7, 1), ("r", 7, 2), ("r", 6, 1), ("r", 6, 2),
-    ("r", 11, 4), ("r", 5, 0), ("g", 0, 0), ("r", 4, 1), ("r", 9, 3), ("r", 10, 3), ("g", 0, 1), ("r", 3, 0), ("h", 0, 0), ("r", 4, 2), ("g", 0, 2),
-    ("r", 7, 3), ("r", 11, 5), ("r", 11, 6), ("r", 5, 1), ("r", 8, 1), ("g", 1, 2), ("r", 5, 2), ("r", 6, 3), ("r", 4, 3), ("r", 9, 4), ("r", 0, 0),
-    ("r", 4, 4), ("r", 10, 4), ("r", 1, 0), ("r", 3, 1), ("r", 5, 3), ("r", 2, 0), ("r", 3, 2), ("r", 11, 7), ("r", 7, 4), ("r", 5, 4), ("r", 4, 5),
-    ("r", 0, 1), ("r", 1, 1), ("r", 6, 4), ("r", 4, 6), ("r", 0, 2), ("r", 8, 2), ("r", 1, 2), ("r", 5, 5), ("r", 2, 1), ("r", 8, 3), ("u", 9, 0),
-    ("r", 3, 3), ("r", 5, 6), ("r", 2, 2), ("u", 10, 0), ("r", 4, 7), ("r", 11, 8), ("r", 0, 3), ("r", 1, 3), ("u", 7, 0), ("r", 8, 4), ("r", 5, 7),
-    ("r", 2, 3), ("r", 8, 5), ("u", 6, 0), ("r", 3, 4), ("r", 4, 8), ("u", 11, 0), ("r", 8, 6), ("r", 0, 4), ("b", 9, 0), ("r", 8, 7), ("r", 5, 8),
-    ("r", 1, 4), ("b", 10, 0), ("r", 2, 4), ("b", 7, 0), ("u", 4, 0), ("b", 11, 0), ("b", 6, 0), ("u", 3, 0), ("r", 8, 8), ("u", 5, 0), ("b", 9, 1),
-    ("u", 0, 0), ("b", 10, 1), ("u", 1, 0), ("b", 11, 1), ("u", 2, 0), ("b", 4, 0), ("b", 5, 0), ("b", 6, 1), ("u", 8, 0), ("n", 0, 0), ("b", 7, 1),
-    ("b", 3, 0), ("b", 11, 2), ("b", 11, 3), ("b", 0, 0), ("b", 9, 2), ("b", 9, 3), ("b", 4, 1), ("b", 5, 1), ("b", 1, 0), ("b", 8, 0), ("b", 10, 2),
-    ("b", 10, 3), ("b", 2, 0), ("b", 11, 4), ("b", 6, 2), ("b", 6, 3), ("b", 4, 2), ("b", 4, 3), ("b", 3, 1), ("b", 5, 2), ("b", 9, 4), ("b", 0, 1),
-    ("b", 5, 3), ("b", 10, 4), ("b", 9, 5), ("b", 11, 5), ("b", 11, 6), ("b", 1, 1), ("b", 10, 5), ("b", 4, 4), ("b", 8, 1), ("b", 2, 1), ("b", 6, 4),
-    ("b", 5, 4), ("b", 3, 2), ("b", 5, 5), ("b", 11, 7), ("b", 6, 5), ("b", 3, 3), ("b", 0, 2), ("b", 11, 8), ("b", 0, 3), ("b", 1, 2), ("b", 4, 5),
-    ("b", 8, 2), ("b", 11, 9), ("b", 8, 3), ("b", 2, 2), ("b", 1, 3), ("b", 7, 2), ("b", 5, 6), ("b", 7, 3), ("b", 5, 7), ("b", 2, 3), ("b", 3, 4),
-    ("b", 4, 6), ("b", 4, 7), ("b", 0, 4), ("b", 1, 4), ("b", 8, 4), ("b", 3, 5), ("b", 8, 5), ("b", 2, 4), ("b", 0, 5), ("b", 7, 4), ("b", 1, 5),
-    ("s", 0, 0), ("b", 2, 5), ("b", 4, 8), ("b", 7, 5), ("b", 8, 6), ("b", 5, 8), ("s", 1, 0), ("n", 0, 1), ("b", 4, 9), ("b", 8, 7), ("b", 5, 9), ("s", 2, 0),
-    ("b", 8, 8), ("s", 3, 0), ("b", 8, 9), ("s", 4, 0), ("s", 5, 0),
+    ("a", 5, 0), ("a", 1, 0), ("a", 4, 0), ("a", 8, 0), ("a", 0, 0), ("m", 0, 0), ("a", 11, 0), ("a", 2, 0), ("a", 3, 0), ("a", 7, 0), ("a", 6, 0),
+    ("a", 5, 1), ("a", 4, 1), ("a", 11, 1), ("a", 8, 1), ("a", 10, 0), ("a", 9, 0), ("a", 1, 1), ("a", 0, 1), ("a", 2, 1), ("a", 3, 1), ("a", 5, 2),
+    ("a", 4, 2), ("a", 7, 1), ("a", 11, 2), ("a", 6, 1), ("a", 10, 1), ("a", 9, 1), ("a", 1, 2), ("a", 8, 2), ("a", 5, 3), ("a", 0, 2), ("a", 5, 4),
+    ("a", 4, 3), ("a", 3, 2), ("a", 2, 2), ("a", 4, 4), ("a", 11, 3), ("a", 11, 4), ("a", 1, 3), ("a", 0, 3), ("a", 5, 5), ("a", 0, 4), ("a", 8, 3),
+    ("a", 1, 4), ("a", 5, 6), ("a", 4, 5), ("a", 7, 2), ("a", 2, 3), ("a", 3, 3), ("a", 4, 6), ("a", 6, 2), ("a", 11, 5), ("a", 2, 4), ("a", 3, 4),
+    ("a", 11, 6), ("a", 5, 7), ("a", 0, 5), ("a", 1, 5), ("a", 8, 4), ("a", 5, 8), ("a", 8, 5), ("a", 2, 5), ("a", 7, 3), ("a", 0, 6), ("a", 4, 7),
+    ("a", 9, 2), ("a", 1, 6), ("f", 0, 0), ("a", 10, 2), ("m", 0, 1), ("a", 7, 4), ("a", 2, 6), ("a", 11, 7), ("a", 11, 8), ("a", 6, 3), ("a", 3, 5),
+    ("a", 5, 9), ("a", 4, 8), ("a", 8, 6), ("a", 6, 4), ("a", 8, 7), ("a", 9, 3), ("a", 7, 5), ("a", 3, 6), ("f", 1, 0), ("a", 10, 3), ("a", 5, 10),
+    ("a", 4, 9), ("a", 7, 6), ("a", 11, 9), ("a", 9, 4), ("a", 8, 8), ("a", 6, 5), ("a", 8, 9), ("a", 10, 4), ("a", 4, 10), ("f", 2, 0), ("a", 8, 10),
+    ("a", 9, 5), ("a", 11, 10), ("a", 6, 6), ("f", 3, 0), ("a", 10, 5), ("a", 9, 6), ("f", 4, 0), ("a", 10, 6), ("f", 5, 0), ("d", 0, 0), ("l", 0, 0),
+    ("g", 5, 0), ("g", 5, 1), ("g", 4, 0), ("g", 4, 1), ("g", 4, 2), ("r", 11, 0), ("g", 5, 2), ("r", 9, 0), ("g", 3, 1), ("g", 3, 0), ("r", 11, 1),
+    ("r", 11, 2), ("r", 10, 0), ("g", 3, 2), ("r", 9, 1), ("r", 8, 0), ("g", 2, 1), ("r", 9, 2), ("r", 7, 0), ("g", 2, 2), ("r", 10, 1), ("r", 6, 0),
+    ("r", 8, 1), ("g", 2, 0), ("r", 9, 3), ("r", 10, 2), ("r", 8, 2), ("g", 1, 0), ("r", 4, 0), ("r", 11, 3), ("r", 11, 4), ("g", 1, 1), ("r", 7, 1),
+    ("r", 7, 2), ("r", 8, 3), ("r", 6, 1), ("r", 5, 0), ("g", 1, 2), ("r", 4, 1), ("r", 10, 3), ("r", 6, 2), ("r", 8, 4), ("g", 0, 0), ("r", 4, 2),
+    ("r", 3, 0), ("r", 11, 5), ("g", 0, 1), ("r", 9, 4), ("r", 7, 3), ("h", 0, 0), ("r", 11, 6), ("r", 6, 3), ("r", 5, 1), ("r", 8, 5), ("r", 2, 0),
+    ("g", 0, 2), ("r", 4, 3), ("r", 5, 2), ("r", 1, 0), ("r", 10, 4), ("r", 8, 6), ("r", 3, 1), ("r", 4, 4), ("r", 0, 0), ("r", 3, 2), ("r", 11, 7),
+    ("r", 5, 3), ("r", 7, 4), ("r", 2, 1), ("r", 8, 7), ("r", 6, 4), ("r", 4, 5), ("r", 1, 1), ("u", 9, 0), ("r", 2, 2), ("r", 5, 4), ("r", 1, 2),
+    ("r", 0, 1), ("r", 4, 6), ("r", 5, 5), ("r", 3, 3), ("r", 0, 2), ("u", 10, 0), ("r", 2, 3), ("r", 11, 8), ("r", 4, 7), ("r", 1, 3), ("u", 7, 0),
+    ("r", 5, 6), ("r", 8, 8), ("u", 6, 0), ("r", 0, 3), ("r", 5, 7), ("b", 9, 0), ("r", 3, 4), ("u", 11, 0), ("r", 2, 4), ("r", 4, 8), ("b", 10, 0),
+    ("u", 8, 0), ("r", 1, 4), ("r", 0, 4), ("b", 7, 0), ("r", 5, 8), ("b", 6, 0), ("b", 9, 1), ("b", 11, 0), ("u", 4, 0), ("b", 8, 0), ("u", 3, 0),
+    ("b", 10, 1), ("u", 2, 0), ("b", 7, 1), ("u", 5, 0), ("u", 1, 0), ("b", 6, 1), ("u", 0, 0), ("n", 0, 0), ("b", 4, 0), ("b", 11, 1), ("b", 10, 2),
+    ("b", 10, 3), ("b", 3, 0), ("b", 8, 1), ("b", 5, 0), ("b", 6, 2), ("b", 7, 2), ("b", 11, 2), ("b", 6, 3), ("b", 1, 0), ("b", 7, 3), ("b", 11, 3),
+    ("b", 0, 0), ("b", 8, 2), ("b", 4, 1), ("b", 10, 4), ("b", 8, 3), ("b", 9, 2), ("b", 9, 3), ("b", 2, 0), ("b", 3, 1), ("b", 10, 5), ("b", 5, 1),
+    ("b", 6, 4), ("b", 7, 4), ("b", 8, 4), ("b", 6, 5), ("b", 7, 5), ("b", 4, 2), ("b", 1, 1), ("b", 0, 1), ("b", 4, 3), ("b", 9, 4), ("b", 8, 5),
+    ("b", 5, 2), ("b", 9, 5), ("b", 3, 2), ("b", 5, 3), ("b", 2, 1), ("b", 8, 6), ("b", 3, 3), ("b", 4, 4), ("b", 4, 5), ("b", 0, 2), ("b", 1, 2),
+    ("b", 8, 7), ("b", 0, 3), ("b", 5, 4), ("b", 1, 3), ("b", 5, 5), ("b", 2, 2), ("b", 8, 8), ("b", 11, 4), ("b", 3, 4), ("b", 4, 6), ("b", 2, 3),
+    ("b", 8, 9), ("b", 4, 7), ("b", 1, 4), ("b", 3, 5), ("b", 5, 6), ("b", 0, 4), ("b", 5, 7), ("b", 11, 5), ("b", 1, 5), ("b", 11, 6), ("b", 2, 4),
+    ("b", 0, 5), ("s", 0, 0), ("b", 5, 8), ("b", 4, 8), ("b", 2, 5), ("s", 1, 0), ("n", 0, 1), ("b", 5, 9), ("b", 4, 9), ("b", 11, 7), ("s", 2, 0), ("b", 11, 8),
+    ("s", 3, 0), ("s", 4, 0), ("b", 11, 9), ("s", 5, 0),
 )
 
 

time: 145 us -> 144 us (level)
  no operation moved by 1% of the time
where the time goes in v9:
time: 144 us
  Pallas kernels  144 us (100%)
    pallas_call x1, Pallas kernels, device_step(): step(w_one, w_two, mom_one, mom_two, x_zero, y_zero, x_one, y_one)[:6]  141 us

profile of v9, /device:TPU:1, one launch (start us, length us, event | category | flops | bytes accessed | tf_op | source)
XLA Modules:
  0.0 144.3 jit_solution(697807895612378425)
XLA Ops:
  0.6 140.9 %train_step.1 = (f32[6,2,1024]{2,1,0:T(2,128)}, f32[6,4,512]{2,1,0:T(4,128)}, f32[6,2,1024]{2,1,0:T(2,128)}, f32[6,4,512]{2,1,0:T(4,128)}, f32[1,768]{1,0:T(1,12...) custom-call(f32[6,2,1024]{2,1,0:T(2,128)} %w1.1, f32[6,4,512]{2,1,0:T(4,128)} %w2.1, f32[6,2,1024]{2,1,0:T(2,128)} %m1.1, ...), custom_call_target="tpu_custom_call" | custom-call | tf_op jit(solution)/shard_map/train_step/pallas_call | solution.py:746
  141.6 2.8 %hand_over.1 = (f32[6,2,1024]{2,1,0:T(2,128)}, f32[6,4,512]{2,1,0:T(4,128)}, f32[6,2,1024]{2,1,0:T(2,128)}, f32[6,4,512]{2,1,0:T(4,128)}, f32[768]{0:T(1024)}, /*index=5*/f32[768,512]{1,0:T(8,128)}) custom-call(f32[6,2,1024]{2,1,0:T(2,128)} %get-tuple-element.12.refs_0_, f32[6,4,512]{2,1,0:T(4,128)} %get-tuple-element.13.refs_1_, ...), custom_call_target="tpu_custom_call" | custom-call | tf_op jit(solution)/shard_map/hand_over/pallas_call | solution.py:750
